TPU v7x, 256 devices: a whole 4x4x8 slice. The times are simulated.
256 devices in a mesh: section: 4 (over y_hi, core), img: 64 (over x, z, y_lo).
Axes of the slice: x: 4, y: 4 (y_hi: 2, y_lo: 2; y = y_hi * 2 + y_lo), z: 8, core: 2. Of those that a mesh axis runs over, the one named last changes fastest.
Arguments:
- early_feats: bfloat16 [8, 4096, 1280], P('section', 'img'), may hold values from -6 to 6
- final_embed: bfloat16 [8, 4096, 256], P('section', 'img'), may hold values from -240 to 240
- prompt_counts: int32 [8], replicated, may hold values from 16 to 64, as said below
- box_pixels: int32 [8, 64, 4], replicated, may hold values from 0 to 1023
- pair_table: int32 [8], replicated, may hold values from 0 to 7, as said below
- token_table: float32 [8, 256], replicated, may hold values from -6 to 6
- pe_basis: float32 [2, 128], replicated, may hold values from -5 to 5
- w_early: bfloat16 [1280, 256], replicated, may hold values from -0.15625 to 0.15625
- attend_in: bfloat16 [2, 6, 256, 128], replicated, may hold values from -0.375 to 0.375
- attend_out: bfloat16 [2, 2, 128, 256], replicated, may hold values from -0.5 to 0.5
- mlp_up: bfloat16 [2, 256, 2048], replicated, may hold values from -0.375 to 0.375
- mlp_down: bfloat16 [2, 2048, 256], replicated, may hold values from -0.125 to 0.125
- w_hyper: bfloat16 [256, 256], replicated, may hold values from -0.375 to 0.375
Outputs:
- masks: float32 [8, 64, 4096], P('section', None, 'img')
Inputs may be any that keep to these rules, and one draw needn't show every extreme that they name: `prompt_counts`: at least one image has all 64 prompts live. `pair_table`: a permutation of the images that maps all 2 images of an output group to the 2 images of one input group, in any order.
All inputs are finite; a program needn't handle non-finite values.
Results may differ from a plain program's by a relative error of at most 0.017.
The roundings to bfloat16 on the way count: a program that leaves them out, or rounds other values in their place, can miss the bound.
Values may be sent and summed in bfloat16 or wider, within the bound.
No kernel may reach another device: no remote copies, remote signals or barrier semaphores. Data moves between devices by JAX's collectives and lax.ppermute only.
A program may use at most 64 MiB of HBM per device.

v0:
```python
import math

import jax
import jax.numpy as jnp
from jax import lax
from jax.sharding import PartitionSpec as P

HEADS = 8
GRID = 64
IMG_PIX = 1024
TOKS_P = 8
LAYERS = 2


NORM_EPS = 0.01


def side_by_side(arrays, axis, dim, along):
    widths = [a.shape[along] for a in arrays]
    both = jnp.concatenate(arrays, axis=along)
    whole = lax.all_gather(both, axis, axis=dim, tiled=True)
    return tuple(jnp.split(whole, [sum(widths[:k]) for k in range(1, len(widths))], axis=along))


def partner(x, axis, distance):
    return lax.ppermute(x, axis, [(i, i ^ 1 << distance) for i in range(lax.axis_size(axis))])


def shortened(x):
    return jax.tree.map(lambda a: a.astype(jnp.bfloat16) if a.dtype == jnp.float32 else a, x)


def norm_rows(values):
    center = values - jnp.mean(values, axis=-1, keepdims=True)
    spread = jnp.mean(center * center, axis=-1, keepdims=True)
    return center / jnp.sqrt(spread + NORM_EPS)


def fourier(coord_x, coord_y, pe_basis):
    phase = (2.0 * coord_x - 1.0)[..., None] * pe_basis[0] + (2.0 * coord_y - 1.0)[
        ..., None
    ] * pe_basis[1]
    phase = 2.0 * math.pi * phase
    return jnp.concatenate([jnp.sin(phase), jnp.cos(phase)], axis=-1)


def grid_code(index, pe_basis):
    column = (index % GRID).astype(jnp.float32)
    row_idx = (index // GRID).astype(jnp.float32)
    return fourier((column + 0.5) / GRID, (row_idx + 0.5) / GRID, pe_basis)


def start_tokens(box_rows, token_table, pe_basis):
    coords = (box_rows.astype(jnp.float32) + 0.5) / IMG_PIX
    corner_one = fourier(coords[:, 0], coords[:, 1], pe_basis)
    corner_two = fourier(coords[:, 2], coords[:, 3], pe_basis)
    slots = jnp.arange(TOKS_P)[None, :, None]
    tokens = token_table[None] + jnp.where(slots == TOKS_P - 2, corner_one[:, None, :], 0.0)
    tokens = tokens + jnp.where(slots == TOKS_P - 1, corner_two[:, None, :], 0.0)
    return tokens.reshape(-1, token_table.shape[-1])


def bdot(left, right):
    return jnp.dot(left, right, preferred_element_type=jnp.float32)


def make_hq(early_part, w_early):
    hq_part = jax.nn.gelu(bdot(early_part, w_early), approximate=False).astype(jnp.bfloat16)
    return lax.optimization_barrier(hq_part)


def shards(
    early_feats,
    final_embed,
    prompt_counts,
    box_pixels,
    pair_table,
    token_table,
    pe_basis,
    w_early,
    attend_in,
    attend_out,
    mlp_up,
    mlp_down,
    w_hyper,
):
    images = early_feats.shape[0]
    pos_dev = early_feats.shape[1]
    width = final_embed.shape[2]
    prompts = box_pixels.shape[1]
    devices = lax.axis_size("img")
    my_index = lax.axis_index("img")
    my_section = lax.axis_index("section")
    img_bits = images.bit_length() - 1
    all_bits = devices.bit_length() - 1
    group_table = lax.dynamic_slice_in_dim(pair_table, my_section * images, images, 0)
    source = group_table[0] // images
    inner_order = group_table % images
    own_hq = make_hq(early_feats, w_early)

    def choose(older, newer):
        rows_here = newer.shape[0]
        offset = source * images
        inside = (offset >= 0) & (offset + images <= rows_here)
        taken = lax.dynamic_slice_in_dim(newer, jnp.clip(offset, 0, rows_here - images), images, 0)
        return jnp.where(inside, taken, older)

    final_group, hq_group = jax.tree.map(
        choose,
        (jnp.zeros_like(final_embed), jnp.zeros_like(own_hq)),
        side_by_side((final_embed, own_hq), "section", 0, 1),
    )
    final_part = jnp.take(final_group, inner_order, axis=0)
    hq_part = jnp.take(hq_group, inner_order, axis=0)
    stacked = jnp.stack([final_part, hq_part])
    bit = 0
    my_bit = my_index >> bit & 1
    pairs = stacked.reshape(2, stacked.shape[1] // 2, 2, stacked.shape[2], width)
    keep = lax.dynamic_index_in_dim(pairs, my_bit, 2, keepdims=False)
    send = lax.dynamic_index_in_dim(pairs, 1 - my_bit, 2, keepdims=False)
    got = partner(send, "img", bit)
    lower = jnp.where(my_bit == 0, keep, got)
    upper = jnp.where(my_bit == 0, got, keep)
    stacked = jnp.concatenate([lower, upper], axis=2)
    final_here = stacked[0]
    hq_here = stacked[1]
    held = 1
    held_pos = images * pos_dev
    members = devices // images
    my_rank = my_index // images
    table_offset = my_index % images
    first_pos = my_rank * held_pos
    picks = lax.dynamic_slice_in_dim(pair_table, my_section * images + table_offset, held, 0)
    my_counts = jnp.take(prompt_counts, picks, axis=0)
    my_boxes = jnp.take(box_pixels, picks, axis=0)
    per_image = prompts * TOKS_P
    rows_all = held * per_image
    own_rows = rows_all // members
    head_size = attend_in.shape[-1] // HEADS
    scale = head_size ** (-0.5)
    tokens_start = start_tokens(my_boxes.reshape(-1, 4), token_table, pe_basis)
    tok_own = lax.dynamic_slice_in_dim(tokens_start, my_rank * own_rows, own_rows, 0)
    positions = first_pos + jnp.arange(held_pos, dtype=jnp.int32)
    img_code = grid_code(positions, pe_basis)
    image = final_here.astype(jnp.float32)
    live_prompt = jnp.arange(prompts, dtype=jnp.int32)[None, :] < my_counts[:, None]
    live_token = jnp.repeat(live_prompt, TOKS_P, axis=1)
    query_one = bdot(tokens_start.astype(jnp.bfloat16), attend_in[0, 0]).astype(jnp.bfloat16)
    hyper = None
    for layer in range(LAYERS):
        image_bf = image.astype(jnp.bfloat16)
        key_bf = (image + img_code[None]).astype(jnp.bfloat16)
        keys_one = bdot(key_bf, attend_in[layer, 1]).astype(jnp.bfloat16)
        values_one = bdot(image_bf, attend_in[layer, 2]).astype(jnp.bfloat16)
        query_heads = query_one.reshape(held, per_image, HEADS, head_size)
        key_heads = keys_one.reshape(held, held_pos, HEADS, head_size)
        value_heads = values_one.reshape(held, held_pos, HEADS, head_size)
        scores = (
            jnp.einsum(
                "iqhd,ikhd->ihqk", query_heads, key_heads, preferred_element_type=jnp.float32
            )
            * scale
        )
        values = jnp.max(scores, axis=-1)
        for peak_bit in range(img_bits, all_bits):
            values = jnp.maximum(values, partner(values, "img", peak_bit))
        weights = jnp.exp(scores - values[..., None]).astype(jnp.bfloat16)
        summed = jnp.einsum(
            "ihqk,ikhd->iqhd", weights, value_heads, preferred_element_type=jnp.float32
        ).reshape(rows_all, HEADS * head_size)
        totals = jnp.sum(weights.astype(jnp.float32), axis=-1)
        totals = jnp.transpose(totals, (0, 2, 1)).reshape(rows_all, HEADS)
        reduce_summed = summed
        reduce_totals = totals
        for reduce_bit in reversed(range(img_bits, all_bits)):
            reduce_my_bit = my_index >> reduce_bit & 1
            split_s = reduce_summed.reshape(2, reduce_summed.shape[0] // 2, reduce_summed.shape[1])
            split_t = reduce_totals.reshape(2, reduce_totals.shape[0] // 2, reduce_totals.shape[1])
            keep_s = lax.dynamic_index_in_dim(split_s, reduce_my_bit, 0, keepdims=False)
            keep_t = lax.dynamic_index_in_dim(split_t, reduce_my_bit, 0, keepdims=False)
            send_s = lax.dynamic_index_in_dim(split_s, 1 - reduce_my_bit, 0, keepdims=False)
            send_t = lax.dynamic_index_in_dim(split_t, 1 - reduce_my_bit, 0, keepdims=False)
            reduce_got = (
                partner(send_s.astype(jnp.bfloat16), "img", reduce_bit).astype(send_s.dtype),
                partner(send_t.astype(jnp.bfloat16), "img", reduce_bit).astype(send_t.dtype),
            )
            reduce_summed = keep_s + reduce_got[0]
            reduce_totals = keep_t + reduce_got[1]
        first_out = (
            reduce_summed.reshape(own_rows, HEADS, head_size) / reduce_totals[:, :, None]
        ).reshape(own_rows, HEADS * head_size)
        tok_two = norm_rows(tok_own + bdot(first_out.astype(jnp.bfloat16), attend_out[layer, 0]))
        hidden = jax.nn.relu(bdot(tok_two.astype(jnp.bfloat16), mlp_up[layer])).astype(jnp.bfloat16)
        tok_three = norm_rows(tok_two + bdot(hidden, mlp_down[layer]))
        three_own = tok_three.astype(jnp.bfloat16)
        last_layer = layer == LAYERS - 1
        rows = (three_own,)
        for collect_bit in range(img_bits, all_bits):
            collect_my_bit = my_index >> collect_bit & 1
            collect_got = jax.tree.map(
                lambda part, own: part.astype(own.dtype),
                partner(shortened(rows), "img", collect_bit),
                rows,
            )
            rows = tuple(
                (
                    jnp.concatenate(
                        [
                            jnp.where(collect_my_bit == 0, mine, theirs),
                            jnp.where(collect_my_bit == 0, theirs, mine),
                        ],
                        axis=0,
                    )
                    for mine, theirs in zip(rows, collect_got)
                )
            )
        three_all = rows[0]
        keys_two = bdot(three_all, attend_in[layer, 4]).astype(jnp.bfloat16)
        values_two = bdot(three_all, attend_in[layer, 5]).astype(jnp.bfloat16)
        if last_layer:
            hyper = bdot(three_all.reshape(-1, TOKS_P, width)[:, TOKS_P - 3], w_hyper).astype(
                jnp.bfloat16
            )
        else:
            query_one = bdot(three_all, attend_in[layer + 1, 0]).astype(jnp.bfloat16)
        query_two = (
            bdot(key_bf, attend_in[layer, 3])
            .astype(jnp.bfloat16)
            .reshape(held, held_pos, HEADS, head_size)
        )
        token_keys = keys_two.reshape(held, per_image, HEADS, head_size)
        token_values = values_two.reshape(held, per_image, HEADS, head_size)
        scores_two = (
            jnp.einsum("ikhd,iqhd->ihkq", query_two, token_keys, preferred_element_type=jnp.float32)
            * scale
        )
        scores_two = jnp.where(live_token[:, None, None, :], scores_two, -jnp.inf)
        highest_two = jnp.max(scores_two, axis=-1, keepdims=True)
        weights_two = jnp.exp(scores_two - highest_two).astype(jnp.bfloat16)
        summed_two = jnp.einsum(
            "ihkq,iqhd->ikhd", weights_two, token_values, preferred_element_type=jnp.float32
        )
        totals_two = jnp.transpose(jnp.sum(weights_two.astype(jnp.float32), axis=-1), (0, 2, 1))
        second_out = (summed_two / totals_two[..., None]).reshape(held, held_pos, HEADS * head_size)
        image = norm_rows(image + bdot(second_out.astype(jnp.bfloat16), attend_out[layer, 1]))
        tok_own = tok_three
    hyper_rows = hyper.reshape(held, prompts, width)
    mask_feats = (image + hq_here.astype(jnp.float32)).astype(jnp.bfloat16)
    logits = jnp.einsum(
        "ipc,ikc->ipk", hyper_rows, mask_feats, preferred_element_type=jnp.float32
    ) * width ** (-0.5)
    result = jnp.where(live_prompt[:, :, None], logits, 0.0)
    for bit in reversed(range(img_bits)):
        my_bit = my_index >> bit & 1
        halves = result.reshape(result.shape[0], prompts, 2, result.shape[2] // 2)
        keep = lax.dynamic_index_in_dim(halves, my_bit, 2, keepdims=False)
        send = lax.dynamic_index_in_dim(halves, 1 - my_bit, 2, keepdims=False)
        got = partner(send, "img", bit)
        first = jnp.where(my_bit == 0, keep, got)
        second = jnp.where(my_bit == 0, got, keep)
        result = jnp.stack([first, second], axis=1).reshape(
            2 * keep.shape[0], prompts, keep.shape[2]
        )
    return result


def solution(mesh):
    placed = (
        P("section", "img", None),
        P("section", "img", None),
        P(),
        P(),
        P(),
        P(),
        P(),
        P(),
        P(),
        P(),
        P(),
        P(),
        P(),
    )
    return jax.shard_map(
        shards, mesh=mesh, in_specs=placed, out_specs=P("section", None, "img"), check_vma=False
    )
```

profile of v0, /device:TPU:32, one launch (start us, length us, event | category | flops | bytes accessed | tf_op | source)
XLA Modules:
  0.0 224.5 jit_solution(8146273326554413181)
XLA Ops:
  1.1 1.5 fusion.39
  2.7 8.9 %all_gather.3 = bf16[8,128,256]{2,1,0:T(8,128)(2,1)S(1)} all-gather(bf16[2,128,256]{2,1,0:T(8,128)(2,1)S(1)} %pad_maximum_fusion.2), channel_id=1, replica_groups=mesh['section'=4,'img'=64] {'section'}, dimensions={0}, use_global_device_ids=true | all-gather | bytes 655360 | tf_op jit(solution)/shard_map/all_gather | solution.py:21
  12.9 1.1 collective-permute-start
  17.6 1.1 convolution_convert_fusion.5
  19.2 1.1 convolution_convert_fusion.11
  20.9 3.6 %collective-permute-done.1 = f32[1,8,512]{2,1,0:T(8,128)S(1)} collective-permute-done((f32[1,8,512]{2,1,0:T(8,128)S(1)}, f32[1,8,512]{2,1,0:T(8,128)S(1)}, u32[]{:S(2)}, u32[]{:S(2)}) %collective-permute-start.1) | collective-permute-done | bytes 16416 | tf_op jit(solution)/shard_map/ppermute | solution.py:26
  24.5 3.3 %collective-permute-start.2 = (f32[1,8,512]{2,1,0:T(8,128)S(1)}, f32[1,8,512]{2,1,0:T(8,128)S(1)}, u32[]{:S(2)}, u32[]{:S(2)}) collective-permute-start(f32[1,8,512]{2,1,0:T(8,128)S(1)} %bitcast_maximum_fusion.1), channel_id=1, source_target_pairs={{0,4},{1,5},{2,6},{3,7},{4,0},{5,1},{6,2},{7,3},{8,12},{9,13},{10,... | collective-permute-start | bytes 49160 | tf_op jit(solution)/shard_map/ppermute | solution.py:26
  29.5 5.9 %collective-permute-start.3 = (f32[1,8,512]{2,1,0:T(8,128)S(1)}, f32[1,8,512]{2,1,0:T(8,128)S(1)}, u32[]{:S(2)}, u32[]{:S(2)}) collective-permute-start(f32[1,8,512]{2,1,0:T(8,128)S(1)} %max.49), channel_id=1, source_target_pairs={{0,8},{1,9},{2,10},{3,11},{4,12},{5,13},{6,14},{7,15},{8,0},{9,1},... | collective-permute-start | bytes 49160 | tf_op jit(solution)/shard_map/ppermute | solution.py:26
  37.2 1.5 collective-permute-start.4
  39.9 1.0 collective-permute-done.4
  40.9 3.0 %collective-permute-start.5 = (f32[1,8,512]{2,1,0:T(8,128)S(1)}, f32[1,8,512]{2,1,0:T(8,128)S(1)}, u32[]{:S(2)}, u32[]{:S(2)}) collective-permute-start(f32[1,8,512]{2,1,0:T(8,128)S(1)} %max.51), channel_id=1, source_target_pairs={{0,32},{1,33},{2,34},{3,35},{4,36},{5,37},{6,38},{7,39},{8,40},{9,... | collective-permute-start | bytes 49160 | tf_op jit(solution)/shard_map/ppermute | solution.py:26
  44.0 1.1 convolution_convert_fusion.12
  45.0 1.2 collective-permute-done.5
  46.6 3.1 %collective-permute-start.11 = (bf16[256,8]{0,1:T(8,128)(2,1)S(1)}, bf16[256,8]{0,1:T(8,128)(2,1)S(1)}, u32[]{:S(2)}, u32[]{:S(2)}) collective-permute-start(bf16[256,8]{0,1:T(8,128)(2,1)S(1)} %fusion.147), channel_id=1, source_target_pairs={{0,32},{1,33},{2,34},{3,35},{4,36},{5,37},{6,38},{7,39},{8,40},{9,... | collective-permute-start | bytes 12296 | tf_op jit(solution)/shard_map/ppermute | solution.py:26
  50.4 1.4 collective-permute-done.11
  51.8 1.5 collective-permute-start.12
  53.7 2.8 %collective-permute-start.6 = (bf16[256,128]{1,0:T(8,128)(2,1)S(1)}, bf16[256,128]{1,0:T(8,128)(2,1)S(1)}, u32[]{:S(2)}, u32[]{:S(2)}) collective-permute-start(bf16[256,128]{1,0:T(8,128)(2,1)S(1)} %bitcast.395), channel_id=1, source_target_pairs={{0,32},{1,33},{2,34},{3,35},{4,36},{5,37},{6,38},{7,39},{8,40},{9,... | collective-permute-start | bytes 196616 | tf_op jit(solution)/shard_map/ppermute | solution.py:26
  56.6 6.0 %collective-permute-start.13 = (bf16[64,8]{0,1:T(8,128)(2,1)S(1)}, bf16[64,8]{0,1:T(8,128)(2,1)S(1)}, u32[]{:S(2)}, u32[]{:S(2)}) collective-permute-start(bf16[64,8]{0,1:T(8,128)(2,1)S(1)} %bitcast.420), channel_id=1, source_target_pairs={{0,8},{1,9},{2,10},{3,11},{4,12},{5,13},{6,14},{7,15},{8,0},{9,1},... | collective-permute-start | bytes 3080 | tf_op jit(solution)/shard_map/ppermute | solution.py:26
  62.6 1.6 collective-permute-done.13
  64.3 3.0 %collective-permute-start.14 = (bf16[32,8]{0,1:T(8,128)(2,1)S(1)}, bf16[32,8]{0,1:T(8,128)(2,1)S(1)}, u32[]{:S(2)}, u32[]{:S(2)}) collective-permute-start(bf16[32,8]{0,1:T(8,128)(2,1)S(1)} %convert_bitcast_fusion.3), channel_id=1, source_target_pairs={{0,4},{1,5},{2,6},{3,7},{4,0},{5,1},{6,2},{7,3},{8,12},{9,13},{10,... | collective-permute-start | bytes 1544 | tf_op jit(solution)/shard_map/ppermute | solution.py:26
  69.0 2.4 %collective-permute-done.7 = bf16[128,128]{1,0:T(8,128)(2,1)S(1)} collective-permute-done((bf16[128,128]{1,0:T(8,128)(2,1)S(1)}, bf16[128,128]{1,0:T(8,128)(2,1)S(1)}, u32[]{:S(2)}, u32[]{:S(2)}) %collective-permute-start.7) | collective-permute-done | bytes 32800 | tf_op jit(solution)/shard_map/ppermute | solution.py:26
  71.4 4.6 %collective-permute-start.8 = (bf16[64,128]{1,0:T(8,128)(2,1)S(1)}, bf16[64,128]{1,0:T(8,128)(2,1)S(1)}, u32[]{:S(2)}, u32[]{:S(2)}) collective-permute-start(bf16[64,128]{1,0:T(8,128)(2,1)S(1)} %fusion.109), channel_id=1, source_target_pairs={{0,8},{1,9},{2,10},{3,11},{4,12},{5,13},{6,14},{7,15},{8,0},{9,1},... | collective-permute-start | bytes 49160 | tf_op jit(solution)/shard_map/ppermute | solution.py:26
  75.9 3.3 %collective-permute-done.8 = bf16[64,128]{1,0:T(8,128)(2,1)S(1)} collective-permute-done((bf16[64,128]{1,0:T(8,128)(2,1)S(1)}, bf16[64,128]{1,0:T(8,128)(2,1)S(1)}, u32[]{:S(2)}, u32[]{:S(2)}) %collective-permute-start.8) | collective-permute-done | bytes 16416 | tf_op jit(solution)/shard_map/ppermute | solution.py:26
  80.5 3.6 %collective-permute-done.9 = bf16[32,128]{1,0:T(8,128)(2,1)S(1)} collective-permute-done((bf16[32,128]{1,0:T(8,128)(2,1)S(1)}, bf16[32,128]{1,0:T(8,128)(2,1)S(1)}, u32[]{:S(2)}, u32[]{:S(2)}) %collective-permute-start.9) | collective-permute-done | bytes 8224 | tf_op jit(solution)/shard_map/ppermute | solution.py:26
  84.5 3.3 %collective-permute-done.10 = bf16[16,128]{1,0:T(8,128)(2,1)S(1)} collective-permute-done((bf16[16,128]{1,0:T(8,128)(2,1)S(1)}, bf16[16,128]{1,0:T(8,128)(2,1)S(1)}, u32[]{:S(2)}, u32[]{:S(2)}) %collective-permute-start.10) | collective-permute-done | bytes 4128 | tf_op jit(solution)/shard_map/ppermute | solution.py:26
  87.8 1.0 fusion.191
  89.0 2.2 fusion.192
  91.6 3.6 %collective-permute-done.16 = bf16[16,256]{1,0:T(8,128)(2,1)S(1)} collective-permute-done((bf16[16,256]{1,0:T(8,128)(2,1)S(1)}, bf16[16,256]{1,0:T(8,128)(2,1)S(1)}, u32[]{:S(2)}, u32[]{:S(2)}) %collective-permute-start.16) | collective-permute-done | bytes 8224 | tf_op jit(solution)/shard_map/ppermute | solution.py:26
  95.7 4.3 %collective-permute-done.17 = bf16[32,256]{1,0:T(8,128)(2,1)S(1)} collective-permute-done((bf16[32,256]{1,0:T(8,128)(2,1)S(1)}, bf16[32,256]{1,0:T(8,128)(2,1)S(1)}, u32[]{:S(2)}, u32[]{:S(2)}) %collective-permute-start.17) | collective-permute-done | bytes 16416 | tf_op jit(solution)/shard_map/ppermute | solution.py:26
  100.0 4.4 %collective-permute-start.18 = (bf16[64,256]{1,0:T(8,128)(2,1)S(1)}, bf16[64,256]{1,0:T(8,128)(2,1)S(1)}, u32[]{:S(2)}, u32[]{:S(2)}) collective-permute-start(bf16[64,256]{1,0:T(8,128)(2,1)S(1)} %pad_maximum_fusion.15), channel_id=1, source_target_pairs={{0,8},{1,9},{2,10},{3,11},{4,12},{5,13},{6,14},{7,15},{8,0},{9,1},... | collective-permute-start | bytes 98312 | tf_op jit(solution)/shard_map/ppermute | solution.py:26
  106.1 2.1 collective-permute-done.18
  109.1 3.5 %collective-permute-done.19 = bf16[128,256]{1,0:T(8,128)(2,1)S(1)} collective-permute-done((bf16[128,256]{1,0:T(8,128)(2,1)S(1)}, bf16[128,256]{1,0:T(8,128)(2,1)S(1)}, u32[]{:S(2)}, u32[]{:S(2)}) %collective-permute-start.19) | collective-permute-done | bytes 65568 | tf_op jit(solution)/shard_map/ppermute | solution.py:26
  112.6 2.0 collective-permute-start.20
  114.8 4.3 %collective-permute-done.20 = bf16[256,256]{1,0:T(8,128)(2,1)S(1)} collective-permute-done((bf16[256,256]{1,0:T(8,128)(2,1)S(1)}, bf16[256,256]{1,0:T(8,128)(2,1)S(1)}, u32[]{:S(2)}, u32[]{:S(2)}) %collective-permute-start.20) | collective-permute-done | bytes 131104 | tf_op jit(solution)/shard_map/ppermute | solution.py:26
  123.1 3.7 %collective-permute-done.21 = f32[1,8,512]{2,1,0:T(8,128)S(1)} collective-permute-done((f32[1,8,512]{2,1,0:T(8,128)S(1)}, f32[1,8,512]{2,1,0:T(8,128)S(1)}, u32[]{:S(2)}, u32[]{:S(2)}) %collective-permute-start.21) | collective-permute-done | bytes 16416 | tf_op jit(solution)/shard_map/ppermute | solution.py:26
  127.1 4.4 %collective-permute-done.22 = f32[1,8,512]{2,1,0:T(8,128)S(1)} collective-permute-done((f32[1,8,512]{2,1,0:T(8,128)S(1)}, f32[1,8,512]{2,1,0:T(8,128)S(1)}, u32[]{:S(2)}, u32[]{:S(2)}) %collective-permute-start.22) | collective-permute-done | bytes 16416 | tf_op jit(solution)/shard_map/ppermute | solution.py:26
  131.5 4.1 %collective-permute-start.23 = (f32[1,8,512]{2,1,0:T(8,128)S(1)}, f32[1,8,512]{2,1,0:T(8,128)S(1)}, u32[]{:S(2)}, u32[]{:S(2)}) collective-permute-start(f32[1,8,512]{2,1,0:T(8,128)S(1)} %max.56), channel_id=1, source_target_pairs={{0,8},{1,9},{2,10},{3,11},{4,12},{5,13},{6,14},{7,15},{8,0},{9,1},... | collective-permute-start | bytes 49160 | tf_op jit(solution)/shard_map/ppermute | solution.py:26
  135.5 3.6 %collective-permute-done.23 = f32[1,8,512]{2,1,0:T(8,128)S(1)} collective-permute-done((f32[1,8,512]{2,1,0:T(8,128)S(1)}, f32[1,8,512]{2,1,0:T(8,128)S(1)}, u32[]{:S(2)}, u32[]{:S(2)}) %collective-permute-start.23) | collective-permute-done | bytes 16416 | tf_op jit(solution)/shard_map/ppermute | solution.py:26
  139.7 3.2 %collective-permute-done.24 = f32[1,8,512]{2,1,0:T(8,128)S(1)} collective-permute-done((f32[1,8,512]{2,1,0:T(8,128)S(1)}, f32[1,8,512]{2,1,0:T(8,128)S(1)}, u32[]{:S(2)}, u32[]{:S(2)}) %collective-permute-start.24) | collective-permute-done | bytes 16416 | tf_op jit(solution)/shard_map/ppermute | solution.py:26
  142.9 1.9 collective-permute-start.25
  145.0 3.1 %collective-permute-done.25 = f32[1,8,512]{2,1,0:T(8,128)S(1)} collective-permute-done((f32[1,8,512]{2,1,0:T(8,128)S(1)}, f32[1,8,512]{2,1,0:T(8,128)S(1)}, u32[]{:S(2)}, u32[]{:S(2)}) %collective-permute-start.25) | collective-permute-done | bytes 16416 | tf_op jit(solution)/shard_map/ppermute | solution.py:26
  148.5 2.2 collective-permute-start.31
  151.5 2.5 %collective-permute-done.31 = bf16[256,8]{0,1:T(8,128)(2,1)S(1)} collective-permute-done((bf16[256,8]{0,1:T(8,128)(2,1)S(1)}, bf16[256,8]{0,1:T(8,128)(2,1)S(1)}, u32[]{:S(2)}, u32[]{:S(2)}) %collective-permute-start.31) | collective-permute-done | bytes 4128 | tf_op jit(solution)/shard_map/ppermute | solution.py:26
  154.9 2.6 %collective-permute-start.26 = (bf16[256,128]{1,0:T(8,128)(2,1)S(1)}, bf16[256,128]{1,0:T(8,128)(2,1)S(1)}, u32[]{:S(2)}, u32[]{:S(2)}) collective-permute-start(bf16[256,128]{1,0:T(8,128)(2,1)S(1)} %bitcast.396), channel_id=1, source_target_pairs={{0,32},{1,33},{2,34},{3,35},{4,36},{5,37},{6,38},{7,39},{8,40},{9,... | collective-permute-start | bytes 196616 | tf_op jit(solution)/shard_map/ppermute | solution.py:26
  157.6 4.3 %collective-permute-start.33 = (bf16[64,8]{0,1:T(8,128)(2,1)S(1)}, bf16[64,8]{0,1:T(8,128)(2,1)S(1)}, u32[]{:S(2)}, u32[]{:S(2)}) collective-permute-start(bf16[64,8]{0,1:T(8,128)(2,1)S(1)} %bitcast.421), channel_id=1, source_target_pairs={{0,8},{1,9},{2,10},{3,11},{4,12},{5,13},{6,14},{7,15},{8,0},{9,1},... | collective-permute-start | bytes 3080 | tf_op jit(solution)/shard_map/ppermute | solution.py:26
  162.0 3.3 %collective-permute-done.33 = bf16[64,8]{0,1:T(8,128)(2,1)S(1)} collective-permute-done((bf16[64,8]{0,1:T(8,128)(2,1)S(1)}, bf16[64,8]{0,1:T(8,128)(2,1)S(1)}, u32[]{:S(2)}, u32[]{:S(2)}) %collective-permute-start.33) | collective-permute-done | bytes 1056 | tf_op jit(solution)/shard_map/ppermute | solution.py:26
  166.3 3.6 %collective-permute-done.34 = bf16[32,8]{0,1:T(8,128)(2,1)S(1)} collective-permute-done((bf16[32,8]{0,1:T(8,128)(2,1)S(1)}, bf16[32,8]{0,1:T(8,128)(2,1)S(1)}, u32[]{:S(2)}, u32[]{:S(2)}) %collective-permute-start.34) | collective-permute-done | bytes 544 | tf_op jit(solution)/shard_map/ppermute | solution.py:26
  170.0 5.1 %collective-permute-start.28 = (bf16[64,128]{1,0:T(8,128)(2,1)S(1)}, bf16[64,128]{1,0:T(8,128)(2,1)S(1)}, u32[]{:S(2)}, u32[]{:S(2)}) collective-permute-start(bf16[64,128]{1,0:T(8,128)(2,1)S(1)} %fusion.110), channel_id=1, source_target_pairs={{0,8},{1,9},{2,10},{3,11},{4,12},{5,13},{6,14},{7,15},{8,0},{9,1},... | collective-permute-start | bytes 49160 | tf_op jit(solution)/shard_map/ppermute | solution.py:26
  175.1 2.6 %collective-permute-done.28 = bf16[64,128]{1,0:T(8,128)(2,1)S(1)} collective-permute-done((bf16[64,128]{1,0:T(8,128)(2,1)S(1)}, bf16[64,128]{1,0:T(8,128)(2,1)S(1)}, u32[]{:S(2)}, u32[]{:S(2)}) %collective-permute-start.28) | collective-permute-done | bytes 16416 | tf_op jit(solution)/shard_map/ppermute | solution.py:26
  177.8 2.5 %collective-permute-start.29 = (bf16[32,128]{1,0:T(8,128)(2,1)S(1)}, bf16[32,128]{1,0:T(8,128)(2,1)S(1)}, u32[]{:S(2)}, u32[]{:S(2)}) collective-permute-start(bf16[32,128]{1,0:T(8,128)(2,1)S(1)} %fusion.131), channel_id=1, source_target_pairs={{0,4},{1,5},{2,6},{3,7},{4,0},{5,1},{6,2},{7,3},{8,12},{9,13},{10,... | collective-permute-start | bytes 24584 | tf_op jit(solution)/shard_map/ppermute | solution.py:26
  180.6 1.9 collective-permute-done.29
  182.7 1.2 collective-permute-done.35
  184.2 1.9 collective-permute-done.30
  186.6 2.2 fusion.199
  189.3 3.4 %collective-permute-done.36 = bf16[16,256]{1,0:T(8,128)(2,1)S(1)} collective-permute-done((bf16[16,256]{1,0:T(8,128)(2,1)S(1)}, bf16[16,256]{1,0:T(8,128)(2,1)S(1)}, u32[]{:S(2)}, u32[]{:S(2)}) %collective-permute-start.36) | collective-permute-done | bytes 8224 | tf_op jit(solution)/shard_map/ppermute | solution.py:26
  192.8 2.5 %collective-permute-start.37 = (bf16[32,256]{1,0:T(8,128)(2,1)S(1)}, bf16[32,256]{1,0:T(8,128)(2,1)S(1)}, u32[]{:S(2)}, u32[]{:S(2)}) collective-permute-start(bf16[32,256]{1,0:T(8,128)(2,1)S(1)} %pad_maximum_fusion.18), channel_id=1, source_target_pairs={{0,4},{1,5},{2,6},{3,7},{4,0},{5,1},{6,2},{7,3},{8,12},{9,13},{10,... | collective-permute-start | bytes 49160 | tf_op jit(solution)/shard_map/ppermute | solution.py:26
  195.3 2.2 %collective-permute-done.37 = bf16[32,256]{1,0:T(8,128)(2,1)S(1)} collective-permute-done((bf16[32,256]{1,0:T(8,128)(2,1)S(1)}, bf16[32,256]{1,0:T(8,128)(2,1)S(1)}, u32[]{:S(2)}, u32[]{:S(2)}) %collective-permute-start.37) | collective-permute-done | bytes 16416 | tf_op jit(solution)/shard_map/ppermute | solution.py:26
  197.6 5.1 %collective-permute-start.38 = (bf16[64,256]{1,0:T(8,128)(2,1)S(1)}, bf16[64,256]{1,0:T(8,128)(2,1)S(1)}, u32[]{:S(2)}, u32[]{:S(2)}) collective-permute-start(bf16[64,256]{1,0:T(8,128)(2,1)S(1)} %pad_maximum_fusion.16), channel_id=1, source_target_pairs={{0,8},{1,9},{2,10},{3,11},{4,12},{5,13},{6,14},{7,15},{8,0},{9,1},... | collective-permute-start | bytes 98312 | tf_op jit(solution)/shard_map/ppermute | solution.py:26
  202.7 2.8 %collective-permute-done.38 = bf16[64,256]{1,0:T(8,128)(2,1)S(1)} collective-permute-done((bf16[64,256]{1,0:T(8,128)(2,1)S(1)}, bf16[64,256]{1,0:T(8,128)(2,1)S(1)}, u32[]{:S(2)}, u32[]{:S(2)}) %collective-permute-start.38) | collective-permute-done | bytes 32800 | tf_op jit(solution)/shard_map/ppermute | solution.py:26
  206.4 3.5 %collective-permute-done.39 = bf16[128,256]{1,0:T(8,128)(2,1)S(1)} collective-permute-done((bf16[128,256]{1,0:T(8,128)(2,1)S(1)}, bf16[128,256]{1,0:T(8,128)(2,1)S(1)}, u32[]{:S(2)}, u32[]{:S(2)}) %collective-permute-start.39) | collective-permute-done | bytes 65568 | tf_op jit(solution)/shard_map/ppermute | solution.py:26
  209.9 2.2 collective-permute-start.40
  212.3 4.1 %collective-permute-done.40 = bf16[256,256]{1,0:T(8,128)(2,1)S(1)} collective-permute-done((bf16[256,256]{1,0:T(8,128)(2,1)S(1)}, bf16[256,256]{1,0:T(8,128)(2,1)S(1)}, u32[]{:S(2)}, u32[]{:S(2)}) %collective-permute-start.40) | collective-permute-done | bytes 131104 | tf_op jit(solution)/shard_map/ppermute | solution.py:26
  219.8 1.1 collective-permute-start.41
  221.0 2.9 %collective-permute-done.41 = f32[1,64,64]{2,1,0:T(8,128)S(1)} collective-permute-done((f32[1,64,64]{2,1,0:T(8,128)S(1)}, f32[1,64,64]{2,1,0:T(8,128)S(1)}, u32[]{:S(2)}, u32[]{:S(2)}) %collective-permute-start.41) | collective-permute-done | bytes 16416 | tf_op jit(solution)/shard_map/ppermute | solution.py:26
  (228 shorter events, 32.8 us)
Async XLA Ops:
  0.0 1.1 copy-start
  0.0 2.6 %copy-start.2 = (bf16[2,64,256]{2,1,0:T(8,128)(2,1)S(1)}, bf16[2,64,256]{2,1,0:T(8,128)(2,1)}, u32[]{:S(2)}) copy-start(bf16[2,64,256]{2,1,0:T(8,128)(2,1)} %param.16) | copy-start | bytes 196612
  2.6 11.3 %copy-start.5 = (f32[2,128]{1,0:T(2,128)S(1)}, f32[2,128]{1,0:T(2,128)}, u32[]{:S(2)}) copy-start(f32[2,128]{1,0:T(2,128)} %param.21) | copy-start | bytes 3076
  2.6 11.3 %copy-start.6 = (s32[8]{0:T(128)S(1)}, s32[8]{0:T(128)}, u32[]{:S(2)}) copy-start(s32[8]{0:T(128)} %param.19) | copy-start | bytes 100
  2.6 15.0 %copy-start.4 = (f32[8,256]{1,0:T(8,128)S(1)}, f32[8,256]{1,0:T(8,128)}, u32[]{:S(2)}) copy-start(f32[8,256]{1,0:T(8,128)} %param.20) | copy-start | bytes 24580
  12.9 6.2 %collective-permute-start = (bf16[2,1,64,256]{3,2,1,0:T(8,128)(2,1)S(1)}, bf16[2,1,64,256]{3,2,1,0:T(8,128)(2,1)S(1)}, u32[]{:S(2)}, u32[]{:S(2)}) collective-permute-start(bf16[2,1,64,256]{3,2,1,0:T(8,128)(2,1)S(1)} %fusion.56), channel_id=1, source_target_pairs={{0,1},{1,0},{2,3},{3,2},{4,5},{5,4},{6,7},{7,6},{8,9},{9,8},{10,11... | collective-permute-start | bytes 196616 | tf_op jit(solution)/shard_map/ppermute | solution.py:26
  20.7 3.8 %collective-permute-start.1 = (f32[1,8,512]{2,1,0:T(8,128)S(1)}, f32[1,8,512]{2,1,0:T(8,128)S(1)}, u32[]{:S(2)}, u32[]{:S(2)}) collective-permute-start(f32[1,8,512]{2,1,0:T(8,128)S(1)} %bitcast.393), channel_id=1, source_target_pairs={{0,2},{1,3},{2,0},{3,1},{4,6},{5,7},{6,4},{7,5},{8,10},{9,11},{10,... | collective-permute-start | bytes 49160 | tf_op jit(solution)/shard_map/ppermute | solution.py:26
  24.5 5.0 %collective-permute-start.2 = (f32[1,8,512]{2,1,0:T(8,128)S(1)}, f32[1,8,512]{2,1,0:T(8,128)S(1)}, u32[]{:S(2)}, u32[]{:S(2)}) collective-permute-start(f32[1,8,512]{2,1,0:T(8,128)S(1)} %bitcast_maximum_fusion.1), channel_id=1, source_target_pairs={{0,4},{1,5},{2,6},{3,7},{4,0},{5,1},{6,2},{7,3},{8,12},{9,13},{10,... | collective-permute-start | bytes 49160 | tf_op jit(solution)/shard_map/ppermute | solution.py:26
  29.5 7.7 %collective-permute-start.3 = (f32[1,8,512]{2,1,0:T(8,128)S(1)}, f32[1,8,512]{2,1,0:T(8,128)S(1)}, u32[]{:S(2)}, u32[]{:S(2)}) collective-permute-start(f32[1,8,512]{2,1,0:T(8,128)S(1)} %max.49), channel_id=1, source_target_pairs={{0,8},{1,9},{2,10},{3,11},{4,12},{5,13},{6,14},{7,15},{8,0},{9,1},... | collective-permute-start | bytes 49160 | tf_op jit(solution)/shard_map/ppermute | solution.py:26
  37.2 3.7 %collective-permute-start.4 = (f32[1,8,512]{2,1,0:T(8,128)S(1)}, f32[1,8,512]{2,1,0:T(8,128)S(1)}, u32[]{:S(2)}, u32[]{:S(2)}) collective-permute-start(f32[1,8,512]{2,1,0:T(8,128)S(1)} %max.50), channel_id=1, source_target_pairs={{0,16},{1,17},{2,18},{3,19},{4,20},{5,21},{6,22},{7,23},{8,24},{9,... | collective-permute-start | bytes 49160 | tf_op jit(solution)/shard_map/ppermute | solution.py:26
  40.9 5.2 %collective-permute-start.5 = (f32[1,8,512]{2,1,0:T(8,128)S(1)}, f32[1,8,512]{2,1,0:T(8,128)S(1)}, u32[]{:S(2)}, u32[]{:S(2)}) collective-permute-start(f32[1,8,512]{2,1,0:T(8,128)S(1)} %max.51), channel_id=1, source_target_pairs={{0,32},{1,33},{2,34},{3,35},{4,36},{5,37},{6,38},{7,39},{8,40},{9,... | collective-permute-start | bytes 49160 | tf_op jit(solution)/shard_map/ppermute | solution.py:26
  46.6 5.2 %collective-permute-start.11 = (bf16[256,8]{0,1:T(8,128)(2,1)S(1)}, bf16[256,8]{0,1:T(8,128)(2,1)S(1)}, u32[]{:S(2)}, u32[]{:S(2)}) collective-permute-start(bf16[256,8]{0,1:T(8,128)(2,1)S(1)} %fusion.147), channel_id=1, source_target_pairs={{0,32},{1,33},{2,34},{3,35},{4,36},{5,37},{6,38},{7,39},{8,40},{9,... | collective-permute-start | bytes 12296 | tf_op jit(solution)/shard_map/ppermute | solution.py:26
  50.1 37.7 %copy-start.3 = (bf16[2,2,128,256]{3,2,1,0:T(8,128)(2,1)S(1)}, bf16[2,2,128,256]{3,2,1,0:T(8,128)(2,1)}, u32[]{:S(2)}) copy-start(bf16[2,2,128,256]{3,2,1,0:T(8,128)(2,1)} %param.24) | copy-start | bytes 786436
  51.8 4.6 %collective-permute-start.12 = (bf16[128,8]{0,1:T(8,128)(2,1)S(1)}, bf16[128,8]{0,1:T(8,128)(2,1)S(1)}, u32[]{:S(2)}, u32[]{:S(2)}) collective-permute-start(bf16[128,8]{0,1:T(8,128)(2,1)S(1)} %fusion.161), channel_id=1, source_target_pairs={{0,16},{1,17},{2,18},{3,19},{4,20},{5,21},{6,22},{7,23},{8,24},{9,... | collective-permute-start | bytes 6152 | tf_op jit(solution)/shard_map/ppermute | solution.py:26
  53.5 51.3 %copy-start.8 = (s32[8]{0:T(128)S(1)}, s32[8]{0:T(128)}, u32[]{:S(2)}) copy-start(s32[8]{0:T(128)} %param.17) | copy-start | bytes 100
  53.7 13.6 %collective-permute-start.6 = (bf16[256,128]{1,0:T(8,128)(2,1)S(1)}, bf16[256,128]{1,0:T(8,128)(2,1)S(1)}, u32[]{:S(2)}, u32[]{:S(2)}) collective-permute-start(bf16[256,128]{1,0:T(8,128)(2,1)S(1)} %bitcast.395), channel_id=1, source_target_pairs={{0,32},{1,33},{2,34},{3,35},{4,36},{5,37},{6,38},{7,39},{8,40},{9,... | collective-permute-start | bytes 196616 | tf_op jit(solution)/shard_map/ppermute | solution.py:26
  56.6 7.6 %collective-permute-start.13 = (bf16[64,8]{0,1:T(8,128)(2,1)S(1)}, bf16[64,8]{0,1:T(8,128)(2,1)S(1)}, u32[]{:S(2)}, u32[]{:S(2)}) collective-permute-start(bf16[64,8]{0,1:T(8,128)(2,1)S(1)} %bitcast.420), channel_id=1, source_target_pairs={{0,8},{1,9},{2,10},{3,11},{4,12},{5,13},{6,14},{7,15},{8,0},{9,1},... | collective-permute-start | bytes 3080 | tf_op jit(solution)/shard_map/ppermute | solution.py:26
  64.3 4.6 %collective-permute-start.14 = (bf16[32,8]{0,1:T(8,128)(2,1)S(1)}, bf16[32,8]{0,1:T(8,128)(2,1)S(1)}, u32[]{:S(2)}, u32[]{:S(2)}) collective-permute-start(bf16[32,8]{0,1:T(8,128)(2,1)S(1)} %convert_bitcast_fusion.3), channel_id=1, source_target_pairs={{0,4},{1,5},{2,6},{3,7},{4,0},{5,1},{6,2},{7,3},{8,12},{9,13},{10,... | collective-permute-start | bytes 1544 | tf_op jit(solution)/shard_map/ppermute | solution.py:26
  67.3 4.0 %collective-permute-start.7 = (bf16[128,128]{1,0:T(8,128)(2,1)S(1)}, bf16[128,128]{1,0:T(8,128)(2,1)S(1)}, u32[]{:S(2)}, u32[]{:S(2)}) collective-permute-start(bf16[128,128]{1,0:T(8,128)(2,1)S(1)} %fusion.103), channel_id=1, source_target_pairs={{0,16},{1,17},{2,18},{3,19},{4,20},{5,21},{6,22},{7,23},{8,24},{9,... | collective-permute-start | bytes 98312 | tf_op jit(solution)/shard_map/ppermute | solution.py:26
  68.9 45.7 %copy-start.1 = (bf16[2,6,256,128]{3,2,1,0:T(8,128)(2,1)S(1)}, bf16[2,6,256,128]{3,2,1,0:T(8,128)(2,1)}, u32[]{:S(2)}) copy-start(bf16[2,6,256,128]{3,2,1,0:T(8,128)(2,1)} %param.23) | copy-start | bytes 2359300
  71.4 7.9 %collective-permute-start.8 = (bf16[64,128]{1,0:T(8,128)(2,1)S(1)}, bf16[64,128]{1,0:T(8,128)(2,1)S(1)}, u32[]{:S(2)}, u32[]{:S(2)}) collective-permute-start(bf16[64,128]{1,0:T(8,128)(2,1)S(1)} %fusion.109), channel_id=1, source_target_pairs={{0,8},{1,9},{2,10},{3,11},{4,12},{5,13},{6,14},{7,15},{8,0},{9,1},... | collective-permute-start | bytes 49160 | tf_op jit(solution)/shard_map/ppermute | solution.py:26
  79.3 4.8 %collective-permute-start.9 = (bf16[32,128]{1,0:T(8,128)(2,1)S(1)}, bf16[32,128]{1,0:T(8,128)(2,1)S(1)}, u32[]{:S(2)}, u32[]{:S(2)}) collective-permute-start(bf16[32,128]{1,0:T(8,128)(2,1)S(1)} %fusion.130), channel_id=1, source_target_pairs={{0,4},{1,5},{2,6},{3,7},{4,0},{5,1},{6,2},{7,3},{8,12},{9,13},{10,... | collective-permute-start | bytes 24584 | tf_op jit(solution)/shard_map/ppermute | solution.py:26
  79.9 4.3 %collective-permute-start.15 = (bf16[16,8]{0,1:T(8,128)(2,1)S(1)}, bf16[16,8]{0,1:T(8,128)(2,1)S(1)}, u32[]{:S(2)}, u32[]{:S(2)}) collective-permute-start(bf16[16,8]{0,1:T(8,128)(2,1)S(1)} %bitcast.419), channel_id=1, source_target_pairs={{0,2},{1,3},{2,0},{3,1},{4,6},{5,7},{6,4},{7,5},{8,10},{9,11},{10,... | collective-permute-start | bytes 776 | tf_op jit(solution)/shard_map/ppermute | solution.py:26
  84.1 3.7 %collective-permute-start.10 = (bf16[16,128]{1,0:T(8,128)(2,1)S(1)}, bf16[16,128]{1,0:T(8,128)(2,1)S(1)}, u32[]{:S(2)}, u32[]{:S(2)}) collective-permute-start(bf16[16,128]{1,0:T(8,128)(2,1)S(1)} %fusion.148), channel_id=1, source_target_pairs={{0,2},{1,3},{2,0},{3,1},{4,6},{5,7},{6,4},{7,5},{8,10},{9,11},{10,... | collective-permute-start | bytes 12296 | tf_op jit(solution)/shard_map/ppermute | solution.py:26
  91.5 3.7 %collective-permute-start.16 = (bf16[16,256]{1,0:T(8,128)(2,1)S(1)}, bf16[16,256]{1,0:T(8,128)(2,1)S(1)}, u32[]{:S(2)}, u32[]{:S(2)}) collective-permute-start(bf16[16,256]{1,0:T(8,128)(2,1)S(1)} %fusion.187), channel_id=1, source_target_pairs={{0,2},{1,3},{2,0},{3,1},{4,6},{5,7},{6,4},{7,5},{8,10},{9,11},{10,... | collective-permute-start | bytes 24584 | tf_op jit(solution)/shard_map/ppermute | solution.py:26
  95.3 4.7 %collective-permute-start.17 = (bf16[32,256]{1,0:T(8,128)(2,1)S(1)}, bf16[32,256]{1,0:T(8,128)(2,1)S(1)}, u32[]{:S(2)}, u32[]{:S(2)}) collective-permute-start(bf16[32,256]{1,0:T(8,128)(2,1)S(1)} %pad_maximum_fusion.17), channel_id=1, source_target_pairs={{0,4},{1,5},{2,6},{3,7},{4,0},{5,1},{6,2},{7,3},{8,12},{9,13},{10,... | collective-permute-start | bytes 49160 | tf_op jit(solution)/shard_map/ppermute | solution.py:26
  100.0 8.2 %collective-permute-start.18 = (bf16[64,256]{1,0:T(8,128)(2,1)S(1)}, bf16[64,256]{1,0:T(8,128)(2,1)S(1)}, u32[]{:S(2)}, u32[]{:S(2)}) collective-permute-start(bf16[64,256]{1,0:T(8,128)(2,1)S(1)} %pad_maximum_fusion.15), channel_id=1, source_target_pairs={{0,8},{1,9},{2,10},{3,11},{4,12},{5,13},{6,14},{7,15},{8,0},{9,1},... | collective-permute-start | bytes 98312 | tf_op jit(solution)/shard_map/ppermute | solution.py:26
  108.2 4.4 %collective-permute-start.19 = (bf16[128,256]{1,0:T(8,128)(2,1)S(1)}, bf16[128,256]{1,0:T(8,128)(2,1)S(1)}, u32[]{:S(2)}, u32[]{:S(2)}) collective-permute-start(bf16[128,256]{1,0:T(8,128)(2,1)S(1)} %pad_maximum_fusion.13), channel_id=1, source_target_pairs={{0,16},{1,17},{2,18},{3,19},{4,20},{5,21},{6,22},{7,23},{8,24},{9,... | collective-permute-start | bytes 196616 | tf_op jit(solution)/shard_map/ppermute | solution.py:26
  112.6 6.6 %collective-permute-start.20 = (bf16[256,256]{1,0:T(8,128)(2,1)S(1)}, bf16[256,256]{1,0:T(8,128)(2,1)S(1)}, u32[]{:S(2)}, u32[]{:S(2)}) collective-permute-start(bf16[256,256]{1,0:T(8,128)(2,1)S(1)} %pad_maximum_fusion.3), channel_id=1, source_target_pairs={{0,32},{1,33},{2,34},{3,35},{4,36},{5,37},{6,38},{7,39},{8,40},{9,... | collective-permute-start | bytes 393224 | tf_op jit(solution)/shard_map/ppermute | solution.py:26
  123.0 3.8 %collective-permute-start.21 = (f32[1,8,512]{2,1,0:T(8,128)S(1)}, f32[1,8,512]{2,1,0:T(8,128)S(1)}, u32[]{:S(2)}, u32[]{:S(2)}) collective-permute-start(f32[1,8,512]{2,1,0:T(8,128)S(1)} %bitcast.394), channel_id=1, source_target_pairs={{0,2},{1,3},{2,0},{3,1},{4,6},{5,7},{6,4},{7,5},{8,10},{9,11},{10,... | collective-permute-start | bytes 49160 | tf_op jit(solution)/shard_map/ppermute | solution.py:26
  126.8 4.6 %collective-permute-start.22 = (f32[1,8,512]{2,1,0:T(8,128)S(1)}, f32[1,8,512]{2,1,0:T(8,128)S(1)}, u32[]{:S(2)}, u32[]{:S(2)}) collective-permute-start(f32[1,8,512]{2,1,0:T(8,128)S(1)} %bitcast_maximum_fusion), channel_id=1, source_target_pairs={{0,4},{1,5},{2,6},{3,7},{4,0},{5,1},{6,2},{7,3},{8,12},{9,13},{10,... | collective-permute-start | bytes 49160 | tf_op jit(solution)/shard_map/ppermute | solution.py:26
  131.5 7.6 %collective-permute-start.23 = (f32[1,8,512]{2,1,0:T(8,128)S(1)}, f32[1,8,512]{2,1,0:T(8,128)S(1)}, u32[]{:S(2)}, u32[]{:S(2)}) collective-permute-start(f32[1,8,512]{2,1,0:T(8,128)S(1)} %max.56), channel_id=1, source_target_pairs={{0,8},{1,9},{2,10},{3,11},{4,12},{5,13},{6,14},{7,15},{8,0},{9,1},... | collective-permute-start | bytes 49160 | tf_op jit(solution)/shard_map/ppermute | solution.py:26
  139.1 3.7 %collective-permute-start.24 = (f32[1,8,512]{2,1,0:T(8,128)S(1)}, f32[1,8,512]{2,1,0:T(8,128)S(1)}, u32[]{:S(2)}, u32[]{:S(2)}) collective-permute-start(f32[1,8,512]{2,1,0:T(8,128)S(1)} %max.57), channel_id=1, source_target_pairs={{0,16},{1,17},{2,18},{3,19},{4,20},{5,21},{6,22},{7,23},{8,24},{9,... | collective-permute-start | bytes 49160 | tf_op jit(solution)/shard_map/ppermute | solution.py:26
  142.9 5.2 %collective-permute-start.25 = (f32[1,8,512]{2,1,0:T(8,128)S(1)}, f32[1,8,512]{2,1,0:T(8,128)S(1)}, u32[]{:S(2)}, u32[]{:S(2)}) collective-permute-start(f32[1,8,512]{2,1,0:T(8,128)S(1)} %max.58), channel_id=1, source_target_pairs={{0,32},{1,33},{2,34},{3,35},{4,36},{5,37},{6,38},{7,39},{8,40},{9,... | collective-permute-start | bytes 49160 | tf_op jit(solution)/shard_map/ppermute | solution.py:26
  148.5 5.4 %collective-permute-start.31 = (bf16[256,8]{0,1:T(8,128)(2,1)S(1)}, bf16[256,8]{0,1:T(8,128)(2,1)S(1)}, u32[]{:S(2)}, u32[]{:S(2)}) collective-permute-start(bf16[256,8]{0,1:T(8,128)(2,1)S(1)} %fusion.144), channel_id=1, source_target_pairs={{0,32},{1,33},{2,34},{3,35},{4,36},{5,37},{6,38},{7,39},{8,40},{9,... | collective-permute-start | bytes 12296 | tf_op jit(solution)/shard_map/ppermute | solution.py:26
  153.9 3.6 %collective-permute-start.32 = (bf16[128,8]{0,1:T(8,128)(2,1)S(1)}, bf16[128,8]{0,1:T(8,128)(2,1)S(1)}, u32[]{:S(2)}, u32[]{:S(2)}) collective-permute-start(bf16[128,8]{0,1:T(8,128)(2,1)S(1)} %fusion.160), channel_id=1, source_target_pairs={{0,16},{1,17},{2,18},{3,19},{4,20},{5,21},{6,22},{7,23},{8,24},{9,... | collective-permute-start | bytes 6152 | tf_op jit(solution)/shard_map/ppermute | solution.py:26
  154.9 10.8 %collective-permute-start.26 = (bf16[256,128]{1,0:T(8,128)(2,1)S(1)}, bf16[256,128]{1,0:T(8,128)(2,1)S(1)}, u32[]{:S(2)}, u32[]{:S(2)}) collective-permute-start(bf16[256,128]{1,0:T(8,128)(2,1)S(1)} %bitcast.396), channel_id=1, source_target_pairs={{0,32},{1,33},{2,34},{3,35},{4,36},{5,37},{6,38},{7,39},{8,40},{9,... | collective-permute-start | bytes 196616 | tf_op jit(solution)/shard_map/ppermute | solution.py:26
  157.6 7.6 %collective-permute-start.33 = (bf16[64,8]{0,1:T(8,128)(2,1)S(1)}, bf16[64,8]{0,1:T(8,128)(2,1)S(1)}, u32[]{:S(2)}, u32[]{:S(2)}) collective-permute-start(bf16[64,8]{0,1:T(8,128)(2,1)S(1)} %bitcast.421), channel_id=1, source_target_pairs={{0,8},{1,9},{2,10},{3,11},{4,12},{5,13},{6,14},{7,15},{8,0},{9,1},... | collective-permute-start | bytes 3080 | tf_op jit(solution)/shard_map/ppermute | solution.py:26
  165.3 4.6 %collective-permute-start.34 = (bf16[32,8]{0,1:T(8,128)(2,1)S(1)}, bf16[32,8]{0,1:T(8,128)(2,1)S(1)}, u32[]{:S(2)}, u32[]{:S(2)}) collective-permute-start(bf16[32,8]{0,1:T(8,128)(2,1)S(1)} %convert_bitcast_fusion.2), channel_id=1, source_target_pairs={{0,4},{1,5},{2,6},{3,7},{4,0},{5,1},{6,2},{7,3},{8,12},{9,13},{10,... | collective-permute-start | bytes 1544 | tf_op jit(solution)/shard_map/ppermute | solution.py:26
  165.7 4.3 %collective-permute-start.27 = (bf16[128,128]{1,0:T(8,128)(2,1)S(1)}, bf16[128,128]{1,0:T(8,128)(2,1)S(1)}, u32[]{:S(2)}, u32[]{:S(2)}) collective-permute-start(bf16[128,128]{1,0:T(8,128)(2,1)S(1)} %fusion.104), channel_id=1, source_target_pairs={{0,16},{1,17},{2,18},{3,19},{4,20},{5,21},{6,22},{7,23},{8,24},{9,... | collective-permute-start | bytes 98312 | tf_op jit(solution)/shard_map/ppermute | solution.py:26
  170.0 7.7 %collective-permute-start.28 = (bf16[64,128]{1,0:T(8,128)(2,1)S(1)}, bf16[64,128]{1,0:T(8,128)(2,1)S(1)}, u32[]{:S(2)}, u32[]{:S(2)}) collective-permute-start(bf16[64,128]{1,0:T(8,128)(2,1)S(1)} %fusion.110), channel_id=1, source_target_pairs={{0,8},{1,9},{2,10},{3,11},{4,12},{5,13},{6,14},{7,15},{8,0},{9,1},... | collective-permute-start | bytes 49160 | tf_op jit(solution)/shard_map/ppermute | solution.py:26
  177.8 4.6 %collective-permute-start.29 = (bf16[32,128]{1,0:T(8,128)(2,1)S(1)}, bf16[32,128]{1,0:T(8,128)(2,1)S(1)}, u32[]{:S(2)}, u32[]{:S(2)}) collective-permute-start(bf16[32,128]{1,0:T(8,128)(2,1)S(1)} %fusion.131), channel_id=1, source_target_pairs={{0,4},{1,5},{2,6},{3,7},{4,0},{5,1},{6,2},{7,3},{8,12},{9,13},{10,... | collective-permute-start | bytes 24584 | tf_op jit(solution)/shard_map/ppermute | solution.py:26
  180.3 3.7 %collective-permute-start.35 = (bf16[16,8]{0,1:T(8,128)(2,1)S(1)}, bf16[16,8]{0,1:T(8,128)(2,1)S(1)}, u32[]{:S(2)}, u32[]{:S(2)}) collective-permute-start(bf16[16,8]{0,1:T(8,128)(2,1)S(1)} %bitcast.418), channel_id=1, source_target_pairs={{0,2},{1,3},{2,0},{3,1},{4,6},{5,7},{6,4},{7,5},{8,10},{9,11},{10,... | collective-permute-start | bytes 776 | tf_op jit(solution)/shard_map/ppermute | solution.py:26
  182.4 3.7 %collective-permute-start.30 = (bf16[16,128]{1,0:T(8,128)(2,1)S(1)}, bf16[16,128]{1,0:T(8,128)(2,1)S(1)}, u32[]{:S(2)}, u32[]{:S(2)}) collective-permute-start(bf16[16,128]{1,0:T(8,128)(2,1)S(1)} %fusion.145), channel_id=1, source_target_pairs={{0,2},{1,3},{2,0},{3,1},{4,6},{5,7},{6,4},{7,5},{8,10},{9,11},{10,... | collective-permute-start | bytes 12296 | tf_op jit(solution)/shard_map/ppermute | solution.py:26
  189.1 3.7 %collective-permute-start.36 = (bf16[16,256]{1,0:T(8,128)(2,1)S(1)}, bf16[16,256]{1,0:T(8,128)(2,1)S(1)}, u32[]{:S(2)}, u32[]{:S(2)}) collective-permute-start(bf16[16,256]{1,0:T(8,128)(2,1)S(1)} %divide_convert_fusion), channel_id=1, source_target_pairs={{0,2},{1,3},{2,0},{3,1},{4,6},{5,7},{6,4},{7,5},{8,10},{9,11},{10,... | collective-permute-start | bytes 24584 | tf_op jit(solution)/shard_map/ppermute | solution.py:26
  192.8 4.7 %collective-permute-start.37 = (bf16[32,256]{1,0:T(8,128)(2,1)S(1)}, bf16[32,256]{1,0:T(8,128)(2,1)S(1)}, u32[]{:S(2)}, u32[]{:S(2)}) collective-permute-start(bf16[32,256]{1,0:T(8,128)(2,1)S(1)} %pad_maximum_fusion.18), channel_id=1, source_target_pairs={{0,4},{1,5},{2,6},{3,7},{4,0},{5,1},{6,2},{7,3},{8,12},{9,13},{10,... | collective-permute-start | bytes 49160 | tf_op jit(solution)/shard_map/ppermute | solution.py:26
  197.6 7.9 %collective-permute-start.38 = (bf16[64,256]{1,0:T(8,128)(2,1)S(1)}, bf16[64,256]{1,0:T(8,128)(2,1)S(1)}, u32[]{:S(2)}, u32[]{:S(2)}) collective-permute-start(bf16[64,256]{1,0:T(8,128)(2,1)S(1)} %pad_maximum_fusion.16), channel_id=1, source_target_pairs={{0,8},{1,9},{2,10},{3,11},{4,12},{5,13},{6,14},{7,15},{8,0},{9,1},... | collective-permute-start | bytes 98312 | tf_op jit(solution)/shard_map/ppermute | solution.py:26
  205.5 4.4 %collective-permute-start.39 = (bf16[128,256]{1,0:T(8,128)(2,1)S(1)}, bf16[128,256]{1,0:T(8,128)(2,1)S(1)}, u32[]{:S(2)}, u32[]{:S(2)}) collective-permute-start(bf16[128,256]{1,0:T(8,128)(2,1)S(1)} %pad_maximum_fusion.14), channel_id=1, source_target_pairs={{0,16},{1,17},{2,18},{3,19},{4,20},{5,21},{6,22},{7,23},{8,24},{9,... | collective-permute-start | bytes 196616 | tf_op jit(solution)/shard_map/ppermute | solution.py:26
  209.9 6.6 %collective-permute-start.40 = (bf16[256,256]{1,0:T(8,128)(2,1)S(1)}, bf16[256,256]{1,0:T(8,128)(2,1)S(1)}, u32[]{:S(2)}, u32[]{:S(2)}) collective-permute-start(bf16[256,256]{1,0:T(8,128)(2,1)S(1)} %pad_maximum_fusion.4), channel_id=1, source_target_pairs={{0,32},{1,33},{2,34},{3,35},{4,36},{5,37},{6,38},{7,39},{8,40},{9,... | collective-permute-start | bytes 393224 | tf_op jit(solution)/shard_map/ppermute | solution.py:26
  218.2 1.2 copy-start.7
  219.8 4.0 %collective-permute-start.41 = (f32[1,64,64]{2,1,0:T(8,128)S(1)}, f32[1,64,64]{2,1,0:T(8,128)S(1)}, u32[]{:S(2)}, u32[]{:S(2)}) collective-permute-start(f32[1,64,64]{2,1,0:T(8,128)S(1)} %bitcast.403), channel_id=1, source_target_pairs={{0,1},{1,0},{2,3},{3,2},{4,5},{5,4},{6,7},{7,6},{8,9},{9,8},{10,11... | collective-permute-start | bytes 49160 | tf_op jit(solution)/shard_map/ppermute | solution.py:26
where the time goes:
time: 225 us; the launch traced here: 224 us
  waiting for transfers between devices  95.9 us (43%)
  starting transfers between devices  83 us (37%)
  matrix products  17.4 us (8%)
  blocking collectives  8.87 us (4%)
  local copies, waits for them, and re-layouts  8.32 us (4%)
  other arithmetic  7.31 us (3%)
  between operations  3.75 us (2%)
    ppermute x42, waiting for transfers between devices, partner(): lax.ppermute(x, axis, [(i, i ^ 1 << distance) for i in range(lax.axis_siz...  95.9 us
    ppermute x42, starting transfers between devices, partner(): lax.ppermute(x, axis, [(i, i ^ 1 << distance) for i in range(lax.axis_siz...  83 us
    dot_general x19, matrix products, bdot(): return jnp.dot(left, right, preferred_element_type=jnp.float32)  13 us
    all_gather x1, blocking collectives, side_by_side(): whole = lax.all_gather(both, axis, axis=dim, tiled=True)  8.87 us
  transfers between devices with their start and end apart: 42, of which 35 were waited for; matrix products, arithmetic and copies ran while one was open for 5% of the time, Pallas kernels for 0%

commit v1 on v0

v1 whole, which is shorter than its diff:
```python
import math

import jax
import jax.numpy as jnp
from jax import lax
from jax.sharding import Mesh
from jax.sharding import PartitionSpec as P

HEADS = 8
GRID = 64
IMG_PIX = 1024
TOKS_P = 8
LAYERS = 2
NORM_EPS = 0.01
SPLIT = ("section", "x", "zh", "zl", "y")
IMG = ("x", "zh", "zl", "y")
bf16 = jnp.bfloat16
f32 = jnp.float32


def bdot(left, right):
    return jnp.dot(left, right, preferred_element_type=f32)


def norm_rows(values):
    center = values - jnp.mean(values, axis=-1, keepdims=True)
    spread = jnp.mean(center * center, axis=-1, keepdims=True)
    return center / jnp.sqrt(spread + NORM_EPS)


def swapped(x, axis, distance):
    return lax.ppermute(x, axis, [(i, i ^ distance) for i in range(lax.axis_size(axis))])


def fourier(coord_x, coord_y, pe_basis):
    phase = (2.0 * coord_x - 1.0)[..., None] * pe_basis[0] + (2.0 * coord_y - 1.0)[
        ..., None
    ] * pe_basis[1]
    phase = 2.0 * math.pi * phase
    return jnp.concatenate([jnp.sin(phase), jnp.cos(phase)], axis=-1)


def grid_code(grid_rows, pe_basis):
    column = (jnp.arange(GRID, dtype=f32) + 0.5) / GRID
    row = (grid_rows.astype(f32) + 0.5) / GRID
    a = 2.0 * math.pi * (2.0 * column - 1.0)[:, None] * pe_basis[0]
    b = 2.0 * math.pi * (2.0 * row - 1.0)[:, None] * pe_basis[1]
    sa, ca = jnp.sin(a)[None], jnp.cos(a)[None]
    sb, cb = jnp.sin(b)[:, None], jnp.cos(b)[:, None]
    code = jnp.concatenate([sa * cb + ca * sb, ca * cb - sa * sb], axis=-1)
    return code.reshape(-1, code.shape[-1])


def start_tokens(box_rows, token_table, pe_basis):
    coords = (box_rows.astype(f32) + 0.5) / IMG_PIX
    corner_one = fourier(coords[:, 0], coords[:, 1], pe_basis)
    corner_two = fourier(coords[:, 2], coords[:, 3], pe_basis)
    slots = jnp.arange(TOKS_P)[None, :, None]
    tokens = token_table[None] + jnp.where(slots == TOKS_P - 2, corner_one[:, None, :], 0.0)
    tokens = tokens + jnp.where(slots == TOKS_P - 1, corner_two[:, None, :], 0.0)
    return tokens.reshape(-1, token_table.shape[-1])


def pieces(v):
    hi = lax.reduce_precision(v, 8, 7)
    rest = v - hi
    mid = lax.reduce_precision(rest, 8, 7)
    low = rest - mid
    return [hi.astype(bf16), mid.astype(bf16), low.astype(bf16)]


def partial_attend(query, keys, values):
    toks, width = query.shape
    size = width // HEADS
    scores = jnp.einsum(
        "khd,qhd->hkq",
        keys.reshape(-1, HEADS, size),
        query.reshape(-1, HEADS, size),
        preferred_element_type=f32,
    ) * size ** (-0.5)
    top = jnp.max(scores, axis=1)
    weights = jnp.exp(scores - top[:, None]).astype(bf16)
    summed = jnp.einsum(
        "hkq,khd->hdq", weights, values.reshape(-1, HEADS, size), preferred_element_type=f32
    )
    total = jnp.sum(weights.astype(f32), axis=1)
    return jnp.concatenate(
        [summed.reshape(width, toks).astype(bf16), total.astype(bf16)] + pieces(top), axis=0
    )


def combined(parts):
    width = parts.shape[1] - 4 * HEADS
    parts = parts.astype(f32)
    summed, total = parts[:, :width], parts[:, width : width + HEADS]
    hi, mid, low = (
        parts[:, width + (k + 1) * HEADS : width + (k + 2) * HEADS] for k in range(3)
    )
    top = hi + (mid + low)
    share = jnp.exp(top - jnp.max(top, axis=0, keepdims=True))
    size = width // HEADS
    total = jnp.sum(total * share, axis=0)
    summed = jnp.sum(summed.reshape(-1, HEADS, size, summed.shape[-1]) * share[:, :, None], axis=0)
    return (summed / total[:, None]).reshape(width, -1).T


def token_step(parts, tok, out_w, up, down):
    first = combined(parts)
    two = norm_rows(tok + bdot(first.astype(bf16), out_w))
    hidden = jax.nn.relu(bdot(two.astype(bf16), up)).astype(bf16)
    return norm_rows(two + bdot(hidden, down))


def image_step(image, key_bf, toks, live, w_q, w_k, w_v, w_o):
    query = bdot(key_bf, w_q).astype(bf16)
    keys = bdot(toks, w_k).astype(bf16)
    values = bdot(toks, w_v).astype(bf16)
    size = query.shape[1] // HEADS
    scores = jnp.einsum(
        "qhd,khd->hqk",
        query.reshape(-1, HEADS, size),
        keys.reshape(-1, HEADS, size),
        preferred_element_type=f32,
    ) * size ** (-0.5)
    scores = jnp.where(live[None, None, :], scores, -jnp.inf)
    top = jnp.max(scores, axis=-1, keepdims=True)
    weights = jnp.exp(scores - top).astype(bf16)
    summed = jnp.einsum(
        "hqk,khd->qhd", weights, values.reshape(-1, HEADS, size), preferred_element_type=f32
    )
    total = jnp.sum(weights.astype(f32), axis=-1).T
    second = (summed / total[:, :, None]).reshape(query.shape)
    return norm_rows(image + bdot(second.astype(bf16), w_o))


def shards(
    early_feats,
    final_embed,
    prompt_counts,
    box_pixels,
    pair_table,
    token_table,
    pe_basis,
    w_early,
    attend_in,
    attend_out,
    mlp_up,
    mlp_down,
    w_hyper,
):
    images, pos_dev, width = final_embed.shape
    prompts = box_pixels.shape[1]
    n_x, n_zh, n_zl, n_y = (lax.axis_size(a) for a in IMG)
    section = lax.axis_index("section")
    my_x, my_zh, my_zl, my_y = (lax.axis_index(a) for a in IMG)
    mine = section * images + my_y

    sent = jnp.broadcast_to(final_embed[None], (n_x * n_zh,) + final_embed.shape)
    sent = sent.reshape(n_x * n_zh * n_y, pos_dev, width)
    held = lax.all_to_all(sent, ("x", "zh", "y"), 0, 0, tiled=True)
    image = held.reshape(-1, width).astype(f32)

    hq = jax.nn.gelu(bdot(early_feats, w_early), approximate=False).astype(bf16)
    hq_keep = lax.dynamic_index_in_dim(hq, my_y, 0, keepdims=False)
    hq_send = lax.dynamic_index_in_dim(hq, 1 - my_y, 0, keepdims=False)
    hq_got = swapped(hq_send, "y", 1)
    hq_here = jnp.where(
        my_y == 0,
        jnp.concatenate([hq_keep, hq_got], axis=0),
        jnp.concatenate([hq_got, hq_keep], axis=0),
    )

    ids = jnp.arange(n_x * n_zh * n_y, dtype=jnp.int32)
    grid_rows = (ids // 4) * (n_zh * n_zl * n_y) + (ids // 2 % 2) * (n_zl * n_y)
    grid_rows = grid_rows + my_zl * n_y + ids % 2
    code = grid_code(grid_rows, pe_basis)
    count = prompt_counts[mine]
    boxes = lax.dynamic_index_in_dim(box_pixels, mine, 0, keepdims=False)
    own_prompts = prompts // n_x
    boxes = lax.dynamic_slice_in_dim(boxes, my_x * own_prompts, own_prompts, 0)
    tok = start_tokens(boxes, token_table, pe_basis)
    live_prompt = jnp.arange(prompts, dtype=jnp.int32) < count
    live = jnp.repeat(live_prompt, TOKS_P)
    tok_b = tok.astype(bf16)
    own_pos = n_y * pos_dev
    for layer in range(LAYERS):
        w = attend_in[layer]
        image_bf = image.astype(bf16)
        key_bf = (image + code).astype(bf16)
        query = bdot(tok_b, w[0]).astype(bf16)
        keys = bdot(key_bf, w[1]).astype(bf16)
        values = bdot(image_bf, w[2]).astype(bf16)
        part = partial_attend(query, keys, values)
        parts = jnp.stack([part] + [swapped(part, "zl", d) for d in range(1, n_zl)])
        tok = token_step(parts, tok, attend_out[layer, 0], mlp_up[layer], mlp_down[layer])
        tok_b = tok.astype(bf16)
        got = jnp.stack([tok_b] + [swapped(tok_b, "x", d) for d in range(1, n_x)])
        toks = jnp.take(got, jnp.arange(n_x, dtype=jnp.int32) ^ my_x, axis=0).reshape(-1, width)
        if layer == LAYERS - 1:
            start = (my_x * n_zh + my_zh) * own_pos
            image = lax.dynamic_slice_in_dim(image, start, own_pos, 0)
            key_bf = lax.dynamic_slice_in_dim(key_bf, start, own_pos, 0)
        image = image_step(image, key_bf, toks, live, w[3], w[4], w[5], attend_out[layer, 1])
    hyper = bdot(toks.reshape(-1, TOKS_P, width)[:, TOKS_P - 3], w_hyper).astype(bf16)
    feats = (image + hq_here.astype(f32)).astype(bf16)
    logits = lax.dot_general(
        hyper, feats, (((1,), (1,)), ((), ())), preferred_element_type=f32
    ) * width ** (-0.5)
    masks = jnp.where(live_prompt[:, None], logits, 0.0)

    halves = [masks[:, :pos_dev], masks[:, pos_dev:]]
    keep = jnp.where(my_y == 0, halves[0], halves[1])
    give = jnp.where(my_y == 0, halves[1], halves[0])
    got = swapped(give, "y", 1)
    both = jnp.where(my_y == 0, jnp.stack([keep, got]), jnp.stack([got, keep]))
    every = jnp.stack(
        [both] + [swapped(both, "section", d) for d in range(1, lax.axis_size("section"))]
    )
    table = lax.dynamic_slice_in_dim(pair_table, section * images, images, 0)
    chosen = lax.dynamic_index_in_dim(every, (table[0] // images) ^ section, 0, keepdims=False)
    swap = (table[0] % images) == 1
    return jnp.where(swap, chosen[::-1], chosen)


def solution(mesh):
    n_sec, n_img = mesh.devices.shape
    fine = Mesh(mesh.devices.reshape(n_sec, 4, 2, 4, 2), SPLIT)
    placed = (P("section", IMG, None),) * 2 + (P(),) * 11
    return jax.shard_map(
        shards, mesh=fine, in_specs=placed, out_specs=P("section", None, IMG), check_vma=False
    )
```

time: 225 us -> 114 us (0.51)
  the two profiles are of different devices: /device:TPU:32 before, /device:TPU:1 now
where the time goes in v1:
time: 114 us; the launch traced here: 113 us
  starting transfers between devices  44.8 us (39%)
  matrix products  31.7 us (28%)
  waiting for transfers between devices  19.1 us (17%)
  other arithmetic  11.3 us (10%)
  local copies, waits for them, and re-layouts  4.89 us (4%)
    ppermute x17, starting transfers between devices, swapped(): lax.ppermute(x, axis, [(i, i ^ distance) for i in range(lax.axis_size(axi...  32 us
    dot_general x19, matrix products, bdot(): return jnp.dot(left, right, preferred_element_type=f32)  21.9 us
    ppermute x17, waiting for transfers between devices, swapped(): lax.ppermute(x, axis, [(i, i ^ distance) for i in range(lax.axis_size(axi...  12.8 us
    all_to_all x1, starting transfers between devices, shards(): held = lax.all_to_all(sent, ('x', 'zh', 'y'), 0, 0, tiled=True)  12.7 us
    all_to_all x1, waiting for transfers between devices, shards(): held = lax.all_to_all(sent, ('x', 'zh', 'y'), 0, 0, tiled=True)  6.26 us
    reduce_sum x2, other arithmetic, image_step(): total = jnp.sum(weights.astype(f32), axis=-1).T  4.79 us
    dot_general x2, matrix products, image_step(): jnp.einsum('qhd,khd->hqk', query.reshape(-1, HEADS, size), keys.reshape(-...  3.67 us
  transfers between devices with their start and end apart: 18, of which 12 were waited for; matrix products, arithmetic and copies ran while one was open for 39% of the time, Pallas kernels for 0%

profile of v1, /device:TPU:1, one launch (start us, length us, event | category | flops | bytes accessed | tf_op | source)
XLA Modules:
  0.0 112.7 jit_solution(7279942515712391739)
XLA Ops:
  0.0 1.7 %broadcast_in_dim.156 = bf16[8,2,64,256]{3,2,1,0:T(8,128)(2,1)} broadcast(bf16[2,64,256]{2,1,0:T(8,128)(2,1)} %param.16), dimensions={1,2,3} | broadcast | bytes 589824 | tf_op jit(solution)/shard_map/broadcast_in_dim | solution.py:158
  1.8 12.7 %all-to-all-start = ((bf16[16,64,256]{2,1,0:T(8,128)(2,1)}), bf16[16,64,256]{2,1,0:T(8,128)(2,1)S(1)}, u32[]{:S(2)}, u32[]{:S(2)}) async-start(bf16[16,64,256]{2,1,0:T(8,128)(2,1)} %bitcast.12), calls=%async_computation | async-start | bytes 1048576 | tf_op jit(solution)/shard_map/all_to_all | solution.py:160
  14.5 1.5 %fusion.40 = bf16[2,64,256]{2,1,0:T(8,128)(2,1)S(1)} fusion(bf16[2,64,1280]{2,1,0:T(8,128)(2,1)} %param.15, bf16[1280,256]{1,0:T(8,128)(2,1)S(1)} %copy-done), kind=kOutput, calls=%fused_computation.90 | convolution fusion | flops 86016000 | bytes 1048576 | tf_op jit(solution)/shard_map/dot_general | solution.py:22
  16.1 1.4 %collective-permute-start.12 = (bf16[64,256]{0,1:T(8,128)(2,1)S(1)}, bf16[64,256]{0,1:T(8,128)(2,1)}, u32[]{:S(2)}, u32[]{:S(2)}) collective-permute-start(bf16[64,256]{0,1:T(8,128)(2,1)S(1)} %bitcast.285), channel_id=1, source_target_pairs={{0,1},{1,0},{2,3},{3,2},{4,5},{5,4},{6,7},{7,6},{8,9},{9,8},{10,11... | collective-permute-start | bytes 98312 | tf_op jit(solution)/shard_map/ppermute | solution.py:32
  17.6 0.8 fusion.137
  19.6 0.6 dynamic_slice.29
  20.2 0.6 iota_compare_fusion.2
  21.2 1.1 convolution_convert_fusion.12
  22.3 6.3 %all-to-all-done = bf16[16,64,256]{2,1,0:T(8,128)(2,1)S(1)} async-done(((bf16[16,64,256]{2,1,0:T(8,128)(2,1)}), bf16[16,64,256]{2,1,0:T(8,128)(2,1)S(1)}, u32[]{:S(2)}, u32[]{:S(2)}) %all-to-all-start) | async-done | bytes 524320 | tf_op jit(solution)/shard_map/all_to_all | solution.py:160
  28.5 1.1 %convolution_convert_fusion.4 = bf16[1024,128]{0,1:T(8,128)(2,1)S(1)} fusion(bf16[1024,256]{1,0:T(8,128)(2,1)S(1)} %bitcast.230, bf16[2,6,256,128]{3,2,1,0:T(8,128)(2,1)} %param.23), kind=kOutput, calls=%fused_computation.28 | convolution fusion | flops 67239936 | bytes 851968 | tf_op jit(solution)/shard_map/dot_general | solution.py:22
  29.8 1.2 %convolution_convert_fusion.3 = bf16[1024,128]{0,1:T(8,128)(2,1)S(1)} fusion(bf16[1024,256]{1,0:T(8,128)(2,1)S(1)} %bitcast.234, bf16[2,6,256,128]{3,2,1,0:T(8,128)(2,1)} %param.23), kind=kOutput, calls=%fused_computation.27 | convolution fusion | flops 67239936 | bytes 851968 | tf_op jit(solution)/shard_map/dot_general | solution.py:22
  31.0 0.8 multiply_reduce_fusion.1
  31.8 0.7 fusion.34
  32.5 0.8 convolution_convert_fusion.14
  33.3 2.0 %collective-permute-start.2 = (bf16[160,128]{1,0:T(8,128)(2,1)S(1)}, bf16[160,128]{1,0:T(8,128)(2,1)S(1)}, u32[]{:S(2)}, u32[]{:S(2)}) collective-permute-start(bf16[160,128]{1,0:T(8,128)(2,1)S(1)} %constant_dynamic-update-slice_fusion), channel_id=1, source_target_pairs={{0,6},{2,4},{4,2},{6,0},{1,7},{3,5},{5,3},{7,1},{8,14},{10,12},{12... | collective-permute-start | bytes 122888 | tf_op jit(solution)/shard_map/ppermute | solution.py:32
  35.3 5.0 %collective-permute-start.1 = (bf16[160,128]{1,0:T(8,128)(2,1)S(1)}, bf16[160,128]{1,0:T(8,128)(2,1)S(1)}, u32[]{:S(2)}, u32[]{:S(2)}) collective-permute-start(bf16[160,128]{1,0:T(8,128)(2,1)S(1)} %constant_dynamic-update-slice_fusion), channel_id=1, source_target_pairs={{0,4},{2,6},{4,0},{6,2},{1,5},{3,7},{5,1},{7,3},{8,12},{10,14},{12... | collective-permute-start | bytes 122888 | tf_op jit(solution)/shard_map/ppermute | solution.py:32
  40.3 1.1 %convolution_convert_fusion.2 = bf16[1024,128]{0,1:T(8,128)(2,1)S(1)} fusion(bf16[1024,256]{1,0:T(8,128)(2,1)S(1)} %bitcast.235, bf16[2,6,256,128]{3,2,1,0:T(8,128)(2,1)} %param.23), kind=kOutput, calls=%fused_computation.26 | convolution fusion | flops 67239936 | bytes 851968 | tf_op jit(solution)/shard_map/dot_general | solution.py:22
  41.7 0.5 collective-permute-done.1
  42.2 1.0 collective-permute-done
  43.3 1.1 fusion.158
  44.7 2.2 %fusion.159 = (f32[128]{0:T(128)S(1)}, f32[128,256]{1,0:T(8,128)S(1)}) fusion(bf16[2,2048,256]{2,1,0:T(8,128)(2,1)} %param.26, bf16[2,256,2048]{2,1,0:T(8,128)(2,1)} %param.25, f32[128,256]{1,0:T(8,128)S(1)} %get-tuple-element.50, f32[128]{0:T(128)S(1)} %add_sqrt_fusion.5, f32[128]{0:T(128)S(1)} %broadcast_multiply_fusion.5), kind=kOutput, calls=%fused_computation.307 | convolution fusion | flops 269188992 | bytes 2492928 | tf_op jit(solution)/shard_map/dot_general | solution.py:22
  47.2 0.7 collective-permute-start.5
  47.9 1.1 collective-permute-start.4
  48.9 1.6 %collective-permute-start.3 = (bf16[128,256]{1,0:T(8,128)(2,1)S(1)}, bf16[128,256]{1,0:T(8,128)(2,1)S(1)}, u32[]{:S(2)}, u32[]{:S(2)}) collective-permute-start(bf16[128,256]{1,0:T(8,128)(2,1)S(1)} %fusion.157), channel_id=1, source_target_pairs={{0,16},{16,0},{32,48},{48,32},{1,17},{17,1},{33,49},{49,33},{2,18}... | collective-permute-start | bytes 196616 | tf_op jit(solution)/shard_map/ppermute | solution.py:32
  50.7 1.1 convolution_convert_fusion.11
  51.7 0.8 collective-permute-done.4
  52.5 0.4 collective-permute-done.3
  52.9 0.6 gather_fusion
  53.6 1.1 convolution_convert_fusion.8
  54.7 1.1 convolution_convert_fusion.7
  55.8 3.1 %fusion = (f32[8,1024]{1,0:T(8,128)S(1)}, f32[8,1024,512]{1,2,0:T(8,128)S(1)}) fusion(pred[512]{0:T(512)(128)(4,1)S(1)} %broadcast_in_dim.161, bf16[1024,8,16]{0,2,1:T(8,128)(2,1)S(1)} %bitcast.242, bf16[512,8,16]{0,2,1:T(8,128)(2,1)S(1)} %bitcast.255), kind=kOutput, calls=%fused_computation.5 | convolution fusion | flops 146792448 | bytes 17203712 | tf_op jit(solution)/shard_map/qhd,khd->hqk/dot_general | solution.py:119
  58.9 4.2 %convert_reduce_fusion = (f32[8,1024]{1,0:T(8,128)S(1)}, bf16[8,1024,512]{1,2,0:T(8,128)(2,1)S(1)}) fusion(f32[8,1024]{1,0:T(8,128)S(1)} %get-tuple-element.53, f32[8,1024,512]{1,2,0:T(8,128)S(1)} %get-tuple-element.54, pred[512]{0:T(512)(128)(4,1)S(1)} %broadcast_in_dim.161), kind=kLoop, calls=%fused_computation.2 | loop fusion | flops 25157632 | bytes 25231872 | tf_op jit(solution)/shard_map/reduce_sum | solution.py:131
  63.1 1.2 %fusion.7 = bf16[1024,8,16]{0,2,1:T(8,128)(2,1)S(1)} fusion(bf16[512,8,16]{0,2,1:T(8,128)(2,1)S(1)} %bitcast.248, bf16[8,1024,512]{1,2,0:T(8,128)(2,1)S(1)} %get-tuple-element.13, f32[1024,8]{0,1:T(8,128)S(1)} %bitcast.247), kind=kOutput, calls=%fused_computation.23 | convolution fusion | flops 134479872 | bytes 8814592 | tf_op jit(solution)/shard_map/hqk,khd->qhd/dot_general | solution.py:128
  65.2 1.1 convolution_convert_fusion.1
  66.3 1.1 convolution_convert_fusion
  67.4 0.8 multiply_reduce_fusion
  68.2 0.7 fusion.35
  68.9 0.7 convolution_convert_fusion.13
  69.7 1.7 %collective-permute-start.8 = (bf16[160,128]{1,0:T(8,128)(2,1)S(1)}, bf16[160,128]{1,0:T(8,128)(2,1)S(1)}, u32[]{:S(2)}, u32[]{:S(2)}) collective-permute-start(bf16[160,128]{1,0:T(8,128)(2,1)S(1)} %constant_dynamic-update-slice_fusion.5), channel_id=1, source_target_pairs={{0,6},{2,4},{4,2},{6,0},{1,7},{3,5},{5,3},{7,1},{8,14},{10,12},{12... | collective-permute-start | bytes 122888 | tf_op jit(solution)/shard_map/ppermute | solution.py:32
  71.7 1.6 %collective-permute-start.6 = (bf16[160,128]{1,0:T(8,128)(2,1)S(1)}, bf16[160,128]{1,0:T(8,128)(2,1)S(1)}, u32[]{:S(2)}, u32[]{:S(2)}) collective-permute-start(bf16[160,128]{1,0:T(8,128)(2,1)S(1)} %constant_dynamic-update-slice_fusion.5), channel_id=1, source_target_pairs={{0,2},{2,0},{4,6},{6,4},{1,3},{3,1},{5,7},{7,5},{8,10},{10,8},{12,... | collective-permute-start | bytes 122888 | tf_op jit(solution)/shard_map/ppermute | solution.py:32
  73.4 1.1 convolution_convert_fusion.9
  74.5 0.9 collective-permute-done.7
  76.0 2.2 %fusion.166 = (f32[128]{0:T(128)S(1)}, f32[128,256]{1,0:T(8,128)S(1)}) fusion(bf16[2,2048,256]{2,1,0:T(8,128)(2,1)} %param.26, bf16[2,256,2048]{2,1,0:T(8,128)(2,1)} %param.25, f32[128,256]{1,0:T(8,128)S(1)} %get-tuple-element.60, f32[128]{0:T(128)S(1)} %add_sqrt_fusion.3, f32[128]{0:T(128)S(1)} %broadcast_multiply_fusion.3), kind=kOutput, calls=%fused_computation.310 | convolution fusion | flops 269188992 | bytes 2492928 | tf_op jit(solution)/shard_map/dot_general | solution.py:22
  78.5 2.0 %collective-permute-start.11 = (bf16[128,256]{1,0:T(8,128)(2,1)S(1)}, bf16[128,256]{1,0:T(8,128)(2,1)S(1)}, u32[]{:S(2)}, u32[]{:S(2)}) collective-permute-start(bf16[128,256]{1,0:T(8,128)(2,1)S(1)} %divide_convert_fusion), channel_id=1, source_target_pairs={{0,48},{16,32},{32,16},{48,0},{1,49},{17,33},{33,17},{49,1},{2,50}... | collective-permute-start | bytes 196616 | tf_op jit(solution)/shard_map/ppermute | solution.py:32
  80.5 1.0 collective-permute-start.10
  81.6 0.5 collective-permute-start.9
  82.2 1.0 collective-permute-done.11
  83.1 2.0 %collective-permute-done.10 = bf16[128,256]{1,0:T(8,128)(2,1)S(1)} collective-permute-done((bf16[128,256]{1,0:T(8,128)(2,1)S(1)}, bf16[128,256]{1,0:T(8,128)(2,1)S(1)}, u32[]{:S(2)}, u32[]{:S(2)}) %collective-permute-start.10) | collective-permute-done | bytes 65568 | tf_op jit(solution)/shard_map/ppermute | solution.py:32
  85.2 0.6 gather_fusion.1
  85.8 1.1 convolution_convert_fusion.6
  86.9 1.1 convolution_convert_fusion.5
  88.1 0.6 fusion.3
  88.6 0.6 convert_reduce_fusion.1
  89.2 0.6 fusion.11
  89.8 1.1 fusion.171
  91.1 1.2 %fusion.14 = f32[64,128]{1,0:T(8,128)S(1)} fusion(bf16[256,256]{1,0:T(8,128)(2,1)S(1)} %copy-done.3, f32[128,256]{0,1:T(8,128)S(1)} %get-tuple-element.66, bf16[64,256]{0,1:T(8,128)(2,1)} %collective-permute-done.12, bf16[64,256]{0,1:T(8,128)(2,1)S(1)} %bitcast.286, f32[128]{0:T(128)S(1)} %add_sqrt_fusion.1, f32[128]{0:T(128)S(1)} %broadcast_multiply_fusion.1, ...), kind=kOutput, calls=%fused_computation.49 | convolution fusion | flops 13074432 | bytes 394305 | tf_op jit(solution)/shard_map/dot_general | solution.py:206
  92.3 1.3 %collective-permute-start.13 = (f32[64,64]{1,0:T(8,128)S(1)}, f32[64,64]{1,0:T(8,128)S(1)}, u32[]{:S(2)}, u32[]{:S(2)}) collective-permute-start(f32[64,64]{1,0:T(8,128)S(1)} %get-tuple-element.24), channel_id=1, source_target_pairs={{0,1},{1,0},{2,3},{3,2},{4,5},{5,4},{6,7},{7,6},{8,9},{9,8},{10,11... | collective-permute-start | bytes 49160 | tf_op jit(solution)/shard_map/ppermute | solution.py:32
  93.9 1.3 %collective-permute-done.13 = f32[64,64]{1,0:T(8,128)S(1)} collective-permute-done((f32[64,64]{1,0:T(8,128)S(1)}, f32[64,64]{1,0:T(8,128)S(1)}, u32[]{:S(2)}, u32[]{:S(2)}) %collective-permute-start.13) | collective-permute-done | bytes 16416 | tf_op jit(solution)/shard_map/ppermute | solution.py:32
  95.2 8.6 %collective-permute-start.14 = (f32[2,64,64]{2,1,0:T(8,128)S(1)}, f32[2,64,64]{2,1,0:T(8,128)S(1)}, u32[]{:S(2)}, u32[]{:S(2)}) collective-permute-start(f32[2,64,64]{2,1,0:T(8,128)S(1)} %maximum_select_fusion.3), channel_id=1, source_target_pairs={{0,64},{64,0},{128,192},{192,128},{1,65},{65,1},{129,193},{193,129... | collective-permute-start | bytes 98312 | tf_op jit(solution)/shard_map/ppermute | solution.py:32
  103.8 2.6 %collective-permute-start.15 = (f32[2,64,64]{2,1,0:T(8,128)S(1)}, f32[2,64,64]{2,1,0:T(8,128)S(1)}, u32[]{:S(2)}, u32[]{:S(2)}) collective-permute-start(f32[2,64,64]{2,1,0:T(8,128)S(1)} %maximum_select_fusion.3), channel_id=1, source_target_pairs={{0,128},{64,192},{128,0},{192,64},{1,129},{65,193},{129,1},{193,65... | collective-permute-start | bytes 98312 | tf_op jit(solution)/shard_map/ppermute | solution.py:32
  106.4 0.6 collective-permute-start.16
  107.0 1.8 %collective-permute-done.15 = f32[2,64,64]{2,1,0:T(8,128)S(1)} collective-permute-done((f32[2,64,64]{2,1,0:T(8,128)S(1)}, f32[2,64,64]{2,1,0:T(8,128)S(1)}, u32[]{:S(2)}, u32[]{:S(2)}) %collective-permute-start.15) | collective-permute-done | bytes 32800 | tf_op jit(solution)/shard_map/ppermute | solution.py:32
  108.8 3.2 %collective-permute-done.16 = f32[2,64,64]{2,1,0:T(8,128)S(1)} collective-permute-done((f32[2,64,64]{2,1,0:T(8,128)S(1)}, f32[2,64,64]{2,1,0:T(8,128)S(1)}, u32[]{:S(2)}, u32[]{:S(2)}) %collective-permute-start.16) | collective-permute-done | bytes 32800 | tf_op jit(solution)/shard_map/ppermute | solution.py:32
  112.0 0.6 reverse_select_fusion
  (103 shorter events, 5.5 us)
Async XLA Ops:
  0.0 14.5 %copy-start = (bf16[1280,256]{1,0:T(8,128)(2,1)S(1)}, bf16[1280,256]{1,0:T(8,128)(2,1)}, u32[]{:S(2)}) copy-start(bf16[1280,256]{1,0:T(8,128)(2,1)} %param.22) | copy-start | bytes 1966084
  0.0 17.6 %copy-start.2 = (f32[2,128]{1,0:T(2,128)S(1)}, f32[2,128]{1,0:T(2,128)}, u32[]{:S(2)}) copy-start(f32[2,128]{1,0:T(2,128)} %param.21) | copy-start | bytes 3076
  1.7 17.8 %copy-start.5 = (s32[8]{0:T(128)S(1)}, s32[8]{0:T(128)}, u32[]{:S(2)}) copy-start(s32[8]{0:T(128)} %param.17) | copy-start | bytes 100
  1.8 19.4 %copy-start.4 = (f32[8,256]{1,0:T(8,128)S(1)}, f32[8,256]{1,0:T(8,128)}, u32[]{:S(2)}) copy-start(f32[8,256]{1,0:T(8,128)} %param.20) | copy-start | bytes 24580
  1.8 26.8 %all-to-all-start = ((bf16[16,64,256]{2,1,0:T(8,128)(2,1)}), bf16[16,64,256]{2,1,0:T(8,128)(2,1)S(1)}, u32[]{:S(2)}, u32[]{:S(2)}) async-start(bf16[16,64,256]{2,1,0:T(8,128)(2,1)} %bitcast.12), calls=%async_computation | async-start | bytes 1048576 | tf_op jit(solution)/shard_map/all_to_all | solution.py:160
  16.1 74.9 %collective-permute-start.12 = (bf16[64,256]{0,1:T(8,128)(2,1)S(1)}, bf16[64,256]{0,1:T(8,128)(2,1)}, u32[]{:S(2)}, u32[]{:S(2)}) collective-permute-start(bf16[64,256]{0,1:T(8,128)(2,1)S(1)} %bitcast.285), channel_id=1, source_target_pairs={{0,1},{1,0},{2,3},{3,2},{4,5},{5,4},{6,7},{7,6},{8,9},{9,8},{10,11... | collective-permute-start | bytes 98312 | tf_op jit(solution)/shard_map/ppermute | solution.py:32
  33.3 8.4 %collective-permute-start.2 = (bf16[160,128]{1,0:T(8,128)(2,1)S(1)}, bf16[160,128]{1,0:T(8,128)(2,1)S(1)}, u32[]{:S(2)}, u32[]{:S(2)}) collective-permute-start(bf16[160,128]{1,0:T(8,128)(2,1)S(1)} %constant_dynamic-update-slice_fusion), channel_id=1, source_target_pairs={{0,6},{2,4},{4,2},{6,0},{1,7},{3,5},{5,3},{7,1},{8,14},{10,12},{12... | collective-permute-start | bytes 122888 | tf_op jit(solution)/shard_map/ppermute | solution.py:32
  35.3 6.9 %collective-permute-start.1 = (bf16[160,128]{1,0:T(8,128)(2,1)S(1)}, bf16[160,128]{1,0:T(8,128)(2,1)S(1)}, u32[]{:S(2)}, u32[]{:S(2)}) collective-permute-start(bf16[160,128]{1,0:T(8,128)(2,1)S(1)} %constant_dynamic-update-slice_fusion), channel_id=1, source_target_pairs={{0,4},{2,6},{4,0},{6,2},{1,5},{3,7},{5,1},{7,3},{8,12},{10,14},{12... | collective-permute-start | bytes 122888 | tf_op jit(solution)/shard_map/ppermute | solution.py:32
  40.3 2.9 %collective-permute-start = (bf16[160,128]{1,0:T(8,128)(2,1)S(1)}, bf16[160,128]{1,0:T(8,128)(2,1)S(1)}, u32[]{:S(2)}, u32[]{:S(2)}) collective-permute-start(bf16[160,128]{1,0:T(8,128)(2,1)S(1)} %constant_dynamic-update-slice_fusion), channel_id=1, source_target_pairs={{0,2},{2,0},{4,6},{6,4},{1,3},{3,1},{5,7},{7,5},{8,10},{10,8},{12,... | collective-permute-start | bytes 122888 | tf_op jit(solution)/shard_map/ppermute | solution.py:32
  47.2 4.5 %collective-permute-start.5 = (bf16[128,256]{1,0:T(8,128)(2,1)S(1)}, bf16[128,256]{1,0:T(8,128)(2,1)S(1)}, u32[]{:S(2)}, u32[]{:S(2)}) collective-permute-start(bf16[128,256]{1,0:T(8,128)(2,1)S(1)} %fusion.157), channel_id=1, source_target_pairs={{0,48},{16,32},{32,16},{48,0},{1,49},{17,33},{33,17},{49,1},{2,50}... | collective-permute-start | bytes 196616 | tf_op jit(solution)/shard_map/ppermute | solution.py:32
  47.9 4.6 %collective-permute-start.4 = (bf16[128,256]{1,0:T(8,128)(2,1)S(1)}, bf16[128,256]{1,0:T(8,128)(2,1)S(1)}, u32[]{:S(2)}, u32[]{:S(2)}) collective-permute-start(bf16[128,256]{1,0:T(8,128)(2,1)S(1)} %fusion.157), channel_id=1, source_target_pairs={{0,32},{16,48},{32,0},{48,16},{1,33},{17,49},{33,1},{49,17},{2,34}... | collective-permute-start | bytes 196616 | tf_op jit(solution)/shard_map/ppermute | solution.py:32
  48.9 4.0 %collective-permute-start.3 = (bf16[128,256]{1,0:T(8,128)(2,1)S(1)}, bf16[128,256]{1,0:T(8,128)(2,1)S(1)}, u32[]{:S(2)}, u32[]{:S(2)}) collective-permute-start(bf16[128,256]{1,0:T(8,128)(2,1)S(1)} %fusion.157), channel_id=1, source_target_pairs={{0,16},{16,0},{32,48},{48,32},{1,17},{17,1},{33,49},{49,33},{2,18}... | collective-permute-start | bytes 196616 | tf_op jit(solution)/shard_map/ppermute | solution.py:32
  63.1 1.2 %copy-start.1 = (bf16[2,2,128,256]{3,2,1,0:T(8,128)(2,1)S(1)}, bf16[2,2,128,256]{3,2,1,0:T(8,128)(2,1)}, u32[]{:S(2)}) copy-start(bf16[2,2,128,256]{3,2,1,0:T(8,128)(2,1)} %param.24) | copy-start | bytes 786436
  69.7 4.7 %collective-permute-start.8 = (bf16[160,128]{1,0:T(8,128)(2,1)S(1)}, bf16[160,128]{1,0:T(8,128)(2,1)S(1)}, u32[]{:S(2)}, u32[]{:S(2)}) collective-permute-start(bf16[160,128]{1,0:T(8,128)(2,1)S(1)} %constant_dynamic-update-slice_fusion.5), channel_id=1, source_target_pairs={{0,6},{2,4},{4,2},{6,0},{1,7},{3,5},{5,3},{7,1},{8,14},{10,12},{12... | collective-permute-start | bytes 122888 | tf_op jit(solution)/shard_map/ppermute | solution.py:32
  71.5 3.9 %collective-permute-start.7 = (bf16[160,128]{1,0:T(8,128)(2,1)S(1)}, bf16[160,128]{1,0:T(8,128)(2,1)S(1)}, u32[]{:S(2)}, u32[]{:S(2)}) collective-permute-start(bf16[160,128]{1,0:T(8,128)(2,1)S(1)} %constant_dynamic-update-slice_fusion.5), channel_id=1, source_target_pairs={{0,4},{2,6},{4,0},{6,2},{1,5},{3,7},{5,1},{7,3},{8,12},{10,14},{12... | collective-permute-start | bytes 122888 | tf_op jit(solution)/shard_map/ppermute | solution.py:32
  71.7 3.6 %collective-permute-start.6 = (bf16[160,128]{1,0:T(8,128)(2,1)S(1)}, bf16[160,128]{1,0:T(8,128)(2,1)S(1)}, u32[]{:S(2)}, u32[]{:S(2)}) collective-permute-start(bf16[160,128]{1,0:T(8,128)(2,1)S(1)} %constant_dynamic-update-slice_fusion.5), channel_id=1, source_target_pairs={{0,2},{2,0},{4,6},{6,4},{1,3},{3,1},{5,7},{7,5},{8,10},{10,8},{12,... | collective-permute-start | bytes 122888 | tf_op jit(solution)/shard_map/ppermute | solution.py:32
  78.5 4.6 %collective-permute-start.11 = (bf16[128,256]{1,0:T(8,128)(2,1)S(1)}, bf16[128,256]{1,0:T(8,128)(2,1)S(1)}, u32[]{:S(2)}, u32[]{:S(2)}) collective-permute-start(bf16[128,256]{1,0:T(8,128)(2,1)S(1)} %divide_convert_fusion), channel_id=1, source_target_pairs={{0,48},{16,32},{32,16},{48,0},{1,49},{17,33},{33,17},{49,1},{2,50}... | collective-permute-start | bytes 196616 | tf_op jit(solution)/shard_map/ppermute | solution.py:32
  80.5 4.6 %collective-permute-start.10 = (bf16[128,256]{1,0:T(8,128)(2,1)S(1)}, bf16[128,256]{1,0:T(8,128)(2,1)S(1)}, u32[]{:S(2)}, u32[]{:S(2)}) collective-permute-start(bf16[128,256]{1,0:T(8,128)(2,1)S(1)} %divide_convert_fusion), channel_id=1, source_target_pairs={{0,32},{16,48},{32,0},{48,16},{1,33},{17,49},{33,1},{49,17},{2,34}... | collective-permute-start | bytes 196616 | tf_op jit(solution)/shard_map/ppermute | solution.py:32
  81.6 3.6 %collective-permute-start.9 = (bf16[128,256]{1,0:T(8,128)(2,1)S(1)}, bf16[128,256]{1,0:T(8,128)(2,1)S(1)}, u32[]{:S(2)}, u32[]{:S(2)}) collective-permute-start(bf16[128,256]{1,0:T(8,128)(2,1)S(1)} %divide_convert_fusion), channel_id=1, source_target_pairs={{0,16},{16,0},{32,48},{48,32},{1,17},{17,1},{33,49},{49,33},{2,18}... | collective-permute-start | bytes 196616 | tf_op jit(solution)/shard_map/ppermute | solution.py:32
  86.9 4.1 %copy-start.3 = (bf16[256,256]{1,0:T(8,128)(2,1)S(1)}, bf16[256,256]{1,0:T(8,128)(2,1)}, u32[]{:S(2)}) copy-start(bf16[256,256]{1,0:T(8,128)(2,1)} %param.27) | copy-start | bytes 393220
  88.0 5.6 %copy-start.6 = (s32[8]{0:T(128)S(1)}, s32[8]{0:T(128)}, u32[]{:S(2)}) copy-start(s32[8]{0:T(128)} %param.19) | copy-start | bytes 100
  92.3 2.8 %collective-permute-start.13 = (f32[64,64]{1,0:T(8,128)S(1)}, f32[64,64]{1,0:T(8,128)S(1)}, u32[]{:S(2)}, u32[]{:S(2)}) collective-permute-start(f32[64,64]{1,0:T(8,128)S(1)} %get-tuple-element.24), channel_id=1, source_target_pairs={{0,1},{1,0},{2,3},{3,2},{4,5},{5,4},{6,7},{7,6},{8,9},{9,8},{10,11... | collective-permute-start | bytes 49160 | tf_op jit(solution)/shard_map/ppermute | solution.py:32
  95.2 11.8 %collective-permute-start.14 = (f32[2,64,64]{2,1,0:T(8,128)S(1)}, f32[2,64,64]{2,1,0:T(8,128)S(1)}, u32[]{:S(2)}, u32[]{:S(2)}) collective-permute-start(f32[2,64,64]{2,1,0:T(8,128)S(1)} %maximum_select_fusion.3), channel_id=1, source_target_pairs={{0,64},{64,0},{128,192},{192,128},{1,65},{65,1},{129,193},{193,129... | collective-permute-start | bytes 98312 | tf_op jit(solution)/shard_map/ppermute | solution.py:32
  103.8 5.1 %collective-permute-start.15 = (f32[2,64,64]{2,1,0:T(8,128)S(1)}, f32[2,64,64]{2,1,0:T(8,128)S(1)}, u32[]{:S(2)}, u32[]{:S(2)}) collective-permute-start(f32[2,64,64]{2,1,0:T(8,128)S(1)} %maximum_select_fusion.3), channel_id=1, source_target_pairs={{0,128},{64,192},{128,0},{192,64},{1,129},{65,193},{129,1},{193,65... | collective-permute-start | bytes 98312 | tf_op jit(solution)/shard_map/ppermute | solution.py:32
  106.4 5.6 %collective-permute-start.16 = (f32[2,64,64]{2,1,0:T(8,128)S(1)}, f32[2,64,64]{2,1,0:T(8,128)S(1)}, u32[]{:S(2)}, u32[]{:S(2)}) collective-permute-start(f32[2,64,64]{2,1,0:T(8,128)S(1)} %maximum_select_fusion.3), channel_id=1, source_target_pairs={{0,192},{64,128},{128,64},{192,0},{1,193},{65,129},{129,65},{193,1... | collective-permute-start | bytes 98312 | tf_op jit(solution)/shard_map/ppermute | solution.py:32

commit v2 on v1

v2 whole, which is shorter than its diff:
```python
import math

import jax
import jax.numpy as jnp
from jax import lax
from jax.experimental import pallas as pl
from jax.experimental.pallas import tpu as pltpu
from jax.sharding import Mesh
from jax.sharding import PartitionSpec as P

HEADS = 8
GRID = 64
IMG_PIX = 1024
TOKS_P = 8
NORM_EPS = 0.01
SPLIT = ("section", "x", "zh", "zl", "y")
IMG = ("x", "zh", "zl", "y")
bf16 = jnp.bfloat16
f32 = jnp.float32


def bdot(left, right):
    return jnp.dot(left, right, preferred_element_type=f32)


def norm_rows(values):
    center = values - jnp.mean(values, axis=-1, keepdims=True)
    spread = jnp.mean(center * center, axis=-1, keepdims=True)
    return center / jnp.sqrt(spread + NORM_EPS)


def swapped(x, axis, distance):
    return lax.ppermute(x, axis, [(i, i ^ distance) for i in range(lax.axis_size(axis))])


def fourier(coord_x, coord_y, pe_basis):
    phase = (2.0 * coord_x - 1.0)[..., None] * pe_basis[0] + (2.0 * coord_y - 1.0)[
        ..., None
    ] * pe_basis[1]
    phase = 2.0 * math.pi * phase
    return jnp.concatenate([jnp.sin(phase), jnp.cos(phase)], axis=-1)


def grid_tables(grid_rows, pe_basis):
    column = (jnp.arange(GRID, dtype=f32) + 0.5) / GRID
    row = (grid_rows.astype(f32) + 0.5) / GRID
    a = 2.0 * math.pi * (2.0 * column - 1.0)[:, None] * pe_basis[0]
    b = 2.0 * math.pi * (2.0 * row - 1.0)[:, None] * pe_basis[1]
    return (
        jnp.concatenate([jnp.sin(a), jnp.cos(a)], axis=-1),
        jnp.concatenate([jnp.sin(b), jnp.cos(b)], axis=-1),
    )


def start_tokens(box_rows, token_table, pe_basis):
    coords = (box_rows.astype(f32) + 0.5) / IMG_PIX
    corner_one = fourier(coords[:, 0], coords[:, 1], pe_basis)
    corner_two = fourier(coords[:, 2], coords[:, 3], pe_basis)
    slots = jnp.arange(TOKS_P)[None, :, None]
    tokens = token_table[None] + jnp.where(slots == TOKS_P - 2, corner_one[:, None, :], 0.0)
    tokens = tokens + jnp.where(slots == TOKS_P - 1, corner_two[:, None, :], 0.0)
    return tokens.reshape(-1, token_table.shape[-1])


def dot_at(left, right, l_dim, r_dim):
    return lax.dot_general(
        left, right, (((l_dim,), (r_dim,)), ((), ())), preferred_element_type=f32
    )


def code_rows(cols_ref, rows_ref, row, count):
    half = cols_ref.shape[1] // 2
    sa, ca = cols_ref[:, :half], cols_ref[:, half:]
    out = []
    for k in range(count):
        sb = rows_ref[row + k][:, :half]
        cb = rows_ref[row + k][:, half:]
        out.append(jnp.concatenate([sa * cb + ca * sb, ca * cb - sa * sb], axis=1))
    return jnp.concatenate(out, axis=0)


def one_head(values, head, size):
    lane = lax.broadcasted_iota(jnp.int32, values.shape, 1)
    return jnp.where(lane // size == head, values, jnp.zeros_like(values))


def pieces(v):
    hi = v.astype(bf16)
    rest = v - hi.astype(f32)
    mid = rest.astype(bf16)
    low = (rest - mid.astype(f32)).astype(bf16)
    return [hi, mid, low]


def partial_attend(query, key_ref, image_ref, w_k, w_v, out_ref):
    width = w_k.shape[1]
    size = width // HEADS
    query = (query * size ** (-0.5)).astype(bf16)
    keys = bdot(key_ref[...], w_k).astype(bf16)
    values = dot_at(w_v, image_ref[...], 0, 1).astype(bf16)
    ones = jnp.ones((size, values.shape[1]), bf16)
    totals, tops = [], []
    for head in range(HEADS):
        scores = dot_at(keys, one_head(query, head, size), 1, 1)
        top = jnp.max(scores, axis=0, keepdims=True)
        weights = jnp.exp(scores - top).astype(bf16)
        own = values[head * size : (head + 1) * size]
        both = bdot(jnp.concatenate([own, ones], axis=0), weights)
        out_ref[head * size : (head + 1) * size, :] = both[:size].astype(bf16)
        totals.append(both[size : size + 1])
        tops.append(top)
    total = jnp.concatenate(totals, axis=0)
    tops = pieces(jnp.concatenate(tops, axis=0))
    tail = jnp.concatenate([total] + [t.astype(f32) for t in tops], axis=0)
    out_ref[width:, :] = tail.astype(bf16)


def first_kernel(tok_ref, image_ref, cols_ref, rows_ref, w_ref, out_ref, key_ref):
    step = 4
    for k in range(0, rows_ref.shape[0], step):
        at = slice(k * GRID, (k + step) * GRID)
        code = code_rows(cols_ref, rows_ref, k, step)
        key_ref[at, :] = (image_ref[at, :].astype(f32) + code).astype(bf16)
    query = bdot(tok_ref[...].astype(bf16), w_ref[0]).astype(bf16)
    partial_attend(query.astype(f32), key_ref, image_ref, w_ref[1], w_ref[2], out_ref)


def token_kernel(p0, p1, p2, p3, tok_ref, w_ref, up_ref, down_ref, out_ref, short_ref):
    refs = (p0, p1, p2, p3)
    width = w_ref.shape[0]
    size = width // HEADS
    tails = [r[width:, :].astype(f32) for r in refs]
    tops = [t[HEADS : 2 * HEADS] + (t[2 * HEADS : 3 * HEADS] + t[3 * HEADS :]) for t in tails]
    peak = jnp.maximum(jnp.maximum(tops[0], tops[1]), jnp.maximum(tops[2], tops[3]))
    shares = [jnp.exp(t - peak) for t in tops]
    total = sum(t[:HEADS] * s for t, s in zip(tails, shares))
    heads = []
    for head in range(HEADS):
        at = slice(head * size, (head + 1) * size)
        row = slice(head, head + 1)
        summed = sum(r[at, :].astype(f32) * s[row] for r, s in zip(refs, shares))
        heads.append(summed / total[row])
    first = jnp.concatenate(heads, axis=0).astype(bf16)
    two = norm_rows(tok_ref[...] + dot_at(first, w_ref[...], 0, 0))
    hidden = jnp.maximum(bdot(two.astype(bf16), up_ref[...]), 0.0).astype(bf16)
    three = norm_rows(two + bdot(hidden, down_ref[...]))
    out_ref[...] = three
    short_ref[...] = three.astype(bf16)


def token_sides(tok_refs, scal_ref, w_k, w_v, k_ref, v_ref):
    width = w_k.shape[1]
    toks = tok_refs[0].shape[0]
    for k, ref in enumerate(tok_refs):
        at = slice(k * toks, (k + 1) * toks)
        tok = ref[...]
        first = (scal_ref[0] ^ k) * toks
        k_ref[at, :width] = bdot(tok, w_k).astype(bf16)
        row = lax.broadcasted_iota(jnp.int32, (toks, width), 0) + first
        lane = lax.broadcasted_iota(jnp.int32, (toks, width), 1)
        dead = (row >= scal_ref[1] * TOKS_P) & (lane == 0)
        k_ref[at, width:] = jnp.where(dead, -1e30, 0.0).astype(bf16)
        v_ref[:, at] = dot_at(w_v, tok, 0, 1).astype(bf16)


def image_attend(key, w_q, w_o, k_ref, v_ref):
    width = w_q.shape[1]
    size = width // HEADS
    query = bdot(key, w_q).astype(bf16).astype(f32) * size ** (-0.5)
    lane = lax.broadcasted_iota(jnp.int32, query.shape, 1)
    query = jnp.concatenate([query, jnp.where(lane == 0, 1.0, 0.0)], axis=1).astype(bf16)
    ones = jnp.ones((size, v_ref.shape[1]), bf16)
    heads = []
    for head in range(HEADS):
        keys = jnp.concatenate(
            [one_head(k_ref[:, :width], head, size), k_ref[:, width:]], axis=1
        )
        scores = dot_at(keys, query, 1, 1)
        top = jnp.max(scores, axis=0, keepdims=True)
        weights = jnp.exp(scores - top).astype(bf16)
        own = v_ref[head * size : (head + 1) * size, :]
        both = bdot(jnp.concatenate([own, ones], axis=0), weights)
        heads.append(both[:size] / both[size : size + 1])
    second = jnp.concatenate(heads, axis=0).astype(bf16)
    return dot_at(second, w_o, 0, 0)


def middle_kernel(
    scal_ref, t0, t1, t2, t3, image_ref, cols_ref, rows_ref, w_ref, next_ref, o_ref,
    out_ref, own_ref, own_key_ref, k_ref, v_ref, key_ref, new_ref, full_ref,
):
    token_sides((t0, t1, t2, t3), scal_ref, w_ref[4], w_ref[5], k_ref, v_ref)
    step = 4
    chunk = step * GRID

    def one(c, carry):
        at = pl.ds(pl.multiple_of(c * chunk, chunk), chunk)
        code = code_rows(cols_ref, rows_ref, c * step, step)
        image = image_ref[at, :].astype(f32)
        key = (image + code).astype(bf16)
        image = norm_rows(image + image_attend(key, w_ref[3], o_ref[...], k_ref, v_ref))
        full_ref[at, :] = image
        new_ref[at, :] = image.astype(bf16)
        key_ref[at, :] = (image + code).astype(bf16)
        return carry

    lax.fori_loop(0, image_ref.shape[0] // chunk, one, 0)
    own = pl.ds(pl.multiple_of(scal_ref[2], own_ref.shape[0]), own_ref.shape[0])
    own_ref[...] = full_ref[own, :]
    own_key_ref[...] = key_ref[own, :]
    query = bdot(t0[...], next_ref[0]).astype(bf16)
    partial_attend(query.astype(f32), key_ref, new_ref, next_ref[1], next_ref[2], out_ref)


def last_kernel(
    scal_ref, t0, t1, t2, t3, image_ref, key_ref, w_ref, o_ref, hq_ref, hyper_ref,
    out_ref, k_ref, v_ref, logit_ref,
):
    refs = (t0, t1, t2, t3)
    token_sides(refs, scal_ref, w_ref[4], w_ref[5], k_ref, v_ref)
    image = image_ref[...]
    image = norm_rows(
        image + image_attend(key_ref[...], w_ref[3], o_ref[...], k_ref, v_ref)
    )
    feats = (image + hq_ref[...].astype(f32)).astype(bf16)
    scale = image.shape[1] ** (-0.5)
    toks = t0.shape[0]
    prompts = toks // TOKS_P
    for k, ref in enumerate(refs):
        hyper = bdot(ref[...], hyper_ref[...]).astype(bf16)
        logit_ref[...] = dot_at(hyper, feats, 1, 1) * scale
        rows = logit_ref[pl.ds(TOKS_P - 3, prompts, stride=TOKS_P), :]
        first = (scal_ref[0] ^ k) * prompts
        live = lax.broadcasted_iota(jnp.int32, rows.shape, 0) + first < scal_ref[1]
        out_ref[pl.ds(pl.multiple_of(first, prompts), prompts), :] = jnp.where(live, rows, 0.0)


def call(kernel, name, outs, scratch=(), scalars=0):
    vmem = pl.BlockSpec(memory_space=pltpu.VMEM)

    def run(*args):
        specs = [pl.BlockSpec(memory_space=pltpu.SMEM)] * scalars
        specs += [vmem] * (len(args) - scalars)
        return pl.pallas_call(
            kernel,
            out_shape=[jax.ShapeDtypeStruct(s, d) for s, d in outs],
            in_specs=specs,
            out_specs=[vmem] * len(outs),
            scratch_shapes=[pltpu.VMEM(s, d) for s, d in scratch],
            compiler_params=pltpu.CompilerParams(vmem_limit_bytes=48 * 2**20),
            name=name,
        )(*args)

    return run


def shards(
    early_feats,
    final_embed,
    prompt_counts,
    box_pixels,
    pair_table,
    token_table,
    pe_basis,
    w_early,
    attend_in,
    attend_out,
    mlp_up,
    mlp_down,
    w_hyper,
):
    images, pos_dev, width = final_embed.shape
    prompts = box_pixels.shape[1]
    n_x, n_zh, n_zl, n_y = (lax.axis_size(a) for a in IMG)
    section = lax.axis_index("section")
    my_x, my_zh, my_zl, my_y = (lax.axis_index(a) for a in IMG)
    mine = section * images + my_y

    sent = jnp.broadcast_to(final_embed[None], (n_x * n_zh,) + final_embed.shape)
    sent = sent.reshape(n_x * n_zh * n_y, pos_dev, width)
    held = lax.all_to_all(sent, ("x", "zh", "y"), 0, 0, tiled=True)
    image = held.reshape(-1, width)

    hq = jax.nn.gelu(bdot(early_feats, w_early), approximate=False).astype(bf16)
    hq_keep = lax.dynamic_index_in_dim(hq, my_y, 0, keepdims=False)
    hq_send = lax.dynamic_index_in_dim(hq, 1 - my_y, 0, keepdims=False)
    hq_got = swapped(hq_send, "y", 1)
    hq_here = jnp.where(
        my_y == 0,
        jnp.concatenate([hq_keep, hq_got], axis=0),
        jnp.concatenate([hq_got, hq_keep], axis=0),
    )

    ids = jnp.arange(n_x * n_zh * n_y, dtype=jnp.int32)
    grid_rows = (ids // 4) * (n_zh * n_zl * n_y) + (ids // 2 % 2) * (n_zl * n_y)
    grid_rows = grid_rows + my_zl * n_y + ids % 2
    cols, rows = grid_tables(grid_rows, pe_basis)
    rows = rows[:, None]
    count = prompt_counts[mine]
    boxes = lax.dynamic_index_in_dim(box_pixels, mine, 0, keepdims=False)
    own_prompts = prompts // n_x
    boxes = lax.dynamic_slice_in_dim(boxes, my_x * own_prompts, own_prompts, 0)
    tok = start_tokens(boxes, token_table, pe_basis)
    own_pos = n_y * pos_dev
    scal = jnp.stack([my_x, count, (my_x * n_zh + my_zh) * own_pos]).astype(jnp.int32)
    n_tok, n_pos, att = tok.shape[0], image.shape[0], attend_in.shape[-1]
    packed = ((att + 4 * HEADS, n_tok), bf16)
    sides = [((n_x * n_tok, 2 * att), bf16), ((att, n_x * n_tok), bf16)]

    def token_step(part, tok, layer):
        parts = [part] + [swapped(part, "zl", d) for d in range(1, n_zl)]
        outs = [(tok.shape, f32), (tok.shape, bf16)]
        tok, short = call(token_kernel, "tokens", outs)(
            *parts, tok, attend_out[layer, 0], mlp_up[layer], mlp_down[layer]
        )
        return tok, [short] + [swapped(short, "x", d) for d in range(1, n_x)]

    (part,) = call(first_kernel, "first", [packed], [((n_pos, width), bf16)])(
        tok, image, cols, rows, attend_in[0]
    )
    tok, toks = token_step(part, tok, 0)
    part, own, own_key = call(
        middle_kernel,
        "middle",
        [packed, ((own_pos, width), f32), ((own_pos, width), bf16)],
        sides + [((n_pos, width), d) for d in (bf16, bf16, f32)],
        1,
    )(scal, *toks, image, cols, rows, attend_in[0], attend_in[1], attend_out[0, 1])
    tok, toks = token_step(part, tok, 1)
    (masks,) = call(
        last_kernel,
        "last",
        [((prompts, own_pos), f32)],
        sides + [((n_tok, own_pos), f32)],
        1,
    )(scal, *toks, own, own_key, attend_in[1], attend_out[1, 1], hq_here, w_hyper)

    halves = [masks[:, :pos_dev], masks[:, pos_dev:]]
    keep = jnp.where(my_y == 0, halves[0], halves[1])
    give = jnp.where(my_y == 0, halves[1], halves[0])
    got = swapped(give, "y", 1)
    both = jnp.where(my_y == 0, jnp.stack([keep, got]), jnp.stack([got, keep]))
    every = jnp.stack(
        [both] + [swapped(both, "section", d) for d in range(1, lax.axis_size("section"))]
    )
    table = lax.dynamic_slice_in_dim(pair_table, section * images, images, 0)
    chosen = lax.dynamic_index_in_dim(every, (table[0] // images) ^ section, 0, keepdims=False)
    swap = (table[0] % images) == 1
    return jnp.where(swap, chosen[::-1], chosen)


def solution(mesh):
    n_sec, n_img = mesh.devices.shape
    fine = Mesh(mesh.devices.reshape(n_sec, 4, 2, 4, 2), SPLIT)
    placed = (P("section", IMG, None),) * 2 + (P(),) * 11
    return jax.shard_map(
        shards, mesh=fine, in_specs=placed, out_specs=P("section", None, IMG), check_vma=False
    )
```

time: 114 us -> 126 us (1.11)
  Pallas kernels: 0 us -> 34.1 us
  matrix products: 31.7 us -> 1.15 us
  local copies, waits for them, and re-layouts: 4.89 us -> 21.5 us
  other arithmetic: 11.3 us -> 3.53 us
  starting transfers between devices: 44.8 us -> 46.7 us
  waiting for transfers between devices: 19.1 us -> 17.6 us
    pallas_call x0 -> x5, Pallas kernels: none -> 34.1 us  [run(): pl.pallas_call(kernel, out_shape=[jax.ShapeDtypeStruct(s, d) for s, d in...]
    dot_general x19 -> x1, matrix products: 21.9 us -> 1.15 us  [bdot(): return jnp.dot(left, right, preferred_element_type=f32)]
    unnamed x18 -> x60, local copies, waits for them, and re-layouts: 0.06 us -> 11.3 us
    dot_general x9 -> x0, matrix products: 9.79 us -> none  [the longest x2 3.67 us: image_step(): jnp.einsum('qhd,khd->hqk', query.reshape(-1, HEADS, size), keys.reshape(-...]
    reduce_sum x14 -> x0, other arithmetic: 7.18 us -> none  [the longest x2 4.79 us: image_step(): total = jnp.sum(weights.astype(f32), axis=-1).T]
    squeeze x0 -> x5, local copies, waits for them, and re-layouts: none -> 5.47 us  [the longest x1 1.61 us: shards(): attend_out[1, 1]]
    ppermute x17, starting transfers between devices: 32 us -> 34.2 us  [swapped(): lax.ppermute(x, axis, [(i, i ^ distance) for i in range(lax.axis_size(axi...]
    ppermute x17, waiting for transfers between devices: 12.8 us -> 11.5 us  [swapped(): lax.ppermute(x, axis, [(i, i ^ distance) for i in range(lax.axis_size(axi...]
  transfers between devices with their start and end apart: 18 -> 18, of which waited for: 12 -> 10; matrix products, arithmetic and copies ran while one was open for 39% -> 10% of each run, Pallas kernels for 0% -> 2%
where the time goes in v2:
time: 126 us; the launch traced here: 125 us
  starting transfers between devices  46.7 us (37%)
  Pallas kernels  34.1 us (27%)
  local copies, waits for them, and re-layouts  21.5 us (17%)
  waiting for transfers between devices  17.6 us (14%)
  other arithmetic  3.53 us (3%)
    ppermute x17, starting transfers between devices, swapped(): lax.ppermute(x, axis, [(i, i ^ distance) for i in range(lax.axis_size(axi...  34.2 us
    pallas_call x5, Pallas kernels, run(): pl.pallas_call(kernel, out_shape=[jax.ShapeDtypeStruct(s, d) for s, d in...  34.1 us
    all_to_all x1, starting transfers between devices, shards(): held = lax.all_to_all(sent, ('x', 'zh', 'y'), 0, 0, tiled=True)  12.6 us
    ppermute x17, waiting for transfers between devices, swapped(): lax.ppermute(x, axis, [(i, i ^ distance) for i in range(lax.axis_size(axi...  11.5 us
    unnamed x60, local copies, waits for them, and re-layouts  11.3 us
    all_to_all x1, waiting for transfers between devices, shards(): held = lax.all_to_all(sent, ('x', 'zh', 'y'), 0, 0, tiled=True)  6.18 us
  transfers between devices with their start and end apart: 18, of which 10 were waited for; matrix products, arithmetic and copies ran while one was open for 10% of the time, Pallas kernels for 2%

profile of v2, /device:TPU:1, one launch (start us, length us, event | category | flops | bytes accessed | tf_op | source)
XLA Modules:
  0.0 125.1 jit_solution(6953557709382635178)
XLA Ops:
  0.0 1.8 %broadcast_in_dim.73 = bf16[8,2,64,256]{3,2,1,0:T(8,128)(2,1)} broadcast(bf16[2,64,256]{2,1,0:T(8,128)(2,1)} %param.14), dimensions={1,2,3} | broadcast | bytes 589824 | tf_op jit(solution)/shard_map/broadcast_in_dim | solution.py:279
  1.8 12.6 %all-to-all-start = ((bf16[16,64,256]{2,1,0:T(8,128)(2,1)}), bf16[16,64,256]{2,1,0:T(8,128)(2,1)S(1)}, u32[]{:S(2)}, u32[]{:S(2)}) async-start(bf16[16,64,256]{2,1,0:T(8,128)(2,1)} %bitcast.13), calls=%async_computation | async-start | bytes 1048576 | tf_op jit(solution)/shard_map/all_to_all | solution.py:281
  14.5 0.8 slice_bitcast_fusion.11
  15.2 0.8 multiply_bitcast_fusion
  16.0 0.1 broadcast_in_dim.69
  16.1 0.1 broadcast_in_dim.63
  16.2 0.2 multiply_sine_fusion
  16.4 0.2 multiply_sine_fusion.1
  16.6 0.9 slice_bitcast_fusion.4
  17.6 1.2 fusion.4
  18.8 0.1 fusion.5.tok_ref
  18.9 0.3 copy-done.23
  19.2 1.2 slice_bitcast_fusion.1
  20.4 0.8 copy-done.24
  21.2 1.1 slice_bitcast_fusion
  22.3 6.2 %all-to-all-done = bf16[16,64,256]{2,1,0:T(8,128)(2,1)S(1)} async-done(((bf16[16,64,256]{2,1,0:T(8,128)(2,1)}), bf16[16,64,256]{2,1,0:T(8,128)(2,1)S(1)}, u32[]{:S(2)}, u32[]{:S(2)}) %all-to-all-start) | async-done | bytes 524320 | tf_op jit(solution)/shard_map/all_to_all | solution.py:281
  28.5 1.0 copy-done.5
  29.5 4.1 %first.1.p0 = bf16[160,128]{1,0:T(8,128)(2,1)} custom-call(f32[128,256]{1,0:T(8,128)S(1)} %fusion.5.tok_ref, bf16[1024,256]{1,0:T(8,128)(2,1)S(1)} %bitcast.73, f32[64,256]{1,0:T(8,128)S(1)} %pad_maximum_fusion.cols_ref, f32[16,1,256]{2,1,0:T(1,128)S(1)} %broadcast_in_dim.74.rows_ref, bf16[6,256,128]{2,1,0:T(8,128)(2,1)S(1)} %copy-done.5), custom_call_target="tpu_custom_call" | custom-call | tf_op jit(solution)/shard_map/first/pallas_call | solution.py:244
  33.6 5.7 %collective-permute-start = (bf16[160,128]{1,0:T(8,128)(2,1)}, bf16[160,128]{1,0:T(8,128)(2,1)}, u32[]{:S(2)}, u32[]{:S(2)}) collective-permute-start(bf16[160,128]{1,0:T(8,128)(2,1)} %first.1.p0), channel_id=1, source_target_pairs={{0,2},{2,0},{4,6},{6,4},{1,3},{3,1},{5,7},{7,5},{8,10},{10,8},{12,... | collective-permute-start | bytes 122888 | tf_op jit(solution)/shard_map/ppermute | solution.py:33
  39.3 0.5 collective-permute-start.1
  39.8 1.6 %collective-permute-start.2 = (bf16[160,128]{1,0:T(8,128)(2,1)}, bf16[160,128]{1,0:T(8,128)(2,1)}, u32[]{:S(2)}, u32[]{:S(2)}) collective-permute-start(bf16[160,128]{1,0:T(8,128)(2,1)} %first.1.p0), channel_id=1, source_target_pairs={{0,6},{2,4},{4,2},{6,0},{1,7},{3,5},{5,3},{7,1},{8,14},{10,12},{12... | collective-permute-start | bytes 122888 | tf_op jit(solution)/shard_map/ppermute | solution.py:33
  41.4 1.6 %slice_bitcast_fusion.6 = (bf16[128,256]{1,0:T(8,128)(2,1)S(1)}, bf16[128,256]{1,0:T(8,128)(2,1)}, bf16[128,256]{1,0:T(8,128)(2,1)}, bf16[128,256]{1,0:T(8,128)(2,1)}) fusion(bf16[2,2,128,256]{3,2,1,0:T(8,128)(2,1)} %param.22), kind=kLoop, calls=%fused_computation.44 | loop fusion | bytes 524288 | tf_op jit(solution)/shard_map/squeeze | solution.py:336
  43.0 1.2 dynamic_slice.23
  44.2 1.0 collective-permute-done.2.p3
  45.2 1.2 copy-done.1
  46.4 1.2 copy-done.2
  47.6 0.8 copy-done.9
  48.5 2.0 %tokens.2 = (f32[128,256]{1,0:T(8,128)S(1)}, bf16[128,256]{1,0:T(8,128)(2,1)S(1)}) custom-call(bf16[160,128]{1,0:T(8,128)(2,1)} %first.1.p0, bf16[160,128]{1,0:T(8,128)(2,1)} %collective-permute-done.p1, bf16[160,128]{1,0:T(8,128)(2,1)} %collective-permute-done.1.p2, bf16[160,128]{1,0:T(8,128)(2,1)} %collective-permute-done.2.p3, ...), custom_call_target="tpu_custom_call" | custom-call | tf_op jit(solution)/shard_map/tokens/pallas_call | solution.py:244
  50.6 1.4 %collective-permute-start.4 = (bf16[128,256]{1,0:T(8,128)(2,1)S(1)}, bf16[128,256]{1,0:T(8,128)(2,1)S(1)}, u32[]{:S(2)}, u32[]{:S(2)}) collective-permute-start(bf16[128,256]{1,0:T(8,128)(2,1)S(1)} %get-tuple-element.11.t0), channel_id=1, source_target_pairs={{0,32},{16,48},{32,0},{48,16},{1,33},{17,49},{33,1},{49,17},{2,34}... | collective-permute-start | bytes 196616 | tf_op jit(solution)/shard_map/ppermute | solution.py:33
  52.0 2.5 %collective-permute-start.5 = (bf16[128,256]{1,0:T(8,128)(2,1)S(1)}, bf16[128,256]{1,0:T(8,128)(2,1)S(1)}, u32[]{:S(2)}, u32[]{:S(2)}) collective-permute-start(bf16[128,256]{1,0:T(8,128)(2,1)S(1)} %get-tuple-element.11.t0), channel_id=1, source_target_pairs={{0,48},{16,32},{32,16},{48,0},{1,49},{17,33},{33,17},{49,1},{2,50}... | collective-permute-start | bytes 196616 | tf_op jit(solution)/shard_map/ppermute | solution.py:33
  54.4 0.6 pad_add_fusion.scal_ref
  55.1 0.2 collective-permute-done.4.t2
  55.3 1.0 collective-permute-done.5.t3
  56.3 21.2 %middle.1 = (bf16[160,128]{1,0:T(8,128)(2,1)}, f32[128,256]{1,0:T(8,128)S(1)}, bf16[128,256]{1,0:T(8,128)(2,1)S(1)}) custom-call(s32[3]{0:T(128)S(1)} %pad_add_fusion.scal_ref, bf16[128,256]{1,0:T(8,128)(2,1)S(1)} %get-tuple-element.11.t0, bf16[128,256]{1,0:T(8,128)(2,1)S(1)} %collective-permute-done.3.t1, bf16[128,256]{1,0:T(8,128)(2,1)S(1)} %collective-permute-done.4.t2, ...), custom_call_target="tpu_custom_call" | custom-call | tf_op jit(solution)/shard_map/middle/pallas_call | solution.py:244
  77.5 0.6 copy-done.13
  78.1 0.6 copy-done.15
  78.8 1.9 %collective-permute-start.7 = (bf16[160,128]{1,0:T(8,128)(2,1)}, bf16[160,128]{1,0:T(8,128)(2,1)S(1)}, u32[]{:S(2)}, u32[]{:S(2)}) collective-permute-start(bf16[160,128]{1,0:T(8,128)(2,1)} %get-tuple-element.12.p0), channel_id=1, source_target_pairs={{0,4},{2,6},{4,0},{6,2},{1,5},{3,7},{5,1},{7,3},{8,12},{10,14},{12... | collective-permute-start | bytes 122888 | tf_op jit(solution)/shard_map/ppermute | solution.py:33
  80.6 1.7 %collective-permute-start.8 = (bf16[160,128]{1,0:T(8,128)(2,1)}, bf16[160,128]{1,0:T(8,128)(2,1)S(1)}, u32[]{:S(2)}, u32[]{:S(2)}) collective-permute-start(bf16[160,128]{1,0:T(8,128)(2,1)} %get-tuple-element.12.p0), channel_id=1, source_target_pairs={{0,6},{2,4},{4,2},{6,0},{1,7},{3,5},{5,3},{7,1},{8,14},{10,12},{12... | collective-permute-start | bytes 122888 | tf_op jit(solution)/shard_map/ppermute | solution.py:33
  82.3 0.6 dynamic-slice_bitcast_fusion.1
  83.0 1.6 %collective-permute-start.12 = (bf16[64,256]{1,0:T(8,128)(2,1)}, bf16[64,256]{1,0:T(8,128)(2,1)}, u32[]{:S(2)}, u32[]{:S(2)}) collective-permute-start(bf16[64,256]{1,0:T(8,128)(2,1)} %get-tuple-element.28), channel_id=1, source_target_pairs={{0,1},{1,0},{2,3},{3,2},{4,5},{5,4},{6,7},{7,6},{8,9},{9,8},{10,11... | collective-permute-start | bytes 98312 | tf_op jit(solution)/shard_map/ppermute | solution.py:33
  84.5 0.6 copy-done.17
  85.1 0.4 collective-permute-done.8.p3
  85.5 0.6 copy-done.19
  86.1 0.8 copy-done.7
  86.9 0.9 copy-done.11
  87.9 0.8 copy-done.18
  88.6 0.8 copy-done.20
  89.4 2.5 %tokens.3 = (f32[128,256]{1,0:T(8,128)}, bf16[128,256]{1,0:T(8,128)(2,1)S(1)}) custom-call(bf16[160,128]{1,0:T(8,128)(2,1)} %get-tuple-element.12.p0, bf16[160,128]{1,0:T(8,128)(2,1)S(1)} %collective-permute-done.6.p1, bf16[160,128]{1,0:T(8,128)(2,1)S(1)} %copy-done.18, bf16[160,128]{1,0:T(8,128)(2,1)S(1)} %copy-done.20, f32[128,256]{1,0:T(8,128)S(1)} %copy-done.11, ...), custom_call_target="tpu_custom_call" | custom-call | tf_op jit(solution)/shard_map/tokens/pallas_call | solution.py:244
  92.0 0.4 collective-permute-start.9
  92.3 3.3 %collective-permute-start.10 = (bf16[128,256]{1,0:T(8,128)(2,1)S(1)}, bf16[128,256]{1,0:T(8,128)(2,1)S(1)}, u32[]{:S(2)}, u32[]{:S(2)}) collective-permute-start(bf16[128,256]{1,0:T(8,128)(2,1)S(1)} %get-tuple-element.14.t0), channel_id=1, source_target_pairs={{0,32},{16,48},{32,0},{48,16},{1,33},{17,49},{33,1},{49,17},{2,34}... | collective-permute-start | bytes 196616 | tf_op jit(solution)/shard_map/ppermute | solution.py:33
  95.6 0.2 collective-permute-start.11
  95.8 0.9 maximum_select_fusion.hq_ref
  96.7 1.3 %collective-permute-done.10.t2 = bf16[128,256]{1,0:T(8,128)(2,1)S(1)} collective-permute-done((bf16[128,256]{1,0:T(8,128)(2,1)S(1)}, bf16[128,256]{1,0:T(8,128)(2,1)S(1)}, u32[]{:S(2)}, u32[]{:S(2)}) %collective-permute-start.10) | collective-permute-done | bytes 65568 | tf_op jit(solution)/shard_map/ppermute | solution.py:33
  98.0 2.0 %collective-permute-done.11.t3 = bf16[128,256]{1,0:T(8,128)(2,1)S(1)} collective-permute-done((bf16[128,256]{1,0:T(8,128)(2,1)S(1)}, bf16[128,256]{1,0:T(8,128)(2,1)S(1)}, u32[]{:S(2)}, u32[]{:S(2)}) %collective-permute-start.11) | collective-permute-done | bytes 65568 | tf_op jit(solution)/shard_map/ppermute | solution.py:33
  100.0 4.3 %last.1 = f32[64,128]{1,0:T(8,128)S(1)} custom-call(s32[3]{0:T(128)S(1)} %copy-done.22, bf16[128,256]{1,0:T(8,128)(2,1)S(1)} %get-tuple-element.14.t0, bf16[128,256]{1,0:T(8,128)(2,1)S(1)} %collective-permute-done.9.t1, bf16[128,256]{1,0:T(8,128)(2,1)S(1)} %collective-permute-done.10.t2, bf16[128,256]{1,0:T(8,128)(2,1)S(1)} %collective-permute-done.11.t3, ...), custom_call_target="tpu_custom_call" | custom-call | tf_op jit(solution)/shard_map/last/pallas_call | solution.py:244
  104.4 1.3 %collective-permute-start.13 = (f32[64,64]{1,0:T(8,128)S(1)}, f32[64,64]{1,0:T(8,128)S(1)}, u32[]{:S(2)}, u32[]{:S(2)}) collective-permute-start(f32[64,64]{1,0:T(8,128)S(1)} %get-tuple-element.31), channel_id=1, source_target_pairs={{0,1},{1,0},{2,3},{3,2},{4,5},{5,4},{6,7},{7,6},{8,9},{9,8},{10,11... | collective-permute-start | bytes 49160 | tf_op jit(solution)/shard_map/ppermute | solution.py:33
  105.7 0.7 dynamic_slice.22
  106.6 0.7 collective-permute-done.13
  107.3 8.9 %collective-permute-start.14 = (f32[2,64,64]{2,1,0:T(8,128)S(1)}, f32[2,64,64]{2,1,0:T(8,128)S(1)}, u32[]{:S(2)}, u32[]{:S(2)}) collective-permute-start(f32[2,64,64]{2,1,0:T(8,128)S(1)} %maximum_select_fusion.2), channel_id=1, source_target_pairs={{0,64},{64,0},{128,192},{192,128},{1,65},{65,1},{129,193},{193,129... | collective-permute-start | bytes 98312 | tf_op jit(solution)/shard_map/ppermute | solution.py:33
  116.2 2.6 %collective-permute-start.15 = (f32[2,64,64]{2,1,0:T(8,128)S(1)}, f32[2,64,64]{2,1,0:T(8,128)S(1)}, u32[]{:S(2)}, u32[]{:S(2)}) collective-permute-start(f32[2,64,64]{2,1,0:T(8,128)S(1)} %maximum_select_fusion.2), channel_id=1, source_target_pairs={{0,128},{64,192},{128,0},{192,64},{1,129},{65,193},{129,1},{193,65... | collective-permute-start | bytes 98312 | tf_op jit(solution)/shard_map/ppermute | solution.py:33
  118.8 0.6 collective-permute-start.16
  119.5 1.8 %collective-permute-done.15 = f32[2,64,64]{2,1,0:T(8,128)S(1)} collective-permute-done((f32[2,64,64]{2,1,0:T(8,128)S(1)}, f32[2,64,64]{2,1,0:T(8,128)S(1)}, u32[]{:S(2)}, u32[]{:S(2)}) %collective-permute-start.15) | collective-permute-done | bytes 32800 | tf_op jit(solution)/shard_map/ppermute | solution.py:33
  121.3 3.2 %collective-permute-done.16 = f32[2,64,64]{2,1,0:T(8,128)S(1)} collective-permute-done((f32[2,64,64]{2,1,0:T(8,128)S(1)}, f32[2,64,64]{2,1,0:T(8,128)S(1)}, u32[]{:S(2)}, u32[]{:S(2)}) %collective-permute-start.16) | collective-permute-done | bytes 32800 | tf_op jit(solution)/shard_map/ppermute | solution.py:33
  124.5 0.6 reverse_select_fusion
  (71 shorter events, 0.4 us)
Async XLA Ops:
  0.0 17.6 %copy-start = (bf16[1280,256]{1,0:T(8,128)(2,1)S(1)}, bf16[1280,256]{1,0:T(8,128)(2,1)}, u32[]{:S(2)}) copy-start(bf16[1280,256]{1,0:T(8,128)(2,1)} %param.20) | copy-start | bytes 1966084
  0.0 16.6 %copy-start.25 = (bf16[2,6,256,128]{3,2,1,0:T(8,128)(2,1)S(1)}, bf16[2,6,256,128]{3,2,1,0:T(8,128)(2,1)}, u32[]{:S(2)}) copy-start(bf16[2,6,256,128]{3,2,1,0:T(8,128)(2,1)} %param.21) | copy-start | bytes 2359300
  0.0 17.6 %copy-start.29 = (bf16[2,64,1280]{2,1,0:T(8,128)(2,1)S(1)}, bf16[2,64,1280]{2,1,0:T(8,128)(2,1)}, u32[]{:S(2)}) copy-start(bf16[2,64,1280]{2,1,0:T(8,128)(2,1)} %param.13) | copy-start | bytes 983044
  1.8 26.7 %all-to-all-start = ((bf16[16,64,256]{2,1,0:T(8,128)(2,1)}), bf16[16,64,256]{2,1,0:T(8,128)(2,1)S(1)}, u32[]{:S(2)}, u32[]{:S(2)}) async-start(bf16[16,64,256]{2,1,0:T(8,128)(2,1)} %bitcast.13), calls=%async_computation | async-start | bytes 1048576 | tf_op jit(solution)/shard_map/all_to_all | solution.py:281
  17.6 1.2 copy-start.28
  17.6 1.6 %copy-start.23 = (bf16[2,256,2048]{2,1,0:T(8,128)(2,1)S(1)}, bf16[2,256,2048]{2,1,0:T(8,128)(2,1)}, u32[]{:S(2)}) copy-start(bf16[2,256,2048]{2,1,0:T(8,128)(2,1)} %param.23) | copy-start | bytes 6291460
  19.2 2.0 %copy-start.24 = (bf16[2,2048,256]{2,1,0:T(8,128)(2,1)S(1)}, bf16[2,2048,256]{2,1,0:T(8,128)(2,1)}, u32[]{:S(2)}) copy-start(bf16[2,2048,256]{2,1,0:T(8,128)(2,1)} %param.24) | copy-start | bytes 6291460
  28.5 1.0 copy-start.5
  33.6 10.7 %collective-permute-start = (bf16[160,128]{1,0:T(8,128)(2,1)}, bf16[160,128]{1,0:T(8,128)(2,1)}, u32[]{:S(2)}, u32[]{:S(2)}) collective-permute-start(bf16[160,128]{1,0:T(8,128)(2,1)} %first.1.p0), channel_id=1, source_target_pairs={{0,2},{2,0},{4,6},{6,4},{1,3},{3,1},{5,7},{7,5},{8,10},{10,8},{12,... | collective-permute-start | bytes 122888 | tf_op jit(solution)/shard_map/ppermute | solution.py:33
  39.3 4.9 %collective-permute-start.1 = (bf16[160,128]{1,0:T(8,128)(2,1)}, bf16[160,128]{1,0:T(8,128)(2,1)}, u32[]{:S(2)}, u32[]{:S(2)}) collective-permute-start(bf16[160,128]{1,0:T(8,128)(2,1)} %first.1.p0), channel_id=1, source_target_pairs={{0,4},{2,6},{4,0},{6,2},{1,5},{3,7},{5,1},{7,3},{8,12},{10,14},{12... | collective-permute-start | bytes 122888 | tf_op jit(solution)/shard_map/ppermute | solution.py:33
  39.8 5.4 %collective-permute-start.2 = (bf16[160,128]{1,0:T(8,128)(2,1)}, bf16[160,128]{1,0:T(8,128)(2,1)}, u32[]{:S(2)}, u32[]{:S(2)}) collective-permute-start(bf16[160,128]{1,0:T(8,128)(2,1)} %first.1.p0), channel_id=1, source_target_pairs={{0,6},{2,4},{4,2},{6,0},{1,7},{3,5},{5,3},{7,1},{8,14},{10,12},{12... | collective-permute-start | bytes 122888 | tf_op jit(solution)/shard_map/ppermute | solution.py:33
  45.2 1.2 copy-start.1
  46.4 1.2 copy-start.2
  47.6 0.8 copy-start.9
  48.5 7.8 %copy-start.3 = (bf16[6,256,128]{2,1,0:T(8,128)(2,1)S(1)}, bf16[6,256,128]{2,1,0:T(8,128)(2,1)}, u32[]{:S(2)}) copy-start(bf16[6,256,128]{2,1,0:T(8,128)(2,1)} %get-tuple-element.21.next_ref.w_ref) | copy-start | bytes 1179652
  48.5 7.8 %copy-start.6 = (bf16[6,256,128]{2,1,0:T(8,128)(2,1)S(1)}, bf16[6,256,128]{2,1,0:T(8,128)(2,1)}, u32[]{:S(2)}) copy-start(bf16[6,256,128]{2,1,0:T(8,128)(2,1)} %get-tuple-element.22.w_ref) | copy-start | bytes 1179652
  48.5 7.8 %copy-start.8 = (bf16[128,256]{1,0:T(8,128)(2,1)S(1)}, bf16[128,256]{1,0:T(8,128)(2,1)}, u32[]{:S(2)}) copy-start(bf16[128,256]{1,0:T(8,128)(2,1)} %get-tuple-element.24.o_ref) | copy-start | bytes 196612
  48.5 33.8 %copy-start.27 = (bf16[2,64,256]{2,1,0:T(8,128)(2,1)S(1)}, bf16[2,64,256]{2,1,0:T(8,128)(2,1)}, u32[]{:S(2)}) copy-start(bf16[2,64,256]{2,1,0:T(8,128)(2,1)} %fusion.4) | copy-start | bytes 196612
  50.5 27.0 %copy-start.10 = (f32[128,256]{1,0:T(8,128)}, f32[128,256]{1,0:T(8,128)S(1)}, u32[]{:S(2)}) copy-start(f32[128,256]{1,0:T(8,128)S(1)} %get-tuple-element.13.tok_ref) | copy-start | bytes 393220
  50.5 4.6 %collective-permute-start.3 = (bf16[128,256]{1,0:T(8,128)(2,1)S(1)}, bf16[128,256]{1,0:T(8,128)(2,1)S(1)}, u32[]{:S(2)}, u32[]{:S(2)}) collective-permute-start(bf16[128,256]{1,0:T(8,128)(2,1)S(1)} %get-tuple-element.11.t0), channel_id=1, source_target_pairs={{0,16},{16,0},{32,48},{48,32},{1,17},{17,1},{33,49},{49,33},{2,18}... | collective-permute-start | bytes 196616 | tf_op jit(solution)/shard_map/ppermute | solution.py:33
  50.6 4.7 %collective-permute-start.4 = (bf16[128,256]{1,0:T(8,128)(2,1)S(1)}, bf16[128,256]{1,0:T(8,128)(2,1)S(1)}, u32[]{:S(2)}, u32[]{:S(2)}) collective-permute-start(bf16[128,256]{1,0:T(8,128)(2,1)S(1)} %get-tuple-element.11.t0), channel_id=1, source_target_pairs={{0,32},{16,48},{32,0},{48,16},{1,33},{17,49},{33,1},{49,17},{2,34}... | collective-permute-start | bytes 196616 | tf_op jit(solution)/shard_map/ppermute | solution.py:33
  52.0 4.3 %collective-permute-start.5 = (bf16[128,256]{1,0:T(8,128)(2,1)S(1)}, bf16[128,256]{1,0:T(8,128)(2,1)S(1)}, u32[]{:S(2)}, u32[]{:S(2)}) collective-permute-start(bf16[128,256]{1,0:T(8,128)(2,1)S(1)} %get-tuple-element.11.t0), channel_id=1, source_target_pairs={{0,48},{16,32},{32,16},{48,0},{1,49},{17,33},{33,17},{49,1},{2,50}... | collective-permute-start | bytes 196616 | tf_op jit(solution)/shard_map/ppermute | solution.py:33
  55.1 23.7 %copy-start.21 = (s32[3]{0:T(128)}, s32[3]{0:T(128)S(1)}, u32[]{:S(2)}) copy-start(s32[3]{0:T(128)S(1)} %pad_add_fusion.scal_ref) | copy-start | bytes 40
  56.3 43.7 %copy-start.12 = (bf16[256,256]{1,0:T(8,128)(2,1)S(1)}, bf16[256,256]{1,0:T(8,128)(2,1)}, u32[]{:S(2)}) copy-start(bf16[256,256]{1,0:T(8,128)(2,1)} %hyper_ref.1) | copy-start | bytes 393220
  77.5 0.6 copy-start.13
  78.1 0.6 copy-start.15
  78.8 21.2 %copy-start.4 = (bf16[6,256,128]{2,1,0:T(8,128)(2,1)S(1)}, bf16[6,256,128]{2,1,0:T(8,128)(2,1)}, u32[]{:S(2)}) copy-start(bf16[6,256,128]{2,1,0:T(8,128)(2,1)} %get-tuple-element.21.next_ref.w_ref) | copy-start | bytes 1179652
  78.8 5.7 %collective-permute-start.6 = (bf16[160,128]{1,0:T(8,128)(2,1)}, bf16[160,128]{1,0:T(8,128)(2,1)S(1)}, u32[]{:S(2)}, u32[]{:S(2)}) collective-permute-start(bf16[160,128]{1,0:T(8,128)(2,1)} %get-tuple-element.12.p0), channel_id=1, source_target_pairs={{0,2},{2,0},{4,6},{6,4},{1,3},{3,1},{5,7},{7,5},{8,10},{10,8},{12,... | collective-permute-start | bytes 122888 | tf_op jit(solution)/shard_map/ppermute | solution.py:33
  78.8 5.7 %collective-permute-start.7 = (bf16[160,128]{1,0:T(8,128)(2,1)}, bf16[160,128]{1,0:T(8,128)(2,1)S(1)}, u32[]{:S(2)}, u32[]{:S(2)}) collective-permute-start(bf16[160,128]{1,0:T(8,128)(2,1)} %get-tuple-element.12.p0), channel_id=1, source_target_pairs={{0,4},{2,6},{4,0},{6,2},{1,5},{3,7},{5,1},{7,3},{8,12},{10,14},{12... | collective-permute-start | bytes 122888 | tf_op jit(solution)/shard_map/ppermute | solution.py:33
  80.6 4.9 %collective-permute-start.8 = (bf16[160,128]{1,0:T(8,128)(2,1)}, bf16[160,128]{1,0:T(8,128)(2,1)S(1)}, u32[]{:S(2)}, u32[]{:S(2)}) collective-permute-start(bf16[160,128]{1,0:T(8,128)(2,1)} %get-tuple-element.12.p0), channel_id=1, source_target_pairs={{0,6},{2,4},{4,2},{6,0},{1,7},{3,5},{5,3},{7,1},{8,14},{10,12},{12... | collective-permute-start | bytes 122888 | tf_op jit(solution)/shard_map/ppermute | solution.py:33
  83.0 12.9 %collective-permute-start.12 = (bf16[64,256]{1,0:T(8,128)(2,1)}, bf16[64,256]{1,0:T(8,128)(2,1)}, u32[]{:S(2)}, u32[]{:S(2)}) collective-permute-start(bf16[64,256]{1,0:T(8,128)(2,1)} %get-tuple-element.28), channel_id=1, source_target_pairs={{0,1},{1,0},{2,3},{3,2},{4,5},{5,4},{6,7},{7,6},{8,9},{9,8},{10,11... | collective-permute-start | bytes 98312 | tf_op jit(solution)/shard_map/ppermute | solution.py:33
  84.5 0.6 copy-start.17
  85.5 0.6 copy-start.19
  86.1 0.8 copy-start.7
  86.9 0.9 copy-start.11
  87.9 0.8 copy-start.18
  88.6 0.8 copy-start.20
  89.4 6.4 %copy-start.26 = (bf16[64,256]{1,0:T(8,128)(2,1)S(1)}, bf16[64,256]{1,0:T(8,128)(2,1)}, u32[]{:S(2)}) copy-start(bf16[64,256]{1,0:T(8,128)(2,1)} %get-tuple-element.27) | copy-start | bytes 98308
  89.4 10.5 %copy-start.14 = (f32[128,256]{1,0:T(8,128)S(1)}, f32[128,256]{1,0:T(8,128)}, u32[]{:S(2)}) copy-start(f32[128,256]{1,0:T(8,128)} %copy-done.13) | copy-start | bytes 393220
  89.4 10.6 %copy-start.16 = (bf16[128,256]{1,0:T(8,128)(2,1)S(1)}, bf16[128,256]{1,0:T(8,128)(2,1)}, u32[]{:S(2)}) copy-start(bf16[128,256]{1,0:T(8,128)(2,1)} %copy-done.15) | copy-start | bytes 196612
  89.4 10.6 %copy-start.22 = (s32[3]{0:T(128)S(1)}, s32[3]{0:T(128)}, u32[]{:S(2)}) copy-start(s32[3]{0:T(128)} %copy-done.21) | copy-start | bytes 40
  92.0 4.7 %collective-permute-start.9 = (bf16[128,256]{1,0:T(8,128)(2,1)S(1)}, bf16[128,256]{1,0:T(8,128)(2,1)S(1)}, u32[]{:S(2)}, u32[]{:S(2)}) collective-permute-start(bf16[128,256]{1,0:T(8,128)(2,1)S(1)} %get-tuple-element.14.t0), channel_id=1, source_target_pairs={{0,16},{16,0},{32,48},{48,32},{1,17},{17,1},{33,49},{49,33},{2,18}... | collective-permute-start | bytes 196616 | tf_op jit(solution)/shard_map/ppermute | solution.py:33
  92.3 5.6 %collective-permute-start.10 = (bf16[128,256]{1,0:T(8,128)(2,1)S(1)}, bf16[128,256]{1,0:T(8,128)(2,1)S(1)}, u32[]{:S(2)}, u32[]{:S(2)}) collective-permute-start(bf16[128,256]{1,0:T(8,128)(2,1)S(1)} %get-tuple-element.14.t0), channel_id=1, source_target_pairs={{0,32},{16,48},{32,0},{48,16},{1,33},{17,49},{33,1},{49,17},{2,34}... | collective-permute-start | bytes 196616 | tf_op jit(solution)/shard_map/ppermute | solution.py:33
  95.6 4.3 %collective-permute-start.11 = (bf16[128,256]{1,0:T(8,128)(2,1)S(1)}, bf16[128,256]{1,0:T(8,128)(2,1)S(1)}, u32[]{:S(2)}, u32[]{:S(2)}) collective-permute-start(bf16[128,256]{1,0:T(8,128)(2,1)S(1)} %get-tuple-element.14.t0), channel_id=1, source_target_pairs={{0,48},{16,32},{32,16},{48,0},{1,49},{17,33},{33,17},{49,1},{2,50}... | collective-permute-start | bytes 196616 | tf_op jit(solution)/shard_map/ppermute | solution.py:33
  104.4 2.9 %collective-permute-start.13 = (f32[64,64]{1,0:T(8,128)S(1)}, f32[64,64]{1,0:T(8,128)S(1)}, u32[]{:S(2)}, u32[]{:S(2)}) collective-permute-start(f32[64,64]{1,0:T(8,128)S(1)} %get-tuple-element.31), channel_id=1, source_target_pairs={{0,1},{1,0},{2,3},{3,2},{4,5},{5,4},{6,7},{7,6},{8,9},{9,8},{10,11... | collective-permute-start | bytes 49160 | tf_op jit(solution)/shard_map/ppermute | solution.py:33
  107.3 12.2 %collective-permute-start.14 = (f32[2,64,64]{2,1,0:T(8,128)S(1)}, f32[2,64,64]{2,1,0:T(8,128)S(1)}, u32[]{:S(2)}, u32[]{:S(2)}) collective-permute-start(f32[2,64,64]{2,1,0:T(8,128)S(1)} %maximum_select_fusion.2), channel_id=1, source_target_pairs={{0,64},{64,0},{128,192},{192,128},{1,65},{65,1},{129,193},{193,129... | collective-permute-start | bytes 98312 | tf_op jit(solution)/shard_map/ppermute | solution.py:33
  116.2 5.1 %collective-permute-start.15 = (f32[2,64,64]{2,1,0:T(8,128)S(1)}, f32[2,64,64]{2,1,0:T(8,128)S(1)}, u32[]{:S(2)}, u32[]{:S(2)}) collective-permute-start(f32[2,64,64]{2,1,0:T(8,128)S(1)} %maximum_select_fusion.2), channel_id=1, source_target_pairs={{0,128},{64,192},{128,0},{192,64},{1,129},{65,193},{129,1},{193,65... | collective-permute-start | bytes 98312 | tf_op jit(solution)/shard_map/ppermute | solution.py:33
  118.8 5.6 %collective-permute-start.16 = (f32[2,64,64]{2,1,0:T(8,128)S(1)}, f32[2,64,64]{2,1,0:T(8,128)S(1)}, u32[]{:S(2)}, u32[]{:S(2)}) collective-permute-start(f32[2,64,64]{2,1,0:T(8,128)S(1)} %maximum_select_fusion.2), channel_id=1, source_target_pairs={{0,192},{64,128},{128,64},{192,0},{1,193},{65,129},{129,65},{193,1... | collective-permute-start | bytes 98312 | tf_op jit(solution)/shard_map/ppermute | solution.py:33

commit v3 on v2

--- a/solution.py
+++ b/solution.py
@@ -1,3 +1,4 @@
+import functools
 import math
 
 import jax
@@ -13,6 +14,7 @@
 IMG_PIX = 1024
 TOKS_P = 8
 NORM_EPS = 0.01
+A1_AHEAD = 4
 SPLIT = ("section", "x", "zh", "zl", "y")
 IMG = ("x", "zh", "zl", "y")
 bf16 = jnp.bfloat16
@@ -100,8 +102,11 @@
     values = dot_at(w_v, image_ref[...], 0, 1).astype(bf16)
     ones = jnp.ones((size, values.shape[1]), bf16)
     totals, tops = [], []
+    ahead = [dot_at(keys, one_head(query, head, size), 1, 1) for head in range(A1_AHEAD)]
     for head in range(HEADS):
-        scores = dot_at(keys, one_head(query, head, size), 1, 1)
+        if head + A1_AHEAD < HEADS:
+            ahead.append(dot_at(keys, one_head(query, head + A1_AHEAD, size), 1, 1))
+        scores = ahead.pop(0)
         top = jnp.max(scores, axis=0, keepdims=True)
         weights = jnp.exp(scores - top).astype(bf16)
         own = values[head * size : (head + 1) * size]
@@ -121,13 +126,15 @@
         at = slice(k * GRID, (k + step) * GRID)
         code = code_rows(cols_ref, rows_ref, k, step)
         key_ref[at, :] = (image_ref[at, :].astype(f32) + code).astype(bf16)
-    query = bdot(tok_ref[...].astype(bf16), w_ref[0]).astype(bf16)
-    partial_attend(query.astype(f32), key_ref, image_ref, w_ref[1], w_ref[2], out_ref)
-
-
-def token_kernel(p0, p1, p2, p3, tok_ref, w_ref, up_ref, down_ref, out_ref, short_ref):
+    query = bdot(tok_ref[...].astype(bf16), w_ref[0, 0]).astype(bf16)
+    partial_attend(query.astype(f32), key_ref, image_ref, w_ref[0, 1], w_ref[0, 2], out_ref)
+
+
+def token_kernel(
+    layer, p0, p1, p2, p3, tok_ref, w_ref, up_ref, down_ref, out_ref, short_ref
+):
     refs = (p0, p1, p2, p3)
-    width = w_ref.shape[0]
+    width = w_ref.shape[2]
     size = width // HEADS
     tails = [r[width:, :].astype(f32) for r in refs]
     tops = [t[HEADS : 2 * HEADS] + (t[2 * HEADS : 3 * HEADS] + t[3 * HEADS :]) for t in tails]
@@ -141,9 +148,9 @@
         summed = sum(r[at, :].astype(f32) * s[row] for r, s in zip(refs, shares))
         heads.append(summed / total[row])
     first = jnp.concatenate(heads, axis=0).astype(bf16)
-    two = norm_rows(tok_ref[...] + dot_at(first, w_ref[...], 0, 0))
-    hidden = jnp.maximum(bdot(two.astype(bf16), up_ref[...]), 0.0).astype(bf16)
-    three = norm_rows(two + bdot(hidden, down_ref[...]))
+    two = norm_rows(tok_ref[...] + dot_at(first, w_ref[layer, 0], 0, 0))
+    hidden = jnp.maximum(bdot(two.astype(bf16), up_ref[layer]), 0.0).astype(bf16)
+    three = norm_rows(two + bdot(hidden, down_ref[layer]))
     out_ref[...] = three
     short_ref[...] = three.astype(bf16)
 
@@ -163,19 +170,25 @@
         v_ref[:, at] = dot_at(w_v, tok, 0, 1).astype(bf16)
 
 
-def image_attend(key, w_q, w_o, k_ref, v_ref):
+def image_attend(key, w_q, w_o, k_ref, v_ref, early):
     width = w_q.shape[1]
     size = width // HEADS
     query = bdot(key, w_q).astype(bf16).astype(f32) * size ** (-0.5)
     lane = lax.broadcasted_iota(jnp.int32, query.shape, 1)
     query = jnp.concatenate([query, jnp.where(lane == 0, 1.0, 0.0)], axis=1).astype(bf16)
     ones = jnp.ones((size, v_ref.shape[1]), bf16)
+
+
+    def scores_of(head):
+        own = one_head(k_ref[:, :width], head, size)
+        return dot_at(jnp.concatenate([own, k_ref[:, width:]], axis=1), query, 1, 1)
+
     heads = []
+    ahead = [scores_of(head) for head in range(early)]
     for head in range(HEADS):
-        keys = jnp.concatenate(
-            [one_head(k_ref[:, :width], head, size), k_ref[:, width:]], axis=1
-        )
-        scores = dot_at(keys, query, 1, 1)
+        if head + early < HEADS:
+            ahead.append(scores_of(head + early))
+        scores = ahead.pop(0)
         top = jnp.max(scores, axis=0, keepdims=True)
         weights = jnp.exp(scores - top).astype(bf16)
         own = v_ref[head * size : (head + 1) * size, :]
@@ -186,30 +199,26 @@
 
 
 def middle_kernel(
-    scal_ref, t0, t1, t2, t3, image_ref, cols_ref, rows_ref, w_ref, next_ref, o_ref,
+    scal_ref, t0, t1, t2, t3, image_ref, cols_ref, rows_ref, w_ref, o_ref,
     out_ref, own_ref, own_key_ref, k_ref, v_ref, key_ref, new_ref, full_ref,
 ):
-    token_sides((t0, t1, t2, t3), scal_ref, w_ref[4], w_ref[5], k_ref, v_ref)
+    token_sides((t0, t1, t2, t3), scal_ref, w_ref[0, 4], w_ref[0, 5], k_ref, v_ref)
     step = 4
-    chunk = step * GRID
-
-    def one(c, carry):
-        at = pl.ds(pl.multiple_of(c * chunk, chunk), chunk)
-        code = code_rows(cols_ref, rows_ref, c * step, step)
-        image = image_ref[at, :].astype(f32)
-        key = (image + code).astype(bf16)
-        image = norm_rows(image + image_attend(key, w_ref[3], o_ref[...], k_ref, v_ref))
-        full_ref[at, :] = image
-        new_ref[at, :] = image.astype(bf16)
-        key_ref[at, :] = (image + code).astype(bf16)
-        return carry
-
-    lax.fori_loop(0, image_ref.shape[0] // chunk, one, 0)
+    for k in range(0, rows_ref.shape[0], step):
+        at = slice(k * GRID, (k + step) * GRID)
+        code = code_rows(cols_ref, rows_ref, k, step)
+        full_ref[at, :] = code
+        key_ref[at, :] = (image_ref[at, :].astype(f32) + code).astype(bf16)
+    change = image_attend(key_ref[...], w_ref[0, 3], o_ref[0, 1], k_ref, v_ref, 1)
+    image = norm_rows(image_ref[...].astype(f32) + change)
+    new_ref[...] = image.astype(bf16)
+    key_ref[...] = (image + full_ref[...]).astype(bf16)
+    full_ref[...] = image
     own = pl.ds(pl.multiple_of(scal_ref[2], own_ref.shape[0]), own_ref.shape[0])
     own_ref[...] = full_ref[own, :]
     own_key_ref[...] = key_ref[own, :]
-    query = bdot(t0[...], next_ref[0]).astype(bf16)
-    partial_attend(query.astype(f32), key_ref, new_ref, next_ref[1], next_ref[2], out_ref)
+    query = bdot(t0[...], w_ref[1, 0]).astype(bf16)
+    partial_attend(query.astype(f32), key_ref, new_ref, w_ref[1, 1], w_ref[1, 2], out_ref)
 
 
 def last_kernel(
@@ -217,11 +226,10 @@
     out_ref, k_ref, v_ref, logit_ref,
 ):
     refs = (t0, t1, t2, t3)
-    token_sides(refs, scal_ref, w_ref[4], w_ref[5], k_ref, v_ref)
+    token_sides(refs, scal_ref, w_ref[1, 4], w_ref[1, 5], k_ref, v_ref)
     image = image_ref[...]
-    image = norm_rows(
-        image + image_attend(key_ref[...], w_ref[3], o_ref[...], k_ref, v_ref)
-    )
+    change = image_attend(key_ref[...], w_ref[1, 3], o_ref[1, 1], k_ref, v_ref, 4)
+    image = norm_rows(image + change)
     feats = (image + hq_ref[...].astype(f32)).astype(bf16)
     scale = image.shape[1] ** (-0.5)
     toks = t0.shape[0]
@@ -247,7 +255,7 @@
             in_specs=specs,
             out_specs=[vmem] * len(outs),
             scratch_shapes=[pltpu.VMEM(s, d) for s, d in scratch],
-            compiler_params=pltpu.CompilerParams(vmem_limit_bytes=48 * 2**20),
+            compiler_params=pltpu.CompilerParams(vmem_limit_bytes=20 * 2**20),
             name=name,
         )(*args)
 
@@ -303,6 +311,11 @@
     tok = start_tokens(boxes, token_table, pe_basis)
     own_pos = n_y * pos_dev
     scal = jnp.stack([my_x, count, (my_x * n_zh + my_zh) * own_pos]).astype(jnp.int32)
+    table = lax.dynamic_index_in_dim(pair_table, section * images, 0, keepdims=False)
+    place = jnp.stack([(table // images) ^ section, table % images])
+    tok, cols, rows, scal, place, hq_here = lax.optimization_barrier(
+        (tok, cols, rows, scal, place, hq_here)
+    )
     n_tok, n_pos, att = tok.shape[0], image.shape[0], attend_in.shape[-1]
     packed = ((att + 4 * HEADS, n_tok), bf16)
     sides = [((n_x * n_tok, 2 * att), bf16), ((att, n_x * n_tok), bf16)]
@@ -310,13 +323,13 @@
     def token_step(part, tok, layer):
         parts = [part] + [swapped(part, "zl", d) for d in range(1, n_zl)]
         outs = [(tok.shape, f32), (tok.shape, bf16)]
-        tok, short = call(token_kernel, "tokens", outs)(
-            *parts, tok, attend_out[layer, 0], mlp_up[layer], mlp_down[layer]
+        tok, short = call(functools.partial(token_kernel, layer), "tokens", outs)(
+            *parts, tok, attend_out, mlp_up, mlp_down
         )
         return tok, [short] + [swapped(short, "x", d) for d in range(1, n_x)]
 
     (part,) = call(first_kernel, "first", [packed], [((n_pos, width), bf16)])(
-        tok, image, cols, rows, attend_in[0]
+        tok, image, cols, rows, attend_in
     )
     tok, toks = token_step(part, tok, 0)
     part, own, own_key = call(
@@ -325,7 +338,7 @@
         [packed, ((own_pos, width), f32), ((own_pos, width), bf16)],
         sides + [((n_pos, width), d) for d in (bf16, bf16, f32)],
         1,
-    )(scal, *toks, image, cols, rows, attend_in[0], attend_in[1], attend_out[0, 1])
+    )(scal, *toks, image, cols, rows, attend_in, attend_out)
     tok, toks = token_step(part, tok, 1)
     (masks,) = call(
         last_kernel,
@@ -333,7 +346,7 @@
         [((prompts, own_pos), f32)],
         sides + [((n_tok, own_pos), f32)],
         1,
-    )(scal, *toks, own, own_key, attend_in[1], attend_out[1, 1], hq_here, w_hyper)
+    )(scal, *toks, own, own_key, attend_in, attend_out, hq_here, w_hyper)
 
     halves = [masks[:, :pos_dev], masks[:, pos_dev:]]
     keep = jnp.where(my_y == 0, halves[0], halves[1])
@@ -343,9 +356,8 @@
     every = jnp.stack(
         [both] + [swapped(both, "section", d) for d in range(1, lax.axis_size("section"))]
     )
-    table = lax.dynamic_slice_in_dim(pair_table, section * images, images, 0)
-    chosen = lax.dynamic_index_in_dim(every, (table[0] // images) ^ section, 0, keepdims=False)
-    swap = (table[0] % images) == 1
+    chosen = lax.dynamic_index_in_dim(every, place[0], 0, keepdims=False)
+    swap = place[1] == 1
     return jnp.where(swap, chosen[::-1], chosen)
 
 

time: 126 us -> 106 us (0.84)
  Pallas kernels: 34.1 us -> 16.4 us
  local copies, waits for them, and re-layouts: 21.5 us -> 11.3 us
  other arithmetic: 3.53 us -> 12.2 us
  starting transfers between devices: 46.7 us -> 41 us
  between operations: 0.45 us -> 5.34 us
    pallas_call x5, Pallas kernels: 34.1 us -> 16.4 us  [run(): pl.pallas_call(kernel, out_shape=[jax.ShapeDtypeStruct(s, d) for s, d in...]
    all_to_all x1, waiting for transfers between devices: 6.18 us -> 0.01 us  [shards(): held = lax.all_to_all(sent, ('x', 'zh', 'y'), 0, 0, tiled=True)]
    ppermute x17, waiting for transfers between devices: 11.5 us -> 17.6 us  [swapped(): lax.ppermute(x, axis, [(i, i ^ distance) for i in range(lax.axis_size(axi...]
    unnamed x60 -> x36, local copies, waits for them, and re-layouts: 11.3 us -> 5.42 us
    squeeze x4 -> x0, local copies, waits for them, and re-layouts: 4.84 us -> none  [the longest x1 1.61 us: shards(): attend_out[1, 1]]
    ppermute x17, starting transfers between devices: 34.2 us -> 30.2 us  [swapped(): lax.ppermute(x, axis, [(i, i ^ distance) for i in range(lax.axis_size(axi...]
    all_to_all x1, starting transfers between devices: 12.6 us -> 10.8 us  [shards(): held = lax.all_to_all(sent, ('x', 'zh', 'y'), 0, 0, tiled=True)]
    add x1, other arithmetic: 0.1 us -> 1.45 us  [start_tokens(): tokens + jnp.where(slots == TOKS_P - 1, corner_two[:, None, :], 0.0)]
  transfers between devices with their start and end apart: 18 -> 18, of which waited for: 10 -> 10; matrix products, arithmetic and copies ran while one was open for 10% -> 16% of each run, Pallas kernels for 2% -> 0%
where the time goes in v3:
time: 106 us; the launch traced here: 105 us
  starting transfers between devices  41 us (39%)
  waiting for transfers between devices  17.6 us (17%)
  Pallas kernels  16.4 us (15%)
  other arithmetic  12.2 us (12%)
  local copies, waits for them, and re-layouts  11.3 us (11%)
  between operations  5.34 us (5%)
  matrix products  1.58 us (1%)
    ppermute x17, starting transfers between devices, swapped(): lax.ppermute(x, axis, [(i, i ^ distance) for i in range(lax.axis_size(axi...  30.2 us
    ppermute x17, waiting for transfers between devices, swapped(): lax.ppermute(x, axis, [(i, i ^ distance) for i in range(lax.axis_size(axi...  17.6 us
    pallas_call x5, Pallas kernels, run(): pl.pallas_call(kernel, out_shape=[jax.ShapeDtypeStruct(s, d) for s, d in...  16.4 us
    all_to_all x1, starting transfers between devices, shards(): held = lax.all_to_all(sent, ('x', 'zh', 'y'), 0, 0, tiled=True)  10.8 us
    unnamed x36, local copies, waits for them, and re-layouts  5.42 us
  transfers between devices with their start and end apart: 18, of which 10 were waited for; matrix products, arithmetic and copies ran while one was open for 16% of the time, Pallas kernels for 0%

profile of v3, /device:TPU:1, one launch (start us, length us, event | category | flops | bytes accessed | tf_op | source)
XLA Modules:
  0.0 105.3 jit_solution(3506123398874818566)
XLA Ops:
  0.0 1.1 %copy-done = bf16[1280,256]{1,0:T(8,128)(2,1)S(1)} copy-done((bf16[1280,256]{1,0:T(8,128)(2,1)S(1)}, bf16[1280,256]{1,0:T(8,128)(2,1)}, u32[]{:S(2)}) %copy-start) | copy-done | bytes 655384
  1.1 1.6 %fusion.4 = bf16[2,64,256]{2,1,0:T(8,128)(2,1)S(1)} fusion(bf16[2,64,1280]{2,1,0:T(8,128)(2,1)} %param.13, bf16[1280,256]{1,0:T(8,128)(2,1)S(1)} %copy-done), kind=kOutput, calls=%fused_computation.9 | convolution fusion | flops 86016000 | bytes 1048576 | tf_op jit(solution)/shard_map/dot_general | solution.py:25
  2.7 0.0 copy-start.1
  2.7 0.6 dynamic-slice_bitcast_fusion.1
  3.3 2.1 %collective-permute-start = (bf16[64,256]{1,0:T(8,128)(2,1)}, bf16[64,256]{1,0:T(8,128)(2,1)}, u32[]{:S(2)}, u32[]{:S(2)}) collective-permute-start(bf16[64,256]{1,0:T(8,128)(2,1)} %get-tuple-element.30), channel_id=1, source_target_pairs={{0,1},{1,0},{2,3},{3,2},{4,5},{5,4},{6,7},{7,6},{8,9},{9,8},{10,11... | collective-permute-start | bytes 98312 | tf_op jit(solution)/shard_map/ppermute | solution.py:35
  5.5 0.9 broadcast_in_dim.74
  6.3 10.8 %all-to-all-start = ((bf16[16,64,256]{2,1,0:T(8,128)(2,1)}), bf16[16,64,256]{2,1,0:T(8,128)(2,1)}, u32[]{:S(2)}, u32[]{:S(2)}) async-start(bf16[16,64,256]{2,1,0:T(8,128)(2,1)} %bitcast.56), calls=%async_computation | async-start | bytes 1048576 | tf_op jit(solution)/shard_map/all_to_all | solution.py:289
  17.2 0.6 dynamic_slice.25
  20.4 0.5 add_multiply_fusion.2
  20.9 0.8 multiply_bitcast_fusion
  21.7 0.6 add_bitcast_fusion.3
  22.3 0.6 fusion.31
  22.8 0.6 slice_bitcast_fusion.1
  23.4 0.7 broadcast_in_dim.63
  24.1 0.6 broadcast_in_dim.69
  24.7 0.6 dynamic_slice.24
  25.3 1.5 %multiply_sine_fusion.1 = (f32[16,128]{1,0:T(8,128)S(1)}, f32[16,128]{1,0:T(8,128)S(1)}, f32[16,128]{1,0:T(8,128)S(1)}, f32[16,128]{1,0:T(8,128)S(1)}, f32[16,128]{1,0:T(8,128)}, /*index=5*/f32[16,128]{1,0:T(8,128)}) fusion(f32[16]{0:T(128)} %fusion.31, f32[128]{0:T(128)} %get-tuple-element.49, f32[16]{0:T(128)} %get-tuple-element.37, ...), kind=kLoop, calls=%fused_computation.48 | loop fusion | flops 18432 | bytes 50496 | tf_op jit(solution)/shard_map/sin | solution.py:53
  26.7 0.6 pad_maximum_fusion.3
  27.3 0.6 pad_add_fusion.1
  27.9 0.7 pad_maximum_fusion.1
  28.7 0.9 multiply_sine_fusion
  29.5 0.6 pad_maximum_fusion.cols_ref
  30.2 1.4 %fusion.5.tok_ref = f32[128,256]{1,0:T(8,128)} fusion(f32[16,256]{1,0:T(8,128)S(1)} %get-tuple-element.57, f32[16,256]{1,0:T(8,128)S(1)} %get-tuple-element.56, f32[8,256]{1,0:T(8,128)} %param.18, pred[128]{0:T(512)(128)(4,1)} %broadcast_in_dim.69, pred[128]{0:T(512)(128)(4,1)} %broadcast_in_dim.63), kind=kLoop, calls=%fused_computation.11 | loop fusion | flops 131072 | bytes 172288 | tf_op jit(solution)/shard_map/add | solution.py:63
  31.6 1.2 %pad_add_fusion.scal_ref = s32[3]{0:T(128)} fusion(s32[1]{0:T(128)} %bitcast.11, s32[1]{0:T(128)} %dynamic_slice.24, s32[1]{0:T(128)} %bitcast.10), kind=kLoop, calls=%fused_computation.80 | loop fusion | flops 6 | bytes 24 | tf_op jit(solution)/shard_map/stack | solution.py:313
  32.8 0.7 broadcast_in_dim.73.rows_ref
  33.5 0.0 collective-permute-done
  33.5 1.5 %maximum_select_fusion.hq_ref = bf16[128,256]{1,0:T(8,128)(2,1)} fusion(bf16[64,256]{1,0:T(8,128)(2,1)} %collective-permute-done, bf16[64,256]{1,0:T(8,128)(2,1)} %get-tuple-element.29, pred[]{:T(512)S(6)} %eq.35), kind=kLoop, calls=%fused_computation.35 | loop fusion | flops 294912 | bytes 131073 | tf_op jit(solution)/shard_map/jit(_where)/select_n | solution.py:296
  35.0 0.9 copy-done.7
  35.9 0.8 copy-done.8
  36.8 2.8 %first.1.p0 = bf16[160,128]{1,0:T(8,128)(2,1)S(1)} custom-call(f32[128,256]{1,0:T(8,128)S(1)} %copy-done.7, bf16[1024,256]{1,0:T(8,128)(2,1)} %bitcast.20.image_ref, f32[64,256]{1,0:T(8,128)S(1)} %copy-done.8, f32[16,1,256]{2,1,0:T(1,128)S(1)} %broadcast_in_dim.73.rows_ref, bf16[2,6,256,128]{3,2,1,0:T(8,128)(2,1)S(1)} %copy-done.4), custom_call_target="tpu_custom_call" | custom-call | tf_op jit(solution)/shard_map/first/pallas_call | solution.py:252
  39.5 2.1 %collective-permute-start.1 = (bf16[160,128]{1,0:T(8,128)(2,1)S(1)}, bf16[160,128]{1,0:T(8,128)(2,1)S(1)}, u32[]{:S(2)}, u32[]{:S(2)}) collective-permute-start(bf16[160,128]{1,0:T(8,128)(2,1)S(1)} %first.1.p0), channel_id=1, source_target_pairs={{0,2},{2,0},{4,6},{6,4},{1,3},{3,1},{5,7},{7,5},{8,10},{10,8},{12,... | collective-permute-start | bytes 122888 | tf_op jit(solution)/shard_map/ppermute | solution.py:35
  41.6 0.6 collective-permute-start.2
  42.2 1.6 %collective-permute-start.3 = (bf16[160,128]{1,0:T(8,128)(2,1)S(1)}, bf16[160,128]{1,0:T(8,128)(2,1)S(1)}, u32[]{:S(2)}, u32[]{:S(2)}) collective-permute-start(bf16[160,128]{1,0:T(8,128)(2,1)S(1)} %first.1.p0), channel_id=1, source_target_pairs={{0,6},{2,4},{4,2},{6,0},{1,7},{3,5},{5,3},{7,1},{8,14},{10,12},{12... | collective-permute-start | bytes 122888 | tf_op jit(solution)/shard_map/ppermute | solution.py:35
  43.8 1.8 %collective-permute-done.2.p2 = bf16[160,128]{1,0:T(8,128)(2,1)S(1)} collective-permute-done((bf16[160,128]{1,0:T(8,128)(2,1)S(1)}, bf16[160,128]{1,0:T(8,128)(2,1)S(1)}, u32[]{:S(2)}, u32[]{:S(2)}) %collective-permute-start.2) | collective-permute-done | bytes 40992 | tf_op jit(solution)/shard_map/ppermute | solution.py:35
  45.6 1.7 %collective-permute-done.3.p3 = bf16[160,128]{1,0:T(8,128)(2,1)S(1)} collective-permute-done((bf16[160,128]{1,0:T(8,128)(2,1)S(1)}, bf16[160,128]{1,0:T(8,128)(2,1)S(1)}, u32[]{:S(2)}, u32[]{:S(2)}) %collective-permute-start.3) | collective-permute-done | bytes 40992 | tf_op jit(solution)/shard_map/ppermute | solution.py:35
  47.3 1.6 %copy-done.2 = bf16[2,2048,256]{2,1,0:T(8,128)(2,1)S(1)} copy-done((bf16[2,2048,256]{2,1,0:T(8,128)(2,1)S(1)}, bf16[2,2048,256]{2,1,0:T(8,128)(2,1)}, u32[]{:S(2)}) %copy-start.2) | copy-done | bytes 2097176
  48.9 0.9 copy-done.5
  49.8 1.1 %tokens.2 = (f32[128,256]{1,0:T(8,128)S(1)}, bf16[128,256]{1,0:T(8,128)(2,1)S(1)}) custom-call(bf16[160,128]{1,0:T(8,128)(2,1)S(1)} %first.1.p0, bf16[160,128]{1,0:T(8,128)(2,1)S(1)} %collective-permute-done.1.p1, bf16[160,128]{1,0:T(8,128)(2,1)S(1)} %collective-permute-done.2.p2, bf16[160,128]{1,0:T(8,128)(2,1)S(1)} %collective-permute-done.3.p3, ...), custom_call_target="tpu_custom_call" | custom-call | tf_op jit(solution)/shard_map/tokens/pallas_call | solution.py:252
  50.9 0.3 collective-permute-start.4
  51.2 2.4 %collective-permute-start.5 = (bf16[128,256]{1,0:T(8,128)(2,1)S(1)}, bf16[128,256]{1,0:T(8,128)(2,1)S(1)}, u32[]{:S(2)}, u32[]{:S(2)}) collective-permute-start(bf16[128,256]{1,0:T(8,128)(2,1)S(1)} %get-tuple-element.22.t0), channel_id=1, source_target_pairs={{0,32},{16,48},{32,0},{48,16},{1,33},{17,49},{33,1},{49,17},{2,34}... | collective-permute-start | bytes 196616 | tf_op jit(solution)/shard_map/ppermute | solution.py:35
  53.7 1.2 %collective-permute-start.6 = (bf16[128,256]{1,0:T(8,128)(2,1)S(1)}, bf16[128,256]{1,0:T(8,128)(2,1)S(1)}, u32[]{:S(2)}, u32[]{:S(2)}) collective-permute-start(bf16[128,256]{1,0:T(8,128)(2,1)S(1)} %get-tuple-element.22.t0), channel_id=1, source_target_pairs={{0,48},{16,32},{32,16},{48,0},{1,49},{17,33},{33,17},{49,1},{2,50}... | collective-permute-start | bytes 196616 | tf_op jit(solution)/shard_map/ppermute | solution.py:35
  54.9 1.2 %collective-permute-done.5.t2 = bf16[128,256]{1,0:T(8,128)(2,1)S(1)} collective-permute-done((bf16[128,256]{1,0:T(8,128)(2,1)S(1)}, bf16[128,256]{1,0:T(8,128)(2,1)S(1)}, u32[]{:S(2)}, u32[]{:S(2)}) %collective-permute-start.5) | collective-permute-done | bytes 65568 | tf_op jit(solution)/shard_map/ppermute | solution.py:35
  56.0 2.0 %collective-permute-done.6.t3 = bf16[128,256]{1,0:T(8,128)(2,1)S(1)} collective-permute-done((bf16[128,256]{1,0:T(8,128)(2,1)S(1)}, bf16[128,256]{1,0:T(8,128)(2,1)S(1)}, u32[]{:S(2)}, u32[]{:S(2)}) %collective-permute-start.6) | collective-permute-done | bytes 65568 | tf_op jit(solution)/shard_map/ppermute | solution.py:35
  58.0 8.2 %middle.1 = (bf16[160,128]{1,0:T(8,128)(2,1)S(1)}, f32[128,256]{1,0:T(8,128)S(1)}, bf16[128,256]{1,0:T(8,128)(2,1)S(1)}) custom-call(s32[3]{0:T(128)S(1)} %copy-done.12, bf16[128,256]{1,0:T(8,128)(2,1)S(1)} %get-tuple-element.22.t0, bf16[128,256]{1,0:T(8,128)(2,1)S(1)} %collective-permute-done.4.t1, bf16[128,256]{1,0:T(8,128)(2,1)S(1)} %collective-permute-done.5.t2, ...), custom_call_target="tpu_custom_call" | custom-call | tf_op jit(solution)/shard_map/middle/pallas_call | solution.py:252
  66.2 0.1 collective-permute-start.7
  66.3 1.9 %collective-permute-start.8 = (bf16[160,128]{1,0:T(8,128)(2,1)S(1)}, bf16[160,128]{1,0:T(8,128)(2,1)S(1)}, u32[]{:S(2)}, u32[]{:S(2)}) collective-permute-start(bf16[160,128]{1,0:T(8,128)(2,1)S(1)} %get-tuple-element.23.p0), channel_id=1, source_target_pairs={{0,4},{2,6},{4,0},{6,2},{1,5},{3,7},{5,1},{7,3},{8,12},{10,14},{12... | collective-permute-start | bytes 122888 | tf_op jit(solution)/shard_map/ppermute | solution.py:35
  68.2 1.6 %collective-permute-start.9 = (bf16[160,128]{1,0:T(8,128)(2,1)S(1)}, bf16[160,128]{1,0:T(8,128)(2,1)S(1)}, u32[]{:S(2)}, u32[]{:S(2)}) collective-permute-start(bf16[160,128]{1,0:T(8,128)(2,1)S(1)} %get-tuple-element.23.p0), channel_id=1, source_target_pairs={{0,6},{2,4},{4,2},{6,0},{1,7},{3,5},{5,3},{7,1},{8,14},{10,12},{12... | collective-permute-start | bytes 122888 | tf_op jit(solution)/shard_map/ppermute | solution.py:35
  69.9 0.3 collective-permute-done.8.p2
  70.2 2.7 %collective-permute-done.9.p3 = bf16[160,128]{1,0:T(8,128)(2,1)S(1)} collective-permute-done((bf16[160,128]{1,0:T(8,128)(2,1)S(1)}, bf16[160,128]{1,0:T(8,128)(2,1)S(1)}, u32[]{:S(2)}, u32[]{:S(2)}) %collective-permute-start.9) | collective-permute-done | bytes 40992 | tf_op jit(solution)/shard_map/ppermute | solution.py:35
  72.9 1.7 %tokens.3 = (f32[128,256]{1,0:T(8,128)}, bf16[128,256]{1,0:T(8,128)(2,1)S(1)}) custom-call(bf16[160,128]{1,0:T(8,128)(2,1)S(1)} %get-tuple-element.23.p0, bf16[160,128]{1,0:T(8,128)(2,1)S(1)} %collective-permute-done.7.p1, bf16[160,128]{1,0:T(8,128)(2,1)S(1)} %collective-permute-done.8.p2, bf16[160,128]{1,0:T(8,128)(2,1)S(1)} %collective-permute-done.9.p3, ...), custom_call_target="tpu_custom_call" | custom-call | tf_op jit(solution)/shard_map/tokens/pallas_call | solution.py:252
  74.6 2.4 %collective-permute-start.11 = (bf16[128,256]{1,0:T(8,128)(2,1)S(1)}, bf16[128,256]{1,0:T(8,128)(2,1)S(1)}, u32[]{:S(2)}, u32[]{:S(2)}) collective-permute-start(bf16[128,256]{1,0:T(8,128)(2,1)S(1)} %get-tuple-element.25.t0), channel_id=1, source_target_pairs={{0,32},{16,48},{32,0},{48,16},{1,33},{17,49},{33,1},{49,17},{2,34}... | collective-permute-start | bytes 196616 | tf_op jit(solution)/shard_map/ppermute | solution.py:35
  77.0 1.5 %collective-permute-start.12 = (bf16[128,256]{1,0:T(8,128)(2,1)S(1)}, bf16[128,256]{1,0:T(8,128)(2,1)S(1)}, u32[]{:S(2)}, u32[]{:S(2)}) collective-permute-start(bf16[128,256]{1,0:T(8,128)(2,1)S(1)} %get-tuple-element.25.t0), channel_id=1, source_target_pairs={{0,48},{16,32},{32,16},{48,0},{1,49},{17,33},{33,17},{49,1},{2,50}... | collective-permute-start | bytes 196616 | tf_op jit(solution)/shard_map/ppermute | solution.py:35
  78.5 0.9 collective-permute-done.11.t2
  79.3 2.0 %collective-permute-done.12.t3 = bf16[128,256]{1,0:T(8,128)(2,1)S(1)} collective-permute-done((bf16[128,256]{1,0:T(8,128)(2,1)S(1)}, bf16[128,256]{1,0:T(8,128)(2,1)S(1)}, u32[]{:S(2)}, u32[]{:S(2)}) %collective-permute-start.12) | collective-permute-done | bytes 65568 | tf_op jit(solution)/shard_map/ppermute | solution.py:35
  81.3 2.6 %last.1 = f32[64,128]{1,0:T(8,128)S(1)} custom-call(s32[3]{0:T(128)S(1)} %copy-done.12, bf16[128,256]{1,0:T(8,128)(2,1)S(1)} %get-tuple-element.25.t0, bf16[128,256]{1,0:T(8,128)(2,1)S(1)} %collective-permute-done.10.t1, bf16[128,256]{1,0:T(8,128)(2,1)S(1)} %collective-permute-done.11.t2, bf16[128,256]{1,0:T(8,128)(2,1)S(1)} %collective-permute-done.12.t3, ...), custom_call_target="tpu_custom_call" | custom-call | tf_op jit(solution)/shard_map/last/pallas_call | solution.py:252
  83.9 0.1 fusion.20
  84.0 1.3 %collective-permute-start.13 = (f32[64,64]{1,0:T(8,128)S(1)}, f32[64,64]{1,0:T(8,128)S(1)}, u32[]{:S(2)}, u32[]{:S(2)}) collective-permute-start(f32[64,64]{1,0:T(8,128)S(1)} %get-tuple-element.33), channel_id=1, source_target_pairs={{0,1},{1,0},{2,3},{3,2},{4,5},{5,4},{6,7},{7,6},{8,9},{9,8},{10,11... | collective-permute-start | bytes 49160 | tf_op jit(solution)/shard_map/ppermute | solution.py:35
  85.2 0.6 fusion.37
  88.4 7.9 %collective-permute-start.14 = (f32[2,64,64]{2,1,0:T(8,128)S(1)}, f32[2,64,64]{2,1,0:T(8,128)S(1)}, u32[]{:S(2)}, u32[]{:S(2)}) collective-permute-start(f32[2,64,64]{2,1,0:T(8,128)S(1)} %maximum_select_fusion.2), channel_id=1, source_target_pairs={{0,64},{64,0},{128,192},{192,128},{1,65},{65,1},{129,193},{193,129... | collective-permute-start | bytes 98312 | tf_op jit(solution)/shard_map/ppermute | solution.py:35
  96.3 2.8 %collective-permute-start.15 = (f32[2,64,64]{2,1,0:T(8,128)S(1)}, f32[2,64,64]{2,1,0:T(8,128)S(1)}, u32[]{:S(2)}, u32[]{:S(2)}) collective-permute-start(f32[2,64,64]{2,1,0:T(8,128)S(1)} %maximum_select_fusion.2), channel_id=1, source_target_pairs={{0,128},{64,192},{128,0},{192,64},{1,129},{65,193},{129,1},{193,65... | collective-permute-start | bytes 98312 | tf_op jit(solution)/shard_map/ppermute | solution.py:35
  99.1 0.4 collective-permute-start.16
  99.5 1.8 %collective-permute-done.15 = f32[2,64,64]{2,1,0:T(8,128)S(1)} collective-permute-done((f32[2,64,64]{2,1,0:T(8,128)S(1)}, f32[2,64,64]{2,1,0:T(8,128)S(1)}, u32[]{:S(2)}, u32[]{:S(2)}) %collective-permute-start.15) | collective-permute-done | bytes 32800 | tf_op jit(solution)/shard_map/ppermute | solution.py:35
  101.3 3.3 %collective-permute-done.16 = f32[2,64,64]{2,1,0:T(8,128)S(1)} collective-permute-done((f32[2,64,64]{2,1,0:T(8,128)S(1)}, f32[2,64,64]{2,1,0:T(8,128)S(1)}, u32[]{:S(2)}, u32[]{:S(2)}) %collective-permute-start.16) | collective-permute-done | bytes 32800 | tf_op jit(solution)/shard_map/ppermute | solution.py:35
  104.7 0.6 reverse_select_fusion
  (45 shorter events, 0.1 us)
Async XLA Ops:
  0.0 1.1 %copy-start = (bf16[1280,256]{1,0:T(8,128)(2,1)S(1)}, bf16[1280,256]{1,0:T(8,128)(2,1)}, u32[]{:S(2)}) copy-start(bf16[1280,256]{1,0:T(8,128)(2,1)} %param.20) | copy-start | bytes 1966084
  1.1 4.4 %copy-start.13 = (bf16[2,64,256]{2,1,0:T(8,128)(2,1)S(1)}, bf16[2,64,256]{2,1,0:T(8,128)(2,1)}, u32[]{:S(2)}) copy-start(bf16[2,64,256]{2,1,0:T(8,128)(2,1)} %param.14) | copy-start | bytes 196612
  1.1 16.1 %copy-start.16 = (s32[8]{0:T(128)S(1)}, s32[8]{0:T(128)}, u32[]{:S(2)}) copy-start(s32[8]{0:T(128)} %param.17) | copy-start | bytes 100
  1.1 21.7 %copy-start.15 = (f32[2,128]{1,0:T(2,128)S(1)}, f32[2,128]{1,0:T(2,128)}, u32[]{:S(2)}) copy-start(f32[2,128]{1,0:T(2,128)} %param.19) | copy-start | bytes 3076
  1.1 23.6 %copy-start.17 = (s32[8]{0:T(128)S(1)}, s32[8]{0:T(128)}, u32[]{:S(2)}) copy-start(s32[8]{0:T(128)} %param.15) | copy-start | bytes 100
  1.1 33.9 %copy-start.4 = (bf16[2,6,256,128]{3,2,1,0:T(8,128)(2,1)S(1)}, bf16[2,6,256,128]{3,2,1,0:T(8,128)(2,1)}, u32[]{:S(2)}) copy-start(bf16[2,6,256,128]{3,2,1,0:T(8,128)(2,1)} %w_ref.9) | copy-start | bytes 2359300
  2.7 44.6 %copy-start.1 = (bf16[2,256,2048]{2,1,0:T(8,128)(2,1)S(1)}, bf16[2,256,2048]{2,1,0:T(8,128)(2,1)}, u32[]{:S(2)}) copy-start(bf16[2,256,2048]{2,1,0:T(8,128)(2,1)} %up_ref.3) | copy-start | bytes 6291460
  3.3 30.2 %collective-permute-start = (bf16[64,256]{1,0:T(8,128)(2,1)}, bf16[64,256]{1,0:T(8,128)(2,1)}, u32[]{:S(2)}, u32[]{:S(2)}) collective-permute-start(bf16[64,256]{1,0:T(8,128)(2,1)} %get-tuple-element.30), channel_id=1, source_target_pairs={{0,1},{1,0},{2,3},{3,2},{4,5},{5,4},{6,7},{7,6},{8,9},{9,8},{10,11... | collective-permute-start | bytes 98312 | tf_op jit(solution)/shard_map/ppermute | solution.py:35
  6.3 28.7 %all-to-all-start = ((bf16[16,64,256]{2,1,0:T(8,128)(2,1)}), bf16[16,64,256]{2,1,0:T(8,128)(2,1)}, u32[]{:S(2)}, u32[]{:S(2)}) async-start(bf16[16,64,256]{2,1,0:T(8,128)(2,1)} %bitcast.56), calls=%async_computation | async-start | bytes 1048576 | tf_op jit(solution)/shard_map/all_to_all | solution.py:289
  35.0 0.9 copy-start.7
  35.9 0.8 copy-start.8
  36.8 21.2 %copy-start.6 = (bf16[2,2,128,256]{3,2,1,0:T(8,128)(2,1)S(1)}, bf16[2,2,128,256]{3,2,1,0:T(8,128)(2,1)}, u32[]{:S(2)}) copy-start(bf16[2,2,128,256]{3,2,1,0:T(8,128)(2,1)} %o_ref.3) | copy-start | bytes 786436
  36.8 21.2 %copy-start.9 = (f32[64,256]{1,0:T(8,128)S(1)}, f32[64,256]{1,0:T(8,128)}, u32[]{:S(2)}) copy-start(f32[64,256]{1,0:T(8,128)} %pad_maximum_fusion.cols_ref) | copy-start | bytes 196612
  36.8 21.2 %copy-start.12 = (s32[3]{0:T(128)S(1)}, s32[3]{0:T(128)}, u32[]{:S(2)}) copy-start(s32[3]{0:T(128)} %pad_add_fusion.scal_ref) | copy-start | bytes 40
  39.5 4.2 %collective-permute-start.1 = (bf16[160,128]{1,0:T(8,128)(2,1)S(1)}, bf16[160,128]{1,0:T(8,128)(2,1)S(1)}, u32[]{:S(2)}, u32[]{:S(2)}) collective-permute-start(bf16[160,128]{1,0:T(8,128)(2,1)S(1)} %first.1.p0), channel_id=1, source_target_pairs={{0,2},{2,0},{4,6},{6,4},{1,3},{3,1},{5,7},{7,5},{8,10},{10,8},{12,... | collective-permute-start | bytes 122888 | tf_op jit(solution)/shard_map/ppermute | solution.py:35
  41.6 4.0 %collective-permute-start.2 = (bf16[160,128]{1,0:T(8,128)(2,1)S(1)}, bf16[160,128]{1,0:T(8,128)(2,1)S(1)}, u32[]{:S(2)}, u32[]{:S(2)}) collective-permute-start(bf16[160,128]{1,0:T(8,128)(2,1)S(1)} %first.1.p0), channel_id=1, source_target_pairs={{0,4},{2,6},{4,0},{6,2},{1,5},{3,7},{5,1},{7,3},{8,12},{10,14},{12... | collective-permute-start | bytes 122888 | tf_op jit(solution)/shard_map/ppermute | solution.py:35
  42.2 5.1 %collective-permute-start.3 = (bf16[160,128]{1,0:T(8,128)(2,1)S(1)}, bf16[160,128]{1,0:T(8,128)(2,1)S(1)}, u32[]{:S(2)}, u32[]{:S(2)}) collective-permute-start(bf16[160,128]{1,0:T(8,128)(2,1)S(1)} %first.1.p0), channel_id=1, source_target_pairs={{0,6},{2,4},{4,2},{6,0},{1,7},{3,5},{5,3},{7,1},{8,14},{10,12},{12... | collective-permute-start | bytes 122888 | tf_op jit(solution)/shard_map/ppermute | solution.py:35
  47.3 1.6 %copy-start.2 = (bf16[2,2048,256]{2,1,0:T(8,128)(2,1)S(1)}, bf16[2,2048,256]{2,1,0:T(8,128)(2,1)}, u32[]{:S(2)}) copy-start(bf16[2,2048,256]{2,1,0:T(8,128)(2,1)} %down_ref.3) | copy-start | bytes 6291460
  48.9 0.9 copy-start.5
  49.8 23.0 %copy-start.3 = (bf16[2,2048,256]{2,1,0:T(8,128)(2,1)S(1)}, bf16[2,2048,256]{2,1,0:T(8,128)(2,1)}, u32[]{:S(2)}) copy-start(bf16[2,2048,256]{2,1,0:T(8,128)(2,1)} %down_ref.3) | copy-start | bytes 6291460
  50.9 4.0 %collective-permute-start.4 = (bf16[128,256]{1,0:T(8,128)(2,1)S(1)}, bf16[128,256]{1,0:T(8,128)(2,1)S(1)}, u32[]{:S(2)}, u32[]{:S(2)}) collective-permute-start(bf16[128,256]{1,0:T(8,128)(2,1)S(1)} %get-tuple-element.22.t0), channel_id=1, source_target_pairs={{0,16},{16,0},{32,48},{48,32},{1,17},{17,1},{33,49},{49,33},{2,18}... | collective-permute-start | bytes 196616 | tf_op jit(solution)/shard_map/ppermute | solution.py:35
  51.2 4.8 %collective-permute-start.5 = (bf16[128,256]{1,0:T(8,128)(2,1)S(1)}, bf16[128,256]{1,0:T(8,128)(2,1)S(1)}, u32[]{:S(2)}, u32[]{:S(2)}) collective-permute-start(bf16[128,256]{1,0:T(8,128)(2,1)S(1)} %get-tuple-element.22.t0), channel_id=1, source_target_pairs={{0,32},{16,48},{32,0},{48,16},{1,33},{17,49},{33,1},{49,17},{2,34}... | collective-permute-start | bytes 196616 | tf_op jit(solution)/shard_map/ppermute | solution.py:35
  53.7 4.3 %collective-permute-start.6 = (bf16[128,256]{1,0:T(8,128)(2,1)S(1)}, bf16[128,256]{1,0:T(8,128)(2,1)S(1)}, u32[]{:S(2)}, u32[]{:S(2)}) collective-permute-start(bf16[128,256]{1,0:T(8,128)(2,1)S(1)} %get-tuple-element.22.t0), channel_id=1, source_target_pairs={{0,48},{16,32},{32,16},{48,0},{1,49},{17,33},{33,17},{49,1},{2,50}... | collective-permute-start | bytes 196616 | tf_op jit(solution)/shard_map/ppermute | solution.py:35
  66.2 3.6 %collective-permute-start.7 = (bf16[160,128]{1,0:T(8,128)(2,1)S(1)}, bf16[160,128]{1,0:T(8,128)(2,1)S(1)}, u32[]{:S(2)}, u32[]{:S(2)}) collective-permute-start(bf16[160,128]{1,0:T(8,128)(2,1)S(1)} %get-tuple-element.23.p0), channel_id=1, source_target_pairs={{0,2},{2,0},{4,6},{6,4},{1,3},{3,1},{5,7},{7,5},{8,10},{10,8},{12,... | collective-permute-start | bytes 122888 | tf_op jit(solution)/shard_map/ppermute | solution.py:35
  66.3 3.8 %collective-permute-start.8 = (bf16[160,128]{1,0:T(8,128)(2,1)S(1)}, bf16[160,128]{1,0:T(8,128)(2,1)S(1)}, u32[]{:S(2)}, u32[]{:S(2)}) collective-permute-start(bf16[160,128]{1,0:T(8,128)(2,1)S(1)} %get-tuple-element.23.p0), channel_id=1, source_target_pairs={{0,4},{2,6},{4,0},{6,2},{1,5},{3,7},{5,1},{7,3},{8,12},{10,14},{12... | collective-permute-start | bytes 122888 | tf_op jit(solution)/shard_map/ppermute | solution.py:35
  68.2 4.7 %collective-permute-start.9 = (bf16[160,128]{1,0:T(8,128)(2,1)S(1)}, bf16[160,128]{1,0:T(8,128)(2,1)S(1)}, u32[]{:S(2)}, u32[]{:S(2)}) collective-permute-start(bf16[160,128]{1,0:T(8,128)(2,1)S(1)} %get-tuple-element.23.p0), channel_id=1, source_target_pairs={{0,6},{2,4},{4,2},{6,0},{1,7},{3,5},{5,3},{7,1},{8,14},{10,12},{12... | collective-permute-start | bytes 122888 | tf_op jit(solution)/shard_map/ppermute | solution.py:35
  72.9 8.4 %copy-start.10 = (bf16[128,256]{1,0:T(8,128)(2,1)S(1)}, bf16[128,256]{1,0:T(8,128)(2,1)}, u32[]{:S(2)}) copy-start(bf16[128,256]{1,0:T(8,128)(2,1)} %maximum_select_fusion.hq_ref) | copy-start | bytes 196612
  72.9 8.4 %copy-start.11 = (bf16[256,256]{1,0:T(8,128)(2,1)S(1)}, bf16[256,256]{1,0:T(8,128)(2,1)}, u32[]{:S(2)}) copy-start(bf16[256,256]{1,0:T(8,128)(2,1)} %hyper_ref.1) | copy-start | bytes 393220
  72.9 12.3 %copy-start.14 = (s32[2]{0:T(128)S(1)}, s32[2]{0:T(128)}, u32[]{:S(2)}) copy-start(s32[2]{0:T(128)} %pad_add_fusion.1) | copy-start | bytes 28
  74.6 3.9 %collective-permute-start.10 = (bf16[128,256]{1,0:T(8,128)(2,1)S(1)}, bf16[128,256]{1,0:T(8,128)(2,1)S(1)}, u32[]{:S(2)}, u32[]{:S(2)}) collective-permute-start(bf16[128,256]{1,0:T(8,128)(2,1)S(1)} %get-tuple-element.25.t0), channel_id=1, source_target_pairs={{0,16},{16,0},{32,48},{48,32},{1,17},{17,1},{33,49},{49,33},{2,18}... | collective-permute-start | bytes 196616 | tf_op jit(solution)/shard_map/ppermute | solution.py:35
  74.6 4.7 %collective-permute-start.11 = (bf16[128,256]{1,0:T(8,128)(2,1)S(1)}, bf16[128,256]{1,0:T(8,128)(2,1)S(1)}, u32[]{:S(2)}, u32[]{:S(2)}) collective-permute-start(bf16[128,256]{1,0:T(8,128)(2,1)S(1)} %get-tuple-element.25.t0), channel_id=1, source_target_pairs={{0,32},{16,48},{32,0},{48,16},{1,33},{17,49},{33,1},{49,17},{2,34}... | collective-permute-start | bytes 196616 | tf_op jit(solution)/shard_map/ppermute | solution.py:35
  77.0 4.3 %collective-permute-start.12 = (bf16[128,256]{1,0:T(8,128)(2,1)S(1)}, bf16[128,256]{1,0:T(8,128)(2,1)S(1)}, u32[]{:S(2)}, u32[]{:S(2)}) collective-permute-start(bf16[128,256]{1,0:T(8,128)(2,1)S(1)} %get-tuple-element.25.t0), channel_id=1, source_target_pairs={{0,48},{16,32},{32,16},{48,0},{1,49},{17,33},{33,17},{49,1},{2,50}... | collective-permute-start | bytes 196616 | tf_op jit(solution)/shard_map/ppermute | solution.py:35
  84.0 4.4 %collective-permute-start.13 = (f32[64,64]{1,0:T(8,128)S(1)}, f32[64,64]{1,0:T(8,128)S(1)}, u32[]{:S(2)}, u32[]{:S(2)}) collective-permute-start(f32[64,64]{1,0:T(8,128)S(1)} %get-tuple-element.33), channel_id=1, source_target_pairs={{0,1},{1,0},{2,3},{3,2},{4,5},{5,4},{6,7},{7,6},{8,9},{9,8},{10,11... | collective-permute-start | bytes 49160 | tf_op jit(solution)/shard_map/ppermute | solution.py:35
  88.4 11.1 %collective-permute-start.14 = (f32[2,64,64]{2,1,0:T(8,128)S(1)}, f32[2,64,64]{2,1,0:T(8,128)S(1)}, u32[]{:S(2)}, u32[]{:S(2)}) collective-permute-start(f32[2,64,64]{2,1,0:T(8,128)S(1)} %maximum_select_fusion.2), channel_id=1, source_target_pairs={{0,64},{64,0},{128,192},{192,128},{1,65},{65,1},{129,193},{193,129... | collective-permute-start | bytes 98312 | tf_op jit(solution)/shard_map/ppermute | solution.py:35
  96.3 5.1 %collective-permute-start.15 = (f32[2,64,64]{2,1,0:T(8,128)S(1)}, f32[2,64,64]{2,1,0:T(8,128)S(1)}, u32[]{:S(2)}, u32[]{:S(2)}) collective-permute-start(f32[2,64,64]{2,1,0:T(8,128)S(1)} %maximum_select_fusion.2), channel_id=1, source_target_pairs={{0,128},{64,192},{128,0},{192,64},{1,129},{65,193},{129,1},{193,65... | collective-permute-start | bytes 98312 | tf_op jit(solution)/shard_map/ppermute | solution.py:35
  99.1 5.6 %collective-permute-start.16 = (f32[2,64,64]{2,1,0:T(8,128)S(1)}, f32[2,64,64]{2,1,0:T(8,128)S(1)}, u32[]{:S(2)}, u32[]{:S(2)}) collective-permute-start(f32[2,64,64]{2,1,0:T(8,128)S(1)} %maximum_select_fusion.2), channel_id=1, source_target_pairs={{0,192},{64,128},{128,64},{192,0},{1,193},{65,129},{129,65},{193,1... | collective-permute-start | bytes 98312 | tf_op jit(solution)/shard_map/ppermute | solution.py:35
